TPU v7x, 32 devices: a whole 2x2x4 slice. The times are simulated.
32 devices in a mesh: dp: 8 (over z, x), fsdp: 4 (over y, core).
Axes of the slice: x: 2, y: 2, z: 4, core: 2. Of those that a mesh axis runs over, the one named last changes fastest.
Arguments:
- tokens: bfloat16 [8192, 768], P(('dp', 'fsdp')), may hold values from -18 to 18, as said below
- cotangent: bfloat16 [8192, 768], P(('dp', 'fsdp')), may hold values from -6 to 6
- segment_ids: int32 [8192], P('dp'), may hold values from 0 to 239, as said below
- valid_mask: int32 [8192], P(('dp', 'fsdp')), may hold values from 0 to 1, as said below
- ln1_gain: bfloat16 [768], P('fsdp'), may hold values from 0.5 to 1.5
- ln1_bias: bfloat16 [768], P('fsdp'), may hold values from -1.1953125 to 1.1953125
- qkv_weight: bfloat16 [768, 2304], P('fsdp'), may hold values from -0.21875 to 0.21875
- qkv_bias: bfloat16 [2304], P('fsdp'), may hold values from -1.1953125 to 1.1953125
- query_gain: bfloat16 [64], P('fsdp'), may hold values from 0.5 to 1.5
- query_bias: bfloat16 [64], P('fsdp'), may hold values from -1.796875 to 1.796875
- key_gain: bfloat16 [64], P('fsdp'), may hold values from 0.5 to 1.5
- proj_weight: bfloat16 [768, 768], P('fsdp'), may hold values from -0.875 to 0.875
- proj_bias: bfloat16 [768], P('fsdp'), may hold values from -1.1953125 to 1.1953125
- ln2_gain: bfloat16 [768], P('fsdp'), may hold values from 0.5 to 1.5
- ln2_bias: bfloat16 [768], P('fsdp'), may hold values from -1.1953125 to 1.1953125
- fc1_weight: bfloat16 [768, 3072], P('fsdp'), may hold values from -0.21875 to 0.21875
- fc1_bias: bfloat16 [3072], P('fsdp'), may hold values from -1.1953125 to 1.1953125
- fc2_weight: bfloat16 [3072, 768], P('fsdp'), may hold values from -0.109375 to 0.109375
- fc2_bias: bfloat16 [768], P('fsdp'), may hold values from -1.1953125 to 1.1953125
Outputs:
- block_out: bfloat16 [8192, 768], P(('dp', 'fsdp'))
- tokens_grad: float32 [8192, 768], P(('dp', 'fsdp'))
- ln1_gain_grad: float32 [768], P('fsdp')
- ln1_bias_grad: float32 [768], P('fsdp')
- qkv_weight_grad: float32 [768, 2304], P('fsdp')
- qkv_bias_grad: float32 [2304], P('fsdp')
- query_gain_grad: float32 [64], P('fsdp')
- query_bias_grad: float32 [64], P('fsdp')
- key_gain_grad: float32 [64], P('fsdp')
- proj_weight_grad: float32 [768, 768], P('fsdp')
- proj_bias_grad: float32 [768], P('fsdp')
- ln2_gain_grad: float32 [768], P('fsdp')
- ln2_bias_grad: float32 [768], P('fsdp')
- fc1_weight_grad: float32 [768, 3072], P('fsdp')
- fc1_bias_grad: float32 [3072], P('fsdp')
- fc2_weight_grad: float32 [3072, 768], P('fsdp')
- fc2_bias_grad: float32 [768], P('fsdp')
- rms_values: float32 [3], replicated
Inputs may be any that keep to these rules, and one draw needn't show every extreme that they name: `segment_ids`: in each aligned block of 1024 slots (block b) either one image of 576 patches with id 32 b, then padding with id 32 b + 1, or 16 images of 64 patches with ids 32 b + 0, 1, ...; block 0 holds a large image, block 1 and the last block small ones. `valid_mask`: 1 exactly on the slots of images, 0 on padding. `tokens`: row scales differ along the slots.
All inputs are finite; a program needn't handle non-finite values.
Results may differ from a plain program's by a relative error of at most 0.015.
Values may be sent and summed in bfloat16 or wider, within the bound.
A program may use at most 192 MiB of HBM per device.

v0:
```python
import functools

import jax
import jax.numpy as jnp
from jax import lax
from jax.experimental import pallas as pl
from jax.experimental.pallas import tpu as pltpu
from jax.sharding import PartitionSpec as P


HEADS = 12
HEAD_DIM = 64
EPS = 1e-06
MASKED = -1e30
F32 = jnp.float32
BF16 = jnp.bfloat16


def swap(value, axis, size, bit):
    return lax.ppermute(value, axis, [(i, i ^ bit) for i in range(size)])


def dot(first, second):
    return jnp.dot(first, second, preferred_element_type=F32)


def left_cross(first, second):
    return lax.dot_general(first, second, (((0,), (0,)), ((), ())), preferred_element_type=F32)


def right_cross(first, second):
    return lax.dot_general(first, second, (((1,), (1,)), ((), ())), preferred_element_type=F32)


def norm_parts(values):
    average = jnp.mean(values, axis=-1, keepdims=True)
    centred = values - average
    spread = jnp.mean(centred * centred, axis=-1, keepdims=True)
    scale = lax.rsqrt(spread + EPS)
    return centred * scale, scale


def norm_back(grad, unit, scale):
    return scale * (
        grad
        - jnp.mean(grad, axis=-1, keepdims=True)
        - unit * jnp.mean(grad * unit, axis=-1, keepdims=True)
    )


def block_of(step, count):
    return pl.ds(pl.multiple_of(step * count, count), count)


def front_body(
    count, x_ref, w_ref, vec_ref, bias_ref, head_ref, rows_ref, cols_ref,
    o_ref, p_ref, raw_ref, q_ref, k_ref, v_ref,
):
    heads, rows, size = q_ref.shape
    scaling = size**-0.5

    @pl.loop(0, rows // count)
    def _(step):
        at = block_of(step, count)
        unit, _ = norm_parts(x_ref[at].astype(F32))
        normed = (unit * vec_ref[0:1] + vec_ref[1:2]).astype(BF16)
        projected = dot(normed, w_ref[...]) + bias_ref[...]
        for h in range(heads):
            query, key, value = [
                projected[:, (j * heads + h) * size : (j * heads + h + 1) * size] for j in range(3)
            ]
            raw_ref[h, at] = query
            raw_ref[heads + h, at] = key
            unit, _ = norm_parts(query)
            q_ref[h, at] = ((unit * head_ref[0:1] + head_ref[1:2]) * scaling).astype(BF16)
            unit, _ = norm_parts(key)
            k_ref[h, at] = (unit * head_ref[2:3]).astype(BF16)
            v_ref[h, at] = value.astype(BF16)

    for h in range(heads):

        @pl.loop(0, rows // count)
        def _(step):
            at = block_of(step, count)
            scores = right_cross(q_ref[h, at], k_ref[h])
            scores = jnp.where(rows_ref[at] == cols_ref[...], scores, MASKED)
            top = jnp.max(scores, axis=-1, keepdims=True)
            raised = jnp.exp(scores - top)
            total = jnp.sum(raised, axis=-1, keepdims=True)
            probs = (raised * (1.0 / total)).astype(BF16)
            p_ref[h, at] = probs
            o_ref[at, h * size : (h + 1) * size] = dot(probs, v_ref[h]).astype(BF16)


def front(count, tokens_all, w_qkv, vectors, bias, head_vectors, ids):
    rows, width = tokens_all.shape
    size = head_vectors.shape[1]
    part = w_qkv.shape[1] // 3
    heads = part // size
    return pl.pallas_call(
        functools.partial(front_body, count),
        out_shape=[
            jax.ShapeDtypeStruct((rows, part), BF16),
            jax.ShapeDtypeStruct((heads, rows, rows), BF16),
            jax.ShapeDtypeStruct((2 * heads, rows, size), F32),
            jax.ShapeDtypeStruct((heads, rows, size), BF16),
            jax.ShapeDtypeStruct((heads, rows, size), BF16),
            jax.ShapeDtypeStruct((heads, rows, size), BF16),
        ],
        cost_estimate=pl.CostEstimate(
            flops=6 * rows * width * part + 4 * heads * rows * rows * size,
            bytes_accessed=2 * rows * (width + heads * rows + 8 * part) + 6 * width * part,
            transcendentals=heads * rows * rows,
        ),
        name="front",
    )(tokens_all, w_qkv, vectors, bias, head_vectors, ids[:, None], ids[None, :])


def back_body(
    count, z_ref, wp_ref, p_ref, raw_ref, q_ref, k_ref, v_ref, x_ref, w_ref, vec_ref, head_ref,
    dw_ref, da_ref, sum_ref, bias_ref, heads_ref, g_ref, dk_ref, dv_ref, dq_ref,
):
    heads, rows, size = q_ref.shape
    scaling = size**-0.5
    steps = rows // count
    sum_ref[...] = jnp.zeros_like(sum_ref)
    bias_ref[...] = jnp.zeros_like(bias_ref)
    heads_ref[...] = jnp.zeros_like(heads_ref)
    dw_ref[...] = jnp.zeros_like(dw_ref)
    for h in range(heads):
        dk_ref[...] = jnp.zeros_like(dk_ref)
        dv_ref[...] = jnp.zeros_like(dv_ref)

        @pl.loop(0, steps)
        def _(step):
            at = block_of(step, count)
            grad = right_cross(z_ref[at], wp_ref[h * size : (h + 1) * size]).astype(BF16)
            low = p_ref[h, at]
            probs = low.astype(F32)
            grad_probs = right_cross(grad, v_ref[h])
            delta = jnp.sum(probs * grad_probs, axis=-1, keepdims=True)
            grad_scores = (probs * (grad_probs - delta)).astype(BF16)
            dq_ref[at] = dot(grad_scores, k_ref[h])
            dk_ref[...] += left_cross(grad_scores, q_ref[h, at])
            dv_ref[...] += left_cross(low, grad)

        @pl.loop(0, steps)
        def _(step):
            at = block_of(step, count)
            grad = dq_ref[at] * scaling
            unit, scale = norm_parts(raw_ref[h, at])
            heads_ref[0:1] += jnp.sum(grad * unit, axis=0, keepdims=True)
            heads_ref[1:2] += jnp.sum(grad, axis=0, keepdims=True)
            g_ref[at, h * size : (h + 1) * size] = norm_back(
                grad * head_ref[0:1], unit, scale
            ).astype(BF16)
            grad = dk_ref[at]
            unit, scale = norm_parts(raw_ref[heads + h, at])
            heads_ref[2:3] += jnp.sum(grad * unit, axis=0, keepdims=True)
            first = (heads + h) * size
            g_ref[at, first : first + size] = norm_back(grad * head_ref[2:3], unit, scale).astype(
                BF16
            )
            first = (2 * heads + h) * size
            g_ref[at, first : first + size] = dv_ref[at].astype(BF16)

    @pl.loop(0, steps)
    def _(step):
        at = block_of(step, count)
        unit, _ = norm_parts(x_ref[at].astype(F32))
        normed = (unit * vec_ref[0:1] + vec_ref[1:2]).astype(BF16)
        grad = g_ref[at]
        dw_ref[...] += left_cross(normed, grad)
        bias_ref[0:1] += jnp.sum(grad.astype(F32), axis=0, keepdims=True)
        grad_normed = right_cross(grad, w_ref[...])
        da_ref[at] = grad_normed.astype(BF16)
        sum_ref[0:1] += jnp.sum(grad_normed * unit, axis=0, keepdims=True)
        sum_ref[1:2] += jnp.sum(grad_normed, axis=0, keepdims=True)


def back(count, z_all, w_proj, probs, raw, queries, keys, values, tokens_all, w_qkv, vectors, head_vectors):
    rows, width = tokens_all.shape
    heads, _, size = queries.shape
    part = heads * size
    return pl.pallas_call(
        functools.partial(back_body, count),
        out_shape=[
            jax.ShapeDtypeStruct((width, 3 * part), F32),
            jax.ShapeDtypeStruct((rows, width), BF16),
            jax.ShapeDtypeStruct((8, width), F32),
            jax.ShapeDtypeStruct((8, 3 * part), F32),
            jax.ShapeDtypeStruct((8, size), F32),
        ],
        scratch_shapes=[
            pltpu.VMEM((rows, 3 * part), BF16),
            pltpu.VMEM((rows, size), F32),
            pltpu.VMEM((rows, size), F32),
            pltpu.VMEM((rows, size), F32),
        ],
        cost_estimate=pl.CostEstimate(
            flops=14 * rows * width * part + 8 * heads * rows * rows * size,
            bytes_accessed=2 * rows * (3 * width + heads * rows + 12 * part) + 18 * width * part,
            transcendentals=0,
        ),
        name="back",
    )(z_all, w_proj, probs, raw, queries, keys, values, tokens_all, w_qkv, vectors, head_vectors)


def pack_body(*refs):
    out = refs[-1]
    columns = out.shape[1]
    rows = []
    for ref in refs[:-1]:
        value = ref[...].astype(F32)[None]
        size = value.shape[1]
        if size < columns:
            rows.append(jnp.concatenate([value, jnp.zeros((1, columns - size), F32)], axis=1))
        else:
            rows += [value[:, i : i + columns] for i in range(0, size, columns)]
    rows.append(jnp.zeros((out.shape[0] - len(rows), columns), F32))
    out[...] = jnp.concatenate(rows, axis=0).astype(BF16)


def pack(vectors, columns):
    return pl.pallas_call(
        pack_body, out_shape=jax.ShapeDtypeStruct((16, columns), BF16), name="pack"
    )(*vectors)


def arrange_body(share_rows, rank_ref, p0, p1, p2, p3, o_ref):
    pieces = [p[...].astype(F32) for p in (p0, p1, p2, p3)]
    part = pieces[0].shape[1] // 3
    low, high = (rank_ref[0] & 1) == 1, (rank_ref[0] & 2) == 2
    pairs = [
        (jnp.where(low, a, b), jnp.where(low, b, a))
        for a, b in ((pieces[1], pieces[0]), (pieces[3], pieces[2]))
    ]
    total = (pieces[0] + pieces[1]) + (pieces[2] + pieces[3])
    chosen = [jnp.where(high, pairs[1][i], pairs[0][i]) for i in range(2)]
    chosen += [jnp.where(high, pairs[0][i], pairs[1][i]) for i in range(2)]
    placed = jnp.concatenate(
        [c[:, j * part : (j + 1) * part] for j in range(3) for c in chosen], axis=1
    )
    wide = jnp.concatenate([total] * 4, axis=1)
    row = lax.broadcasted_iota(jnp.int32, placed.shape, 0)
    o_ref[...] = jnp.where(row < share_rows, placed, wide).astype(BF16)


def arrange(share_rows, rank, pieces):
    rows, columns = pieces[0].shape
    vmem = pl.BlockSpec(memory_space=pltpu.VMEM)
    return pl.pallas_call(
        functools.partial(arrange_body, share_rows),
        in_specs=[pl.BlockSpec(memory_space=pltpu.SMEM)] + [vmem] * 4,
        out_specs=vmem,
        out_shape=jax.ShapeDtypeStruct((rows, 4 * columns), BF16),
        name="arrange",
    )(rank[None], *pieces)


GELU_SCALE = 0.7978845608028654
GELU_CUBE = 0.044715


def middle_body(
    m0, m1, m2, m3, x_ref, g0, g1, g2, g3, w0, w1, w2, w3, wu_ref, wd_ref, vec_ref, bias_ref,
    z_ref, m_ref, dc_ref, dd_ref, du_ref, sum_ref, g_ref,
):
    step = pl.program_id(0)

    @pl.when(step == 0)
    def _():
        dd_ref[...] = jnp.zeros_like(dd_ref)
        du_ref[...] = jnp.zeros_like(du_ref)
        sum_ref[...] = jnp.zeros_like(sum_ref)

    for r, piece in enumerate((g0, g1, g2, g3)):

        @pl.when(step == r)
        def _(piece=piece):
            g_ref[...] = piece[...]

    branch = vec_ref[0:1]
    for piece, weight in zip((m0, m1, m2, m3), (w0, w1, w2, w3)):
        branch = branch + dot(piece[...], weight[...])

    @pl.when(step == 0)
    def _():
        z_ref[...] = branch

    unit, _ = norm_parts(x_ref[...].astype(F32) + branch)
    normed = (unit * vec_ref[1:2] + vec_ref[2:3]).astype(BF16)
    inner = dot(normed, wu_ref[...]) + bias_ref[...]
    square = inner * inner
    bent = jnp.tanh(GELU_SCALE * (inner + GELU_CUBE * inner * square))
    half = 0.5 * (1.0 + bent)
    active = (inner * half).astype(BF16)
    slope = half + 0.5 * inner * (1.0 - bent * bent) * (
        GELU_SCALE * (1.0 + 3.0 * GELU_CUBE * square)
    )
    grad = g_ref[...]
    m_ref[...] = dot(active, wd_ref[...]).astype(BF16)
    dd_ref[...] += left_cross(active, grad)
    grad_inner = right_cross(grad, wd_ref[...]) * slope
    grad_low = grad_inner.astype(BF16)
    du_ref[...] += left_cross(normed, grad_low)
    grad_normed = right_cross(grad_low, wu_ref[...])
    dc_ref[...] = grad_normed.astype(BF16)
    sum_ref[0:1] += jnp.sum(grad_low.astype(F32), axis=0, keepdims=True)
    sum_ref[1:2] += jnp.sum(grad_normed * unit, axis=0, keepdims=True)
    sum_ref[2:3] += jnp.sum(grad_normed, axis=0, keepdims=True)


def middle(count, pieces, tokens_all, grads, w_proj, w_up, w_down, vectors, bias):
    rows, width = tokens_all.shape
    part = pieces[0].shape[1]
    hidden = w_up.shape[1]
    steps = rows // count

    def held(shape):
        return pl.BlockSpec(shape, lambda i: (0, 0))

    def shifted(r):
        return pl.BlockSpec((count, part), lambda i: (jnp.bitwise_xor(i, r), 0))

    block = pl.BlockSpec((count, width), lambda i: (i, 0))
    return pl.pallas_call(
        middle_body,
        grid=(steps,),
        in_specs=[shifted(r) for r in range(4)]
        + [block]
        + [held(v.shape) for v in (*grads, *w_proj, w_up, w_down)]
        + [held(vectors.shape), held(bias.shape)],
        out_specs=[
            held((count, width)),
            block,
            block,
            held((hidden, width)),
            held((width, hidden)),
            held((8, width)),
        ],
        out_shape=[
            jax.ShapeDtypeStruct((count, width), F32),
            jax.ShapeDtypeStruct((rows, width), BF16),
            jax.ShapeDtypeStruct((rows, width), BF16),
            jax.ShapeDtypeStruct((hidden, width), F32),
            jax.ShapeDtypeStruct((width, hidden), F32),
            jax.ShapeDtypeStruct((8, width), F32),
        ],
        cost_estimate=pl.CostEstimate(
            flops=14 * rows * width * hidden,
            bytes_accessed=10 * rows * width + 14 * width * hidden,
            transcendentals=rows * hidden,
        ),
        scratch_shapes=[pltpu.VMEM((count, width), BF16)],
        name="middle",
    )(*pieces, tokens_all, *grads, *w_proj, w_up, w_down, vectors, bias)


def on_device(
    dp_size,
    fs_size,
    tokens,
    cotangent,
    segment_ids,
    valid_mask,
    ln1_gain,
    ln1_bias,
    qkv_weight,
    qkv_bias,
    query_gain,
    query_bias,
    key_gain,
    proj_weight,
    proj_bias,
    ln2_gain,
    ln2_bias,
    fc1_weight,
    fc1_bias,
    fc2_weight,
    fc2_bias,
):
    count, width = tokens.shape
    rank = lax.axis_index("fsdp")
    place = lax.axis_index("dp")
    near = functools.partial(swap, axis="fsdp", size=fs_size, bit=1)
    far = functools.partial(swap, axis="fsdp", size=fs_size, bit=2)
    own_heads = HEADS // fs_size
    part = own_heads * HEAD_DIM
    hidden = fc1_weight.shape[1]
    hidden_own = hidden // fs_size
    rows_own = qkv_weight.shape[0]
    rounds = [1 << i for i in range(dp_size.bit_length() - 1)]

    def gather(value):
        second = far(value)
        return [value, near(value), second, near(second)]

    def spread(pieces):
        return [pieces[0], near(pieces[1]), far(pieces[2]), swap(pieces[3], "fsdp", fs_size, 3)]

    def collect(low):
        low = [low[r * count : (r + 1) * count] for r in range(4)]
        other = near(jnp.concatenate([low[1], low[3]], axis=0)).astype(F32)
        first = low[0].astype(F32) + other[:count]
        sent = (low[2].astype(F32) + other[count:]).astype(BF16)
        return first + far(sent).astype(F32), sent

    def at(r):
        return rank ^ r

    def ordered(pieces, axis):
        chosen = [lax.select_n(at(i), *[pieces[j] for j in range(4)]) for i in range(4)]
        return jnp.concatenate(chosen, axis=axis)

    small = pack(
        (ln1_gain, ln1_bias, ln2_gain, ln2_bias, proj_bias, fc2_bias, qkv_bias)
        + (query_gain, query_bias, key_gain),
        rows_own,
    )
    small_all = ordered([p[:, None] for p in gather(small)], 1).astype(F32)
    wide = small_all[:6].reshape(6, width)
    gain_one, shift_one, gain_two, shift_two, b_proj, b_down = [wide[i] for i in range(6)]
    narrow = query_gain.shape[0]
    gain_query, shift_query, gain_key = [
        small_all[i, :, :narrow].reshape(-1) for i in (9, 10, 11)
    ]
    b_qkv_all = small_all[6:9].transpose(1, 0, 2).reshape(-1)

    def own_columns(matrix, owner):
        return [
            lax.dynamic_slice_in_dim(matrix, block * width + owner * part, part, matrix.ndim - 1)
            for block in range(3)
        ]

    tokens_all = jnp.concatenate(gather(tokens), axis=0)
    w_qkv = ordered(
        spread([jnp.concatenate(own_columns(qkv_weight, at(r)), axis=1) for r in range(4)]), 0
    )

    def after(value, other):
        return lax.optimization_barrier((value, other))[0]

    w_proj_pieces = gather(after(proj_weight, w_qkv))
    up_pieces = [
        lax.dynamic_slice_in_dim(after(fc1_weight, w_qkv), at(r) * hidden_own, hidden_own, 1)
        for r in range(4)
    ]
    up_pieces[1] = near(up_pieces[1])
    up_pieces[2] = far(up_pieces[2])
    up_pieces[3] = swap(up_pieces[3], "fsdp", fs_size, 3)
    w_up = ordered(up_pieces, 0)
    weights_valid = valid_mask.astype(F32)[:, None]
    grad_mlp_own = (cotangent.astype(F32) * weights_valid).astype(BF16)
    grad_mlp_pieces = gather(after(grad_mlp_own, w_qkv))
    ids = jnp.concatenate(
        [lax.dynamic_slice_in_dim(segment_ids, at(r) * count, count) for r in range(4)]
    )

    b_qkv = jnp.concatenate(own_columns(b_qkv_all, rank))
    vectors_one = jnp.concatenate([gain_one[None], shift_one[None]])
    head_vectors = jnp.concatenate([gain_query[None], shift_query[None], gain_key[None]])
    mixed_own, probs, raw, queries, keys, values = front(
        count, tokens_all, w_qkv, vectors_one, b_qkv[None], head_vectors, ids
    )
    vectors = jnp.concatenate([b_proj[None], gain_two[None], shift_two[None]])
    branch_own, mlp_part, grad_two_part, total_down, total_up, sums_middle = middle(
        count, gather(mixed_own), tokens_all, grad_mlp_pieces, w_proj_pieces, w_up, fc2_weight, vectors,
        fc1_bias.astype(F32)[None],
    )
    inputs = tokens.astype(F32)
    hidden_one = inputs + branch_own

    def held_back(other, marks, order):
        return after(other, marks[order]) if order < len(marks) and marks[order] is not None else other

    def halve(total, marks=(), tail=0):
        seen = []
        first, second = total[:, : total.shape[1] - tail], total[:, total.shape[1] - tail :]
        for order, bit in enumerate(rounds):
            size = first.shape[1] // 2
            some = second.shape[1] // 2
            low, high = first[:, :size], first[:, size:]
            if tail:
                low = jnp.concatenate([low, second[:, :some]], axis=1)
                high = jnp.concatenate([high, second[:, some:]], axis=1)
            upper = (place & bit) != 0
            sent = jnp.where(upper, low, high).astype(BF16)
            other = held_back(swap(sent, "dp", dp_size, bit), marks, order)
            seen.append(other)
            total = jnp.where(upper, high, low).astype(F32) + other.astype(F32)
            first, second = total[:, :size], total[:, size:]
        return total, seen

    def unite(share, marks=()):
        share = share.astype(BF16)[None]
        seen = []
        for order, bit in enumerate(reversed(rounds)):
            other = held_back(swap(share, "dp", dp_size, bit), marks, order)
            seen.append(other)
            upper = (place & bit) != 0
            share = jnp.where(
                upper,
                jnp.concatenate([other, share], axis=0),
                jnp.concatenate([share, other], axis=0),
            )
        return share, seen

    def to_rows(share):
        share = share.astype(BF16)
        return spread([lax.dynamic_index_in_dim(share, at(r), 0, False) for r in range(4)])

    grad_normed_two, mark_two = collect(grad_two_part)
    grad_out = grad_mlp_own.astype(F32)
    unit_two, scale_two = norm_parts(hidden_one)
    grad_hidden = grad_out + norm_back(grad_normed_two * gain_two, unit_two, scale_two)
    grad_branch_own = grad_hidden.astype(BF16)
    grad_branch_low = jnp.concatenate(gather(grad_branch_own), axis=0)
    total_proj = left_cross(mixed_own, grad_branch_low)
    total_qkv, grad_one_part, sums_one, sums_bias, sums_heads = back(
        count, grad_branch_low, proj_weight, probs, raw, queries, keys, values, tokens_all, w_qkv,
        vectors_one, head_vectors,
    )
    grad_normed_one, _ = collect(grad_one_part)
    unit_one, scale_one = norm_parts(inputs)
    tokens_grad = grad_hidden + norm_back(
        grad_normed_one * gain_one, unit_one, scale_one
    )

    branch_mlp = collect(after(mlp_part, sums_heads))[0] + b_down
    result = hidden_one + branch_mlp
    rms_sums = jnp.stack(
        [
            jnp.sum(weights_valid * result * result),
            jnp.sum(weights_valid * branch_own * branch_own),
            jnp.sum(weights_valid * branch_mlp * branch_mlp),
            jnp.sum(weights_valid),
        ]
    )

    bias_qkv = sums_bias[0]
    bias_qkv_all = jnp.zeros((3 * width,), F32)
    for block in range(3):
        bias_qkv_all = lax.dynamic_update_slice(
            bias_qkv_all, bias_qkv[block * part : (block + 1) * part], (block * width + rank * part,)
        )
    bias_up_all = lax.dynamic_update_slice(jnp.zeros((hidden,), F32), sums_middle[0], (rank * hidden_own,))
    packed = [
        sums_one[0],
        sums_one[1],
        bias_qkv_all,
        sums_heads[0],
        sums_heads[1],
        sums_heads[2],
        jnp.sum(grad_branch_own.astype(F32), axis=0),
        sums_middle[1],
        sums_middle[2],
        bias_up_all,
        jnp.sum(grad_out, axis=0),
    ]
    lengths = [v.shape[0] // fs_size for v in packed] + [4]
    vector = jnp.concatenate(
        [v.reshape(fs_size, -1) for v in packed] + [jnp.broadcast_to(rms_sums[None], (fs_size, 4))],
        axis=1,
    )
    vector = jnp.pad(vector, ((0, 0), (0, dp_size * 3 * part - vector.shape[1])))
    vector = vector.reshape(fs_size, dp_size, 3 * part)

    count_rounds = len(rounds)
    total_last = jnp.concatenate([total_qkv.reshape(fs_size, rows_own, 3 * part), vector], axis=1)
    share_last, seen = halve(total_last, tail=dp_size)
    pieces_last = to_rows(share_last)
    share_rows = rows_own // dp_size
    last, seen_back = unite(arrange(share_rows, rank, pieces_last))
    seen = [*seen, pieces_last[3], *seen_back]

    early = [mark_two, grad_branch_own] + [grad_branch_low] * (count_rounds - 2)
    share_down, seen_down = halve(total_down[None], early)
    grad_down, _ = unite(share_down[0], [sums_heads, seen[0], seen[1]])
    grad_down = grad_down.astype(F32).reshape(hidden_own, width)
    total_up = after(total_up, seen_down[0])
    late = [grad_branch_own] + [sums_heads] * (count_rounds - 1)
    share_up, _ = halve(total_up.reshape(fs_size, rows_own, hidden_own), late)
    grad_up, _ = unite(ordered(to_rows(share_up), 1), [seen[1], seen[2], seen[count_rounds]])
    grad_up = grad_up.astype(F32).reshape(rows_own, hidden)
    share_proj, _ = halve(total_proj[None], seen[:count_rounds])
    grad_proj, _ = unite(share_proj[0], seen[count_rounds:])
    grad_proj = grad_proj.astype(F32).reshape(rows_own, width)
    last = last.astype(F32)
    grad_qkv = last[:, :share_rows].reshape(rows_own, 3 * width)
    vector = last[:, share_rows, : 3 * part].reshape(-1)
    finals = []
    start = 0
    for length in lengths:
        finals.append(vector[start : start + length])
        start += length
    sums = finals.pop()
    return (
        result.astype(BF16),
        tokens_grad,
        finals[0],
        finals[1],
        grad_qkv,
        finals[2],
        finals[3],
        finals[4],
        finals[5],
        grad_proj,
        finals[6],
        finals[7],
        finals[8],
        grad_up,
        finals[9],
        grad_down,
        finals[10],
        jnp.sqrt(sums[:3] / sums[3]),
    )


def solution(mesh):
    rows = P(("dp", "fsdp"), None)
    vector = P("fsdp")
    matrix = P("fsdp", None)
    device = functools.partial(on_device, mesh.shape["dp"], mesh.shape["fsdp"])

    return jax.shard_map(
        device,
        mesh=mesh,
        in_specs=(
            rows, rows, P("dp"), P(("dp", "fsdp")), vector, vector, matrix, vector, vector, vector,
            vector, matrix, vector, vector, vector, matrix, vector, matrix, vector,
        ),
        out_specs=(
            rows, rows, vector, vector, matrix, vector, vector, vector, vector, matrix, vector,
            vector, vector, matrix, vector, matrix, vector, P(),
        ),
        check_vma=False,
    )
```

profile of v0, /device:TPU:0, one launch (start us, length us, event | category | flops | bytes accessed | tf_op | source)
XLA Modules:
  0.0 341.4 jit_solution(17411743311903729678)
XLA Ops:
  2.2 3.0 collective-permute-start.7
  5.7 2.8 constant_dynamic-slice_fusion.18
  10.4 1.9 pad_maximum_fusion.13
  17.5 2.0 collective-permute-start.4
  22.1 4.4 %collective-permute-done.4 = bf16[192,576]{1,0:T(8,128)(2,1)S(1)} collective-permute-done((bf16[192,576]{1,0:T(8,128)(2,1)}, bf16[192,576]{1,0:T(8,128)(2,1)S(1)}, u32[]{:S(2)}, u32[]{:S(2)}) %collective-permute-start.4) | collective-permute-done | bytes 221216 | tf_op jit(solution)/shard_map/ppermute | solution.py:20
  26.6 4.0 %collective-permute-done.5 = bf16[192,576]{1,0:T(8,128)(2,1)S(1)} collective-permute-done((bf16[192,576]{1,0:T(8,128)(2,1)}, bf16[192,576]{1,0:T(8,128)(2,1)S(1)}, u32[]{:S(2)}, u32[]{:S(2)}) %collective-permute-start.5) | collective-permute-done | bytes 221216 | tf_op jit(solution)/shard_map/ppermute | solution.py:20
  37.9 27.8 %front.1 = (bf16[1024,192]{1,0:T(8,128)(2,1)}, bf16[3,1024,1024]{2,1,0:T(8,128)(2,1)}, f32[6,1024,64]{2,1,0:T(8,128)}, bf16[3,1024,64]{2,1,0:T(8,128)(2,1)}, bf1...) custom-call(bf16[1024,768]{1,0:T(8,128)(2,1)} %copy-done.13, bf16[768,576]{1,0:T(8,128)(2,1)} %pad_maximum_fusion.2.w_ref, ...), custom_call_target="tpu_custom_call" | custom-call | flops 1711276032 | bytes 11894784 | tf_op jit(solution)/shard_map/front/pallas_call | solution.py:100
  74.0 12.4 %collective-permute-done.20 = bf16[192,768]{1,0:T(8,128)(2,1)S(1)} collective-permute-done((bf16[192,768]{1,0:T(8,128)(2,1)S(1)}, bf16[192,768]{1,0:T(8,128)(2,1)S(1)}, u32[]{:S(2)}, u32[]{:S(2)}) %collective-permute-start.20) | collective-permute-done | bytes 294944 | tf_op jit(solution)/shard_map/ppermute | solution.py:20
  87.0 5.8 %collective-permute-done.19 = bf16[192,768]{1,0:T(8,128)(2,1)S(1)} collective-permute-done((bf16[192,768]{1,0:T(8,128)(2,1)S(1)}, bf16[192,768]{1,0:T(8,128)(2,1)S(1)}, u32[]{:S(2)}, u32[]{:S(2)}) %collective-permute-start.19) | collective-permute-done | bytes 294944 | tf_op jit(solution)/shard_map/ppermute | solution.py:20
  96.5 18.2 %middle.1 = (f32[256,768]{1,0:T(8,128)}, bf16[1024,768]{1,0:T(8,128)(2,1)}, bf16[1024,768]{1,0:T(8,128)(2,1)}, f32[768,768]{1,0:T(8,128)}, f32[768,768]{1,0:T(8,128)}, /*index=5*/f32[8,768]{1,0:T(8,128)}) custom-call(bf16[1024,192]{1,0:T(8,128)(2,1)} %get-tuple-element.58.m0, bf16[1024,192]{1,0:T(8,128)(2,1)} %copy-done.55, ...), custom_call_target="tpu_custom_call" | custom-call | flops 8455716864 | bytes 16121856 | tf_op jit(solution)/shard_map/middle/pallas_call | solution.py:327
  125.2 9.3 %collective-permute-done.45 = bf16[1,384,768]{2,1,0:T(8,128)(2,1)S(1)} collective-permute-done((bf16[1,384,768]{2,1,0:T(8,128)(2,1)S(1)}, bf16[1,384,768]{2,1,0:T(8,128)(2,1)S(1)}, u32[]{:S(2)}, u32[]{:S(2)}) %collective-permute-start.45) | collective-permute-done | bytes 589856 | tf_op jit(solution)/shard_map/ppermute | solution.py:20
  139.7 1.9 convert_reduce_fusion.2
  144.6 2.7 collective-permute-start.56
  147.3 3.7 %collective-permute-done.46 = bf16[4,96,768]{2,1,0:T(8,128)(2,1)} collective-permute-done((bf16[4,96,768]{2,1,0:T(8,128)(2,1)S(1)}, bf16[4,96,768]{2,1,0:T(8,128)(2,1)}, u32[]{:S(2)}, u32[]{:S(2)}) %collective-permute-start.46) | collective-permute-done | bytes 589856 | tf_op jit(solution)/shard_map/ppermute | solution.py:20
  157.6 2.5 pad_maximum_fusion.z_ref
  160.0 32.1 %back.1 = (f32[768,576]{1,0:T(8,128)}, bf16[1024,768]{1,0:T(8,128)(2,1)}, f32[8,768]{1,0:T(8,128)}, f32[8,576]{1,0:T(8,128)}, f32[8,64]{1,0:T(8,128)}) custom-call(bf16[1024,768]{1,0:T(8,128)(2,1)} %pad_maximum_fusion.z_ref, bf16[192,768]{1,0:T(8,128)(2,1)} %wp_ref.1, bf16[3,1024,1024]{2,1,0:T(8,128)(2,1)} %get-tuple-element.65.p_ref, ...), custom_call_target="tpu_custom_call" | custom-call | flops 3724541952 | bytes 18382848 | tf_op jit(solution)/shard_map/back/pallas_call | solution.py:185
  197.1 2.7 collective-permute-start.57
  229.5 2.6 collective-permute-start.52
  233.8 6.4 %collective-permute-done.29 = bf16[256,768]{1,0:T(8,128)(2,1)S(1)} collective-permute-done((bf16[256,768]{1,0:T(8,128)(2,1)S(1)}, bf16[256,768]{1,0:T(8,128)(2,1)S(1)}, u32[]{:S(2)}, u32[]{:S(2)}) %collective-permute-start.29) | collective-permute-done | bytes 393248 | tf_op jit(solution)/shard_map/ppermute | solution.py:20
  242.5 3.8 %collective-permute-done.27 = bf16[256,768]{1,0:T(8,128)(2,1)S(1)} collective-permute-done((bf16[256,768]{1,0:T(8,128)(2,1)S(1)}, bf16[256,768]{1,0:T(8,128)(2,1)S(1)}, u32[]{:S(2)}, u32[]{:S(2)}) %collective-permute-start.27) | collective-permute-done | bytes 393248 | tf_op jit(solution)/shard_map/ppermute | solution.py:20
  248.1 2.7 pad_maximum_fusion.18
  258.9 9.1 %collective-permute-done.30 = bf16[4,100,576]{2,0,1:T(4,128)(2,1)S(1)} collective-permute-done((bf16[4,100,576]{2,0,1:T(4,128)(2,1)S(1)}, bf16[4,100,576]{2,0,1:T(4,128)(2,1)S(1)}, u32[]{:S(2)}, u32[]{:S(2)}) %collective-permute-start.30) | collective-permute-done | bytes 460832 | tf_op jit(solution)/shard_map/ppermute | solution.py:20
  271.7 3.2 collective-permute-done.31
  276.1 3.3 collective-permute-start.41
  281.7 5.1 %collective-permute-done.32 = bf16[4,25,576]{2,0,1:T(4,128)(2,1)S(1)} collective-permute-done((bf16[4,25,576]{2,0,1:T(4,128)(2,1)S(1)}, bf16[4,25,576]{2,0,1:T(4,128)(2,1)S(1)}, u32[]{:S(2)}, u32[]{:S(2)}) %collective-permute-start.32) | collective-permute-done | bytes 115232 | tf_op jit(solution)/shard_map/ppermute | solution.py:20
  294.8 2.9 collective-permute-start.36
  298.9 2.1 collective-permute-start.53
  301.0 2.7 collective-permute-done.43
  308.5 2.5 collective-permute-done.53
  314.1 2.6 collective-permute-done.37
  319.3 8.1 %collective-permute-done.54 = bf16[4,24,3072]{2,1,0:T(8,128)(2,1)S(1)} collective-permute-done((bf16[4,24,3072]{2,1,0:T(8,128)(2,1)S(1)}, bf16[4,24,3072]{2,1,0:T(8,128)(2,1)S(1)}, u32[]{:S(2)}, u32[]{:S(2)}) %collective-permute-start.54) | collective-permute-done | bytes 589856 | tf_op jit(solution)/shard_map/ppermute | solution.py:20
  329.3 5.8 %collective-permute-done.38 = bf16[4,25,2304]{2,0,1:T(4,128)(2,1)S(1)} collective-permute-done((bf16[4,25,2304]{2,0,1:T(4,128)(2,1)S(1)}, bf16[4,25,2304]{2,0,1:T(4,128)(2,1)S(1)}, u32[]{:S(2)}, u32[]{:S(2)}) %collective-permute-start.38) | collective-permute-done | bytes 460832 | tf_op jit(solution)/shard_map/ppermute | solution.py:20
  (380 shorter events, 139.6 us)
Async XLA Ops:
  2.2 11.9 %collective-permute-start.7 = (bf16[16,192]{1,0:T(8,128)(2,1)}, bf16[16,192]{1,0:T(8,128)(2,1)S(1)}, u32[]{:S(2)}, u32[]{:S(2)}) collective-permute-start(bf16[16,192]{1,0:T(8,128)(2,1)} %pack.1), channel_id=1, source_target_pairs={{0,2},{1,3},{2,0},{3,1},{4,6},{5,7},{6,4},{7,5},{8,10},{9,11},{10,... | collective-permute-start | bytes 18440 | tf_op jit(solution)/shard_map/ppermute | solution.py:20
  5.2 12.3 %collective-permute-start.6 = (bf16[16,192]{1,0:T(8,128)(2,1)}, bf16[16,192]{1,0:T(8,128)(2,1)S(1)}, u32[]{:S(2)}, u32[]{:S(2)}) collective-permute-start(bf16[16,192]{1,0:T(8,128)(2,1)} %pack.1), channel_id=1, source_target_pairs={{0,1},{1,0},{2,3},{3,2},{4,5},{5,4},{6,7},{7,6},{8,9},{9,8},{10,11... | collective-permute-start | bytes 18440 | tf_op jit(solution)/shard_map/ppermute | solution.py:20
  5.2 29.5 %collective-permute-start = (bf16[256,768]{1,0:T(8,128)(2,1)}, bf16[256,768]{1,0:T(8,128)(2,1)}, u32[]{:S(2)}, u32[]{:S(2)}) collective-permute-start(bf16[256,768]{1,0:T(8,128)(2,1)} %param.19), channel_id=1, source_target_pairs={{0,1},{1,0},{2,3},{3,2},{4,5},{5,4},{6,7},{7,6},{8,9},{9,8},{10,11... | collective-permute-start | bytes 1179656 | tf_op jit(solution)/shard_map/ppermute | solution.py:20
  5.7 25.1 %collective-permute-start.1 = (bf16[256,768]{1,0:T(8,128)(2,1)}, bf16[256,768]{1,0:T(8,128)(2,1)}, u32[]{:S(2)}, u32[]{:S(2)}) collective-permute-start(bf16[256,768]{1,0:T(8,128)(2,1)} %param.19), channel_id=1, source_target_pairs={{0,2},{1,3},{2,0},{3,1},{4,6},{5,7},{6,4},{7,5},{8,10},{9,11},{10,... | collective-permute-start | bytes 1179656 | tf_op jit(solution)/shard_map/ppermute | solution.py:20
  9.4 12.8 %collective-permute-start.3 = (bf16[192,576]{1,0:T(8,128)(2,1)}, bf16[192,576]{1,0:T(8,128)(2,1)S(1)}, u32[]{:S(2)}, u32[]{:S(2)}) collective-permute-start(bf16[192,576]{1,0:T(8,128)(2,1)} %pad_maximum_fusion.11), channel_id=1, source_target_pairs={{0,1},{1,0},{2,3},{3,2},{4,5},{5,4},{6,7},{7,6},{8,9},{9,8},{10,11... | collective-permute-start | bytes 663560 | tf_op jit(solution)/shard_map/ppermute | solution.py:20
  19.5 11.0 %collective-permute-start.5 = (bf16[192,576]{1,0:T(8,128)(2,1)}, bf16[192,576]{1,0:T(8,128)(2,1)S(1)}, u32[]{:S(2)}, u32[]{:S(2)}) collective-permute-start(bf16[192,576]{1,0:T(8,128)(2,1)} %pad_maximum_fusion.13), channel_id=1, source_target_pairs={{0,3},{1,2},{2,1},{3,0},{4,7},{5,6},{6,5},{7,4},{8,11},{9,10},{10,... | collective-permute-start | bytes 663560 | tf_op jit(solution)/shard_map/ppermute | solution.py:20
  32.6 35.7 %collective-permute-start.16 = (bf16[192,768]{1,0:T(8,128)(2,1)}, bf16[192,768]{1,0:T(8,128)(2,1)}, u32[]{:S(2)}, u32[]{:S(2)}) collective-permute-start(bf16[192,768]{1,0:T(8,128)(2,1)} %wp_ref.1), channel_id=1, source_target_pairs={{0,2},{1,3},{2,0},{3,1},{4,6},{5,7},{6,4},{7,5},{8,10},{9,11},{10,... | collective-permute-start | bytes 884744 | tf_op jit(solution)/shard_map/ppermute | solution.py:20
  34.4 34.4 %collective-permute-start.15 = (bf16[192,768]{1,0:T(8,128)(2,1)}, bf16[192,768]{1,0:T(8,128)(2,1)}, u32[]{:S(2)}, u32[]{:S(2)}) collective-permute-start(bf16[192,768]{1,0:T(8,128)(2,1)} %wp_ref.1), channel_id=1, source_target_pairs={{0,1},{1,0},{2,3},{3,2},{4,5},{5,4},{6,7},{7,6},{8,9},{9,8},{10,11... | collective-permute-start | bytes 884744 | tf_op jit(solution)/shard_map/ppermute | solution.py:20
  34.4 52.6 %collective-permute-start.13 = (bf16[256,768]{1,0:T(8,128)(2,1)S(1)}, bf16[256,768]{1,0:T(8,128)(2,1)}, u32[]{:S(2)}, u32[]{:S(2)}) collective-permute-start(bf16[256,768]{1,0:T(8,128)(2,1)S(1)} %get-tuple-element.59.g0), channel_id=1, source_target_pairs={{0,2},{1,3},{2,0},{3,1},{4,6},{5,7},{6,4},{7,5},{8,10},{9,11},{10,... | collective-permute-start | bytes 1179656 | tf_op jit(solution)/shard_map/ppermute | solution.py:20
  65.7 27.0 %collective-permute-start.10 = (bf16[1024,192]{1,0:T(8,128)(2,1)}, bf16[1024,192]{1,0:T(8,128)(2,1)}, u32[]{:S(2)}, u32[]{:S(2)}) collective-permute-start(bf16[1024,192]{1,0:T(8,128)(2,1)} %get-tuple-element.58.m0), channel_id=1, source_target_pairs={{0,2},{1,3},{2,0},{3,1},{4,6},{5,7},{6,4},{7,5},{8,10},{9,11},{10,... | collective-permute-start | bytes 1179656 | tf_op jit(solution)/shard_map/ppermute | solution.py:20
  68.4 18.0 %collective-permute-start.20 = (bf16[192,768]{1,0:T(8,128)(2,1)S(1)}, bf16[192,768]{1,0:T(8,128)(2,1)S(1)}, u32[]{:S(2)}, u32[]{:S(2)}) collective-permute-start(bf16[192,768]{1,0:T(8,128)(2,1)S(1)} %get-tuple-element.145), channel_id=1, source_target_pairs={{0,3},{1,2},{2,1},{3,0},{4,7},{5,6},{6,5},{7,4},{8,11},{9,10},{10,... | collective-permute-start | bytes 884744 | tf_op jit(solution)/shard_map/ppermute | solution.py:20
  68.8 24.0 %collective-permute-start.19 = (bf16[192,768]{1,0:T(8,128)(2,1)S(1)}, bf16[192,768]{1,0:T(8,128)(2,1)S(1)}, u32[]{:S(2)}, u32[]{:S(2)}) collective-permute-start(bf16[192,768]{1,0:T(8,128)(2,1)S(1)} %get-tuple-element.146), channel_id=1, source_target_pairs={{0,2},{1,3},{2,0},{3,1},{4,6},{5,7},{6,4},{7,5},{8,10},{9,11},{10,... | collective-permute-start | bytes 884744 | tf_op jit(solution)/shard_map/ppermute | solution.py:20
  74.0 20.7 %collective-permute-start.12 = (bf16[256,768]{1,0:T(8,128)(2,1)S(1)}, bf16[256,768]{1,0:T(8,128)(2,1)S(1)}, u32[]{:S(2)}, u32[]{:S(2)}) collective-permute-start(bf16[256,768]{1,0:T(8,128)(2,1)S(1)} %get-tuple-element.59.g0), channel_id=1, source_target_pairs={{0,1},{1,0},{2,3},{3,2},{4,5},{5,4},{6,7},{7,6},{8,9},{9,8},{10,11... | collective-permute-start | bytes 1179656 | tf_op jit(solution)/shard_map/ppermute | solution.py:20
  119.2 15.3 %collective-permute-start.45 = (bf16[1,384,768]{2,1,0:T(8,128)(2,1)S(1)}, bf16[1,384,768]{2,1,0:T(8,128)(2,1)S(1)}, u32[]{:S(2)}, u32[]{:S(2)}) collective-permute-start(bf16[1,384,768]{2,1,0:T(8,128)(2,1)S(1)} %select_convert_fusion.1), channel_id=1, source_target_pairs={{0,4},{4,0},{8,12},{12,8},{16,20},{20,16},{24,28},{28,24},{1,5},{5... | collective-permute-start | bytes 1769480 | tf_op jit(solution)/shard_map/ppermute | solution.py:20
  123.7 14.6 %collective-permute-start.22 = (bf16[256,768]{1,0:T(8,128)(2,1)S(1)}, bf16[256,768]{1,0:T(8,128)(2,1)S(1)}, u32[]{:S(2)}, u32[]{:S(2)}) collective-permute-start(bf16[256,768]{1,0:T(8,128)(2,1)S(1)} %fusion.19), channel_id=1, source_target_pairs={{0,2},{1,3},{2,0},{3,1},{4,6},{5,7},{6,4},{7,5},{8,10},{9,11},{10,... | collective-permute-start | bytes 1179656 | tf_op jit(solution)/shard_map/ppermute | solution.py:20
  136.7 14.3 %collective-permute-start.46 = (bf16[4,96,768]{2,1,0:T(8,128)(2,1)S(1)}, bf16[4,96,768]{2,1,0:T(8,128)(2,1)}, u32[]{:S(2)}, u32[]{:S(2)}) collective-permute-start(bf16[4,96,768]{2,1,0:T(8,128)(2,1)S(1)} %select_convert_fusion), channel_id=1, source_target_pairs={{0,4},{4,0},{8,12},{12,8},{16,20},{20,16},{24,28},{28,24},{1,5},{5... | collective-permute-start | bytes 1769480 | tf_op jit(solution)/shard_map/ppermute | solution.py:20
  143.1 11.0 %collective-permute-start.23 = (bf16[256,768]{1,0:T(8,128)(2,1)}, bf16[256,768]{1,0:T(8,128)(2,1)}, u32[]{:S(2)}, u32[]{:S(2)}) collective-permute-start(bf16[256,768]{1,0:T(8,128)(2,1)} %get-tuple-element.126), channel_id=1, source_target_pairs={{0,1},{1,0},{2,3},{3,2},{4,5},{5,4},{6,7},{7,6},{8,9},{9,8},{10,11... | collective-permute-start | bytes 1179656 | tf_op jit(solution)/shard_map/ppermute | solution.py:20
  144.6 49.3 %collective-permute-start.56 = (bf16[1,96,768]{2,1,0:T(8,128)(2,1)S(1)}, bf16[1,96,768]{2,1,0:T(8,128)(2,1)}, u32[]{:S(2)}, u32[]{:S(2)}) collective-permute-start(bf16[1,96,768]{2,1,0:T(8,128)(2,1)S(1)} %select_convert_fusion.6), channel_id=1, source_target_pairs={{0,16},{4,20},{8,24},{12,28},{16,0},{20,4},{24,8},{28,12},{1,17},{... | collective-permute-start | bytes 442376 | tf_op jit(solution)/shard_map/ppermute | solution.py:20
  153.6 46.8 %collective-permute-start.47 = (bf16[4,48,768]{2,1,0:T(8,128)(2,1)}, bf16[4,48,768]{2,1,0:T(8,128)(2,1)}, u32[]{:S(2)}, u32[]{:S(2)}) collective-permute-start(bf16[4,48,768]{2,1,0:T(8,128)(2,1)} %select_convert_fusion.4), channel_id=1, source_target_pairs={{0,8},{4,12},{8,0},{12,4},{16,24},{20,28},{24,16},{28,20},{1,9},{5... | collective-permute-start | bytes 884744 | tf_op jit(solution)/shard_map/ppermute | solution.py:20
  156.6 111.7 %collective-permute-start.39 = (bf16[1,96,768]{2,1,0:T(8,128)(2,1)}, bf16[1,96,768]{2,1,0:T(8,128)(2,1)}, u32[]{:S(2)}, u32[]{:S(2)}) collective-permute-start(bf16[1,96,768]{2,1,0:T(8,128)(2,1)} %select_convert_fusion.8), channel_id=1, source_target_pairs={{0,4},{4,0},{8,12},{12,8},{16,20},{20,16},{24,28},{28,24},{1,5},{5... | collective-permute-start | bytes 442376 | tf_op jit(solution)/shard_map/ppermute | solution.py:20
  197.1 22.4 %collective-permute-start.57 = (bf16[1,96,768]{2,1,0:T(8,128)(2,1)S(1)}, bf16[1,96,768]{2,1,0:T(8,128)(2,1)}, u32[]{:S(2)}, u32[]{:S(2)}) collective-permute-start(bf16[1,96,768]{2,1,0:T(8,128)(2,1)S(1)} %add_convert_fusion.1), channel_id=1, source_target_pairs={{0,16},{4,20},{8,24},{12,28},{16,0},{20,4},{24,8},{28,12},{1,17},{... | collective-permute-start | bytes 442376 | tf_op jit(solution)/shard_map/ppermute | solution.py:20
  202.4 17.1 %collective-permute-start.48 = (bf16[4,24,768]{2,1,0:T(8,128)(2,1)}, bf16[4,24,768]{2,1,0:T(8,128)(2,1)S(1)}, u32[]{:S(2)}, u32[]{:S(2)}) collective-permute-start(bf16[4,24,768]{2,1,0:T(8,128)(2,1)} %select_convert_fusion.7), channel_id=1, source_target_pairs={{0,16},{4,20},{8,24},{12,28},{16,0},{20,4},{24,8},{28,12},{1,17},{... | collective-permute-start | bytes 442376 | tf_op jit(solution)/shard_map/ppermute | solution.py:20
  204.7 22.0 %collective-permute-start.28 = (bf16[512,768]{1,0:T(8,128)(2,1)}, bf16[512,768]{1,0:T(8,128)(2,1)}, u32[]{:S(2)}, u32[]{:S(2)}) collective-permute-start(bf16[512,768]{1,0:T(8,128)(2,1)} %pad_maximum_fusion.5), channel_id=1, source_target_pairs={{0,1},{1,0},{2,3},{3,2},{4,5},{5,4},{6,7},{7,6},{8,9},{9,8},{10,11... | collective-permute-start | bytes 2359304 | tf_op jit(solution)/shard_map/ppermute | solution.py:20
  225.2 55.3 %collective-permute-start.58 = (bf16[2,96,768]{2,1,0:T(8,128)(2,1)S(1)}, bf16[2,96,768]{2,1,0:T(8,128)(2,1)}, u32[]{:S(2)}, u32[]{:S(2)}) collective-permute-start(bf16[2,96,768]{2,1,0:T(8,128)(2,1)S(1)} %maximum_select_fusion.9), channel_id=1, source_target_pairs={{0,8},{4,12},{8,0},{12,4},{16,24},{20,28},{24,16},{28,20},{1,9},{5... | collective-permute-start | bytes 884744 | tf_op jit(solution)/shard_map/ppermute | solution.py:20
  228.1 12.1 %collective-permute-start.29 = (bf16[256,768]{1,0:T(8,128)(2,1)S(1)}, bf16[256,768]{1,0:T(8,128)(2,1)S(1)}, u32[]{:S(2)}, u32[]{:S(2)}) collective-permute-start(bf16[256,768]{1,0:T(8,128)(2,1)S(1)} %fusion.13), channel_id=1, source_target_pairs={{0,2},{1,3},{2,0},{3,1},{4,6},{5,7},{6,4},{7,5},{8,10},{9,11},{10,... | collective-permute-start | bytes 1179656 | tf_op jit(solution)/shard_map/ppermute | solution.py:20
  229.5 61.0 %collective-permute-start.52 = (bf16[1,24,3072]{2,1,0:T(8,128)(2,1)}, bf16[1,24,3072]{2,1,0:T(8,128)(2,1)}, u32[]{:S(2)}, u32[]{:S(2)}) collective-permute-start(bf16[1,24,3072]{2,1,0:T(8,128)(2,1)} %maximum_bitcast_fusion), channel_id=1, source_target_pairs={{0,16},{4,20},{8,24},{12,28},{16,0},{20,4},{24,8},{28,12},{1,17},{... | collective-permute-start | bytes 442376 | tf_op jit(solution)/shard_map/ppermute | solution.py:20
  232.3 14.0 %collective-permute-start.27 = (bf16[256,768]{1,0:T(8,128)(2,1)S(1)}, bf16[256,768]{1,0:T(8,128)(2,1)S(1)}, u32[]{:S(2)}, u32[]{:S(2)}) collective-permute-start(bf16[256,768]{1,0:T(8,128)(2,1)S(1)} %fusion.16), channel_id=1, source_target_pairs={{0,2},{1,3},{2,0},{3,1},{4,6},{5,7},{6,4},{7,5},{8,10},{9,11},{10,... | collective-permute-start | bytes 1179656 | tf_op jit(solution)/shard_map/ppermute | solution.py:20
  256.5 11.4 %collective-permute-start.30 = (bf16[4,100,576]{2,0,1:T(4,128)(2,1)S(1)}, bf16[4,100,576]{2,0,1:T(4,128)(2,1)S(1)}, u32[]{:S(2)}, u32[]{:S(2)}) collective-permute-start(bf16[4,100,576]{2,0,1:T(4,128)(2,1)S(1)} %bitcast.93), channel_id=1, source_target_pairs={{0,4},{4,0},{8,12},{12,8},{16,20},{20,16},{24,28},{28,24},{1,5},{5... | collective-permute-start | bytes 1382408 | tf_op jit(solution)/shard_map/ppermute | solution.py:20
  290.5 21.8 %collective-permute-start.59 = (bf16[4,96,768]{2,1,0:T(8,128)(2,1)S(1)}, bf16[4,96,768]{2,1,0:T(8,128)(2,1)S(1)}, u32[]{:S(2)}, u32[]{:S(2)}) collective-permute-start(bf16[4,96,768]{2,1,0:T(8,128)(2,1)S(1)} %maximum_select_fusion.5), channel_id=1, source_target_pairs={{0,4},{4,0},{8,12},{12,8},{16,20},{20,16},{24,28},{28,24},{1,5},{5... | collective-permute-start | bytes 1769480 | tf_op jit(solution)/shard_map/ppermute | solution.py:20
  298.9 12.1 %collective-permute-start.53 = (bf16[2,24,3072]{2,1,0:T(8,128)(2,1)S(1)}, bf16[2,24,3072]{2,1,0:T(8,128)(2,1)S(1)}, u32[]{:S(2)}, u32[]{:S(2)}) collective-permute-start(bf16[2,24,3072]{2,1,0:T(8,128)(2,1)S(1)} %maximum_select_fusion.8), channel_id=1, source_target_pairs={{0,8},{4,12},{8,0},{12,4},{16,24},{20,28},{24,16},{28,20},{1,9},{5... | collective-permute-start | bytes 884744 | tf_op jit(solution)/shard_map/ppermute | solution.py:20
  311.1 16.3 %collective-permute-start.54 = (bf16[4,24,3072]{2,1,0:T(8,128)(2,1)S(1)}, bf16[4,24,3072]{2,1,0:T(8,128)(2,1)S(1)}, u32[]{:S(2)}, u32[]{:S(2)}) collective-permute-start(bf16[4,24,3072]{2,1,0:T(8,128)(2,1)S(1)} %maximum_select_fusion.4), channel_id=1, source_target_pairs={{0,4},{4,0},{8,12},{12,8},{16,20},{20,16},{24,28},{28,24},{1,5},{5... | collective-permute-start | bytes 1769480 | tf_op jit(solution)/shard_map/ppermute | solution.py:20
  317.2 17.9 %collective-permute-start.38 = (bf16[4,25,2304]{2,0,1:T(4,128)(2,1)S(1)}, bf16[4,25,2304]{2,0,1:T(4,128)(2,1)S(1)}, u32[]{:S(2)}, u32[]{:S(2)}) collective-permute-start(bf16[4,25,2304]{2,0,1:T(4,128)(2,1)S(1)} %copy.55), channel_id=1, source_target_pairs={{0,4},{4,0},{8,12},{12,8},{16,20},{20,16},{24,28},{28,24},{1,5},{5... | collective-permute-start | bytes 1382408 | tf_op jit(solution)/shard_map/ppermute | solution.py:20
  (87 other events, 606.1 us)
where the time goes:
time: 343 us; the launch traced here: 341 us
  waiting for transfers between devices  95.4 us (28%)
  Pallas kernels  81.2 us (24%)
  starting transfers between devices  57.2 us (17%)
  other arithmetic  53 us (15%)
  local copies, waits for them, and re-layouts  51.2 us (15%)
    ppermute x60, waiting for transfers between devices, swap(): return lax.ppermute(value, axis, [(i, i ^ bit) for i in range(size)])  95.4 us
    ppermute x60, starting transfers between devices, swap(): return lax.ppermute(value, axis, [(i, i ^ bit) for i in range(size)])  57.2 us
    pallas_call x1, Pallas kernels, back(): pl.pallas_call(functools.partial(back_body, count), out_shape=[jax.ShapeD...  32.1 us
    pallas_call x1, Pallas kernels, front(): pl.pallas_call(functools.partial(front_body, count), out_shape=[jax.Shape...  27.8 us
    pallas_call x1, Pallas kernels, middle(): pl.pallas_call(middle_body, grid=(steps,), in_specs=[shifted(r) for r in...  18.2 us
    unnamed x127, local copies, waits for them, and re-layouts  8.76 us
  transfers between devices with their start and end apart: 60, of which 24 were waited for; matrix products, arithmetic and copies ran while one was open for 26% of the time, Pallas kernels for 18%

commit v1 on v0

--- a/solution.py
+++ b/solution.py
@@ -117,8 +117,9 @@
 
 
 def back_body(
-    count, z_ref, wp_ref, p_ref, raw_ref, q_ref, k_ref, v_ref, x_ref, w_ref, vec_ref, head_ref,
-    dw_ref, da_ref, sum_ref, bias_ref, heads_ref, g_ref, dk_ref, dv_ref, dq_ref,
+    count, rank_ref, z_ref, wp_ref, p_ref, raw_ref, q_ref, k_ref, v_ref, x_ref, w_ref, vec_ref,
+    head_ref, early_ref, out_ref, da_ref, sum_ref, bias_ref, heads_ref, dw_ref, g_ref, dk_ref,
+    dv_ref, dq_ref,
 ):
     heads, rows, size = q_ref.shape
     scaling = size**-0.5
@@ -178,20 +179,52 @@
         sum_ref[1:2] += jnp.sum(grad_normed, axis=0, keepdims=True)
 
 
-def back(count, z_all, w_proj, probs, raw, queries, keys, values, tokens_all, w_qkv, vectors, head_vectors):
+    owners, total_rows, columns = out_ref.shape
+    own = dw_ref.shape[0] // owners
+    part = columns // 3
+    rank = rank_ref[0]
+    narrow = size // owners
+    for o in range(owners):
+        out_ref[o, :own] = dw_ref[o * own : (o + 1) * own]
+        first = jnp.concatenate(
+            [sum_ref[i : i + 1, o * own : (o + 1) * own] for i in range(2)]
+            + [jnp.zeros((1, columns - 2 * own), F32)],
+            axis=1,
+        )
+        groups = []
+        for j in range(3):
+            group = 3 * o + j
+            value = bias_ref[0:1, group // owners * part : (group // owners + 1) * part]
+            groups.append(jnp.where(rank == group % owners, value, 0.0))
+        gains = [heads_ref[i : i + 1, o * narrow : (o + 1) * narrow] for i in range(3)]
+        third = jnp.concatenate([*gains, jnp.zeros((1, columns - 3 * narrow), F32)], axis=1)
+        out_ref[o, own:] = jnp.concatenate(
+            [first, jnp.concatenate(groups, axis=1), third, early_ref[o]]
+            + [jnp.zeros((total_rows - own - 3 - early_ref.shape[1], columns), F32)],
+            axis=0,
+        )
+
+
+def back(count, extra, rank, *values):
+    _, _, _, _, queries, _, _, tokens_all, _, _, _, early = values
     rows, width = tokens_all.shape
     heads, _, size = queries.shape
     part = heads * size
+    owners = early.shape[0]
+    vmem = pl.BlockSpec(memory_space=pltpu.VMEM)
     return pl.pallas_call(
         functools.partial(back_body, count),
+        in_specs=[pl.BlockSpec(memory_space=pltpu.SMEM)] + [vmem] * len(values),
+        out_specs=[vmem, vmem],
         out_shape=[
-            jax.ShapeDtypeStruct((width, 3 * part), F32),
+            jax.ShapeDtypeStruct((owners, width // owners + extra, 3 * part), F32),
             jax.ShapeDtypeStruct((rows, width), BF16),
-            jax.ShapeDtypeStruct((8, width), F32),
-            jax.ShapeDtypeStruct((8, 3 * part), F32),
-            jax.ShapeDtypeStruct((8, size), F32),
         ],
         scratch_shapes=[
+            pltpu.VMEM((8, width), F32),
+            pltpu.VMEM((8, 3 * part), F32),
+            pltpu.VMEM((8, size), F32),
+            pltpu.VMEM((width, 3 * part), F32),
             pltpu.VMEM((rows, 3 * part), BF16),
             pltpu.VMEM((rows, size), F32),
             pltpu.VMEM((rows, size), F32),
@@ -203,7 +236,7 @@
             transcendentals=0,
         ),
         name="back",
-    )(z_all, w_proj, probs, raw, queries, keys, values, tokens_all, w_qkv, vectors, head_vectors)
+    )(rank[None], *values)
 
 
 def pack_body(*refs):
@@ -475,7 +508,7 @@
         return after(other, marks[order]) if order < len(marks) and marks[order] is not None else other
 
     def halve(total, marks=(), tail=0):
-        seen = []
+        seen, lead = [], None
         first, second = total[:, : total.shape[1] - tail], total[:, total.shape[1] - tail :]
         for order, bit in enumerate(rounds):
             size = first.shape[1] // 2
@@ -486,11 +519,12 @@
                 high = jnp.concatenate([high, second[:, some:]], axis=1)
             upper = (place & bit) != 0
             sent = jnp.where(upper, low, high).astype(BF16)
+            lead = sent if order == 0 else lead
             other = held_back(swap(sent, "dp", dp_size, bit), marks, order)
             seen.append(other)
             total = jnp.where(upper, high, low).astype(F32) + other.astype(F32)
             first, second = total[:, :size], total[:, size:]
-        return total, seen
+        return total, seen, lead
 
     def unite(share, marks=()):
         share = share.astype(BF16)[None]
@@ -517,17 +551,27 @@
     grad_branch_own = grad_hidden.astype(BF16)
     grad_branch_low = jnp.concatenate(gather(grad_branch_own), axis=0)
     total_proj = left_cross(mixed_own, grad_branch_low)
-    total_qkv, grad_one_part, sums_one, sums_bias, sums_heads = back(
-        count, grad_branch_low, proj_weight, probs, raw, queries, keys, values, tokens_all, w_qkv,
-        vectors_one, head_vectors,
-    )
-    grad_normed_one, _ = collect(grad_one_part)
+    own_sums = [sums_middle[1], sums_middle[2], jnp.sum(grad_branch_own.astype(F32), axis=0)]
+    own_sums = jnp.stack(own_sums).reshape(3, fs_size, rows_own)
+    bias_up = jnp.where(jnp.arange(fs_size)[:, None] == rank, sums_middle[0][None], 0.0)
+    bias_down = jnp.sum(grad_out, axis=0).reshape(fs_size, rows_own)
+    early_rows = jnp.concatenate(
+        [own_sums[0], own_sums[1], own_sums[2], bias_up, bias_down], axis=1
+    )
+    early_rows = jnp.pad(early_rows, ((0, 0), (0, 9 * part - early_rows.shape[1])))
+    early_rows = early_rows.reshape(fs_size, 3, 3 * part)
+    total_last, grad_one_part = back(
+        count, dp_size, rank, grad_branch_low, proj_weight, probs, raw, queries, keys, values,
+        tokens_all, w_qkv, vectors_one, head_vectors, early_rows,
+    )
+    share_last, seen, lead = halve(total_last, tail=dp_size)
+    grad_normed_one, _ = collect(after(grad_one_part, lead))
     unit_one, scale_one = norm_parts(inputs)
     tokens_grad = grad_hidden + norm_back(
         grad_normed_one * gain_one, unit_one, scale_one
     )
 
-    branch_mlp = collect(after(mlp_part, sums_heads))[0] + b_down
+    branch_mlp = collect(after(mlp_part, lead))[0] + b_down
     result = hidden_one + branch_mlp
     rms_sums = jnp.stack(
         [
@@ -538,63 +582,41 @@
         ]
     )
 
-    bias_qkv = sums_bias[0]
-    bias_qkv_all = jnp.zeros((3 * width,), F32)
-    for block in range(3):
-        bias_qkv_all = lax.dynamic_update_slice(
-            bias_qkv_all, bias_qkv[block * part : (block + 1) * part], (block * width + rank * part,)
-        )
-    bias_up_all = lax.dynamic_update_slice(jnp.zeros((hidden,), F32), sums_middle[0], (rank * hidden_own,))
-    packed = [
-        sums_one[0],
-        sums_one[1],
-        bias_qkv_all,
-        sums_heads[0],
-        sums_heads[1],
-        sums_heads[2],
-        jnp.sum(grad_branch_own.astype(F32), axis=0),
-        sums_middle[1],
-        sums_middle[2],
-        bias_up_all,
-        jnp.sum(grad_out, axis=0),
-    ]
-    lengths = [v.shape[0] // fs_size for v in packed] + [4]
-    vector = jnp.concatenate(
-        [v.reshape(fs_size, -1) for v in packed] + [jnp.broadcast_to(rms_sums[None], (fs_size, 4))],
-        axis=1,
-    )
-    vector = jnp.pad(vector, ((0, 0), (0, dp_size * 3 * part - vector.shape[1])))
-    vector = vector.reshape(fs_size, dp_size, 3 * part)
+    rms_sums = jnp.broadcast_to(rms_sums[:, None], (4, 128))
+    for bit in (1, 2):
+        rms_sums = rms_sums + swap(rms_sums, "fsdp", fs_size, bit)
+    for bit in rounds:
+        rms_sums = rms_sums + swap(rms_sums, "dp", dp_size, bit)
+    sums = rms_sums[:, 0]
 
     count_rounds = len(rounds)
-    total_last = jnp.concatenate([total_qkv.reshape(fs_size, rows_own, 3 * part), vector], axis=1)
-    share_last, seen = halve(total_last, tail=dp_size)
     pieces_last = to_rows(share_last)
     share_rows = rows_own // dp_size
     last, seen_back = unite(arrange(share_rows, rank, pieces_last))
     seen = [*seen, pieces_last[3], *seen_back]
 
     early = [mark_two, grad_branch_own] + [grad_branch_low] * (count_rounds - 2)
-    share_down, seen_down = halve(total_down[None], early)
-    grad_down, _ = unite(share_down[0], [sums_heads, seen[0], seen[1]])
+    share_down, seen_down, _ = halve(total_down[None], early)
+    grad_down, _ = unite(share_down[0], [lead, seen[0], seen[1]])
     grad_down = grad_down.astype(F32).reshape(hidden_own, width)
     total_up = after(total_up, seen_down[0])
-    late = [grad_branch_own] + [sums_heads] * (count_rounds - 1)
-    share_up, _ = halve(total_up.reshape(fs_size, rows_own, hidden_own), late)
+    late = [grad_branch_own] + [lead] * (count_rounds - 1)
+    share_up, _, _ = halve(total_up.reshape(fs_size, rows_own, hidden_own), late)
     grad_up, _ = unite(ordered(to_rows(share_up), 1), [seen[1], seen[2], seen[count_rounds]])
     grad_up = grad_up.astype(F32).reshape(rows_own, hidden)
-    share_proj, _ = halve(total_proj[None], seen[:count_rounds])
+    share_proj, _, _ = halve(total_proj[None], seen[:count_rounds])
     grad_proj, _ = unite(share_proj[0], seen[count_rounds:])
     grad_proj = grad_proj.astype(F32).reshape(rows_own, width)
     last = last.astype(F32)
     grad_qkv = last[:, :share_rows].reshape(rows_own, 3 * width)
-    vector = last[:, share_rows, : 3 * part].reshape(-1)
-    finals = []
-    start = 0
-    for length in lengths:
-        finals.append(vector[start : start + length])
-        start += length
-    sums = finals.pop()
+    table = last[:, share_rows, : 3 * part]
+    narrow = HEAD_DIM // fs_size
+    flat = table[3:6].reshape(-1)
+    finals = [table[0, :rows_own], table[0, rows_own : 2 * rows_own], table[1]]
+    finals += [table[2, i * narrow : (i + 1) * narrow] for i in range(3)]
+    finals += [flat[2 * rows_own : 3 * rows_own], flat[:rows_own], flat[rows_own : 2 * rows_own]]
+    finals += [flat[3 * rows_own : 3 * rows_own + hidden_own]]
+    finals += [flat[3 * rows_own + hidden_own : 4 * rows_own + hidden_own]]
     return (
         result.astype(BF16),
         tokens_grad,

time: 343 us -> 321 us (0.936)
  local copies, waits for them, and re-layouts: 51.2 us -> 34.6 us
  waiting for transfers between devices: 95.4 us -> 82.4 us
  other arithmetic: 53 us -> 59.5 us
    ppermute x60 -> x65, waiting for transfers between devices: 95.4 us -> 82.4 us  [swap(): return lax.ppermute(value, axis, [(i, i ^ bit) for i in range(size)])]
    another operation x8 -> x0, local copies, waits for them, and re-layouts: 6.65 us -> none  [the longest x7 6.57 us: on_device(): v.reshape(fs_size, -1)]
    dynamic_update_slice x4 -> x0, local copies, waits for them, and re-layouts: 4.8 us -> none  [the longest x3 4.31 us: on_device(): lax.dynamic_update_slice(bias_qkv_all, bias_qkv[block * part:(block + 1)...]
    slice x9 -> x8, local copies, waits for them, and re-layouts: 7.06 us -> 5.04 us  [the longest x1 1.47 us: on_device(): sums_middle[0][None]]
    unnamed x127 -> x100, local copies, waits for them, and re-layouts: 8.76 us -> 7.4 us
    ppermute x60 -> x65, starting transfers between devices: 57.2 us -> 58.2 us  [swap(): return lax.ppermute(value, axis, [(i, i ^ bit) for i in range(size)])]
  transfers between devices with their start and end apart: 60 -> 65, of which waited for: 24 -> 21; matrix products, arithmetic and copies ran while one was open for 26% -> 26% of each run, Pallas kernels for 18% -> 19%
where the time goes in v1:
time: 321 us; the launch traced here: 320 us
  waiting for transfers between devices  82.4 us (26%)
  Pallas kernels  81.7 us (25%)
  other arithmetic  59.5 us (19%)
  starting transfers between devices  58.2 us (18%)
  local copies, waits for them, and re-layouts  34.6 us (11%)
    ppermute x65, waiting for transfers between devices, swap(): return lax.ppermute(value, axis, [(i, i ^ bit) for i in range(size)])  82.4 us
    ppermute x65, starting transfers between devices, swap(): return lax.ppermute(value, axis, [(i, i ^ bit) for i in range(size)])  58.2 us
    pallas_call x1, Pallas kernels, back(): pl.pallas_call(functools.partial(back_body, count), in_specs=[pl.BlockSpe...  32.6 us
    pallas_call x1, Pallas kernels, front(): pl.pallas_call(functools.partial(front_body, count), out_shape=[jax.Shape...  27.8 us
    pallas_call x1, Pallas kernels, middle(): pl.pallas_call(middle_body, grid=(steps,), in_specs=[shifted(r) for r in...  18.1 us
    unnamed x100, local copies, waits for them, and re-layouts  7.4 us
  transfers between devices with their start and end apart: 65, of which 21 were waited for; matrix products, arithmetic and copies ran while one was open for 26% of the time, Pallas kernels for 19%

profile of v1, /device:TPU:0, one launch (start us, length us, event | category | flops | bytes accessed | tf_op | source)
XLA Modules:
  0.0 319.5 jit_solution(9361973649336473042)
XLA Ops:
  2.2 3.0 collective-permute-start.7
  5.7 2.8 constant_dynamic-slice_fusion.14
  18.0 2.0 collective-permute-start.4
  22.6 4.4 %collective-permute-done.4 = bf16[192,576]{1,0:T(8,128)(2,1)S(1)} collective-permute-done((bf16[192,576]{1,0:T(8,128)(2,1)}, bf16[192,576]{1,0:T(8,128)(2,1)S(1)}, u32[]{:S(2)}, u32[]{:S(2)}) %collective-permute-start.4) | collective-permute-done | bytes 221216 | tf_op jit(solution)/shard_map/ppermute | solution.py:20
  27.0 4.0 %collective-permute-done.5 = bf16[192,576]{1,0:T(8,128)(2,1)S(1)} collective-permute-done((bf16[192,576]{1,0:T(8,128)(2,1)}, bf16[192,576]{1,0:T(8,128)(2,1)S(1)}, u32[]{:S(2)}, u32[]{:S(2)}) %collective-permute-start.5) | collective-permute-done | bytes 221216 | tf_op jit(solution)/shard_map/ppermute | solution.py:20
  38.4 27.8 %front.1 = (bf16[1024,192]{1,0:T(8,128)(2,1)}, bf16[3,1024,1024]{2,1,0:T(8,128)(2,1)}, f32[6,1024,64]{2,1,0:T(8,128)}, bf16[3,1024,64]{2,1,0:T(8,128)(2,1)}, bf1...) custom-call(bf16[1024,768]{1,0:T(8,128)(2,1)} %copy-done.7, bf16[768,576]{1,0:T(8,128)(2,1)} %pad_maximum_fusion.4.w_ref, ...), custom_call_target="tpu_custom_call" | custom-call | flops 1711276032 | bytes 11894784 | tf_op jit(solution)/shard_map/front/pallas_call | solution.py:100
  74.5 12.4 %collective-permute-done.20 = bf16[192,768]{1,0:T(8,128)(2,1)S(1)} collective-permute-done((bf16[192,768]{1,0:T(8,128)(2,1)S(1)}, bf16[192,768]{1,0:T(8,128)(2,1)S(1)}, u32[]{:S(2)}, u32[]{:S(2)}) %collective-permute-start.20) | collective-permute-done | bytes 294944 | tf_op jit(solution)/shard_map/ppermute | solution.py:20
  87.4 5.8 %collective-permute-done.19 = bf16[192,768]{1,0:T(8,128)(2,1)S(1)} collective-permute-done((bf16[192,768]{1,0:T(8,128)(2,1)S(1)}, bf16[192,768]{1,0:T(8,128)(2,1)S(1)}, u32[]{:S(2)}, u32[]{:S(2)}) %collective-permute-start.19) | collective-permute-done | bytes 294944 | tf_op jit(solution)/shard_map/ppermute | solution.py:20
  97.0 18.1 %middle.1 = (f32[256,768]{1,0:T(8,128)}, bf16[1024,768]{1,0:T(8,128)(2,1)}, bf16[1024,768]{1,0:T(8,128)(2,1)}, f32[768,768]{1,0:T(8,128)}, f32[768,768]{1,0:T(8,128)}, /*index=5*/f32[8,768]{1,0:T(8,128)}) custom-call(bf16[1024,192]{1,0:T(8,128)(2,1)} %get-tuple-element.56.m0, bf16[1024,192]{1,0:T(8,128)(2,1)} %copy-done.44, ...), custom_call_target="tpu_custom_call" | custom-call | flops 8455716864 | bytes 16121856 | tf_op jit(solution)/shard_map/middle/pallas_call | solution.py:360
  115.1 2.7 select_convert_fusion.1
  129.0 4.4 %collective-permute-done.45 = bf16[1,384,768]{2,1,0:T(8,128)(2,1)} collective-permute-done((bf16[1,384,768]{2,1,0:T(8,128)(2,1)}, bf16[1,384,768]{2,1,0:T(8,128)(2,1)}, u32[]{:S(2)}, u32[]{:S(2)}) %collective-permute-start.45) | collective-permute-done | bytes 589856 | tf_op jit(solution)/shard_map/ppermute | solution.py:20
  151.4 2.6 collective-permute-start.56
  160.8 2.4 pad_maximum_fusion.z_ref
  163.2 32.6 %back.1 = (f32[4,200,576]{2,1,0:T(8,128)}, bf16[1024,768]{1,0:T(8,128)(2,1)}) custom-call(s32[1]{0:T(128)} %bitcast.7.rank_ref, bf16[1024,768]{1,0:T(8,128)(2,1)} %pad_maximum_fusion.z_ref, bf16[192,768]{1,0:T(8,128)(2,1)} %wp_ref.1, bf16[3,1024,1024]{2,1,0:T(8,128)(2,1)} %get-tuple-element.63.p_ref, f32[6,1024,64]{2,1,0:T(8,128)} %get-tuple-element.64.raw_ref, ...), custom_call_target="tpu_custom_call" | custom-call | flops 3724541952 | bytes 18382848 | tf_op jit(solution)/shard_map/back/pallas_call | solution.py:215
  197.4 2.2 collective-permute-start.57
  204.7 6.0 %collective-permute-done.57 = bf16[1,96,768]{2,1,0:T(8,128)(2,1)S(1)} collective-permute-done((bf16[1,96,768]{2,1,0:T(8,128)(2,1)S(1)}, bf16[1,96,768]{2,1,0:T(8,128)(2,1)S(1)}, u32[]{:S(2)}, u32[]{:S(2)}) %collective-permute-start.57) | collective-permute-done | bytes 147488 | tf_op jit(solution)/shard_map/ppermute | solution.py:20
  210.7 2.6 collective-permute-done.48
  218.7 3.4 %collective-permute-start.52 = (bf16[1,24,3072]{2,1,0:T(8,128)(2,1)S(1)}, bf16[1,24,3072]{2,1,0:T(8,128)(2,1)S(1)}, u32[]{:S(2)}, u32[]{:S(2)}) collective-permute-start(bf16[1,24,3072]{2,1,0:T(8,128)(2,1)S(1)} %maximum_bitcast_fusion), channel_id=1, source_target_pairs={{0,16},{4,20},{8,24},{12,28},{16,0},{20,4},{24,8},{28,12},{1,17},{... | collective-permute-start | bytes 442376 | tf_op jit(solution)/shard_map/ppermute | solution.py:20
  224.5 7.0 %collective-permute-done.58 = bf16[2,96,768]{2,1,0:T(8,128)(2,1)S(1)} collective-permute-done((bf16[2,96,768]{2,1,0:T(8,128)(2,1)S(1)}, bf16[2,96,768]{2,1,0:T(8,128)(2,1)S(1)}, u32[]{:S(2)}, u32[]{:S(2)}) %collective-permute-start.58) | collective-permute-done | bytes 294944 | tf_op jit(solution)/shard_map/ppermute | solution.py:20
  232.4 6.3 %collective-permute-done.40 = bf16[1,48,768]{2,1,0:T(8,128)(2,1)S(1)} collective-permute-done((bf16[1,48,768]{2,1,0:T(8,128)(2,1)S(1)}, bf16[1,48,768]{2,1,0:T(8,128)(2,1)S(1)}, u32[]{:S(2)}, u32[]{:S(2)}) %collective-permute-start.40) | collective-permute-done | bytes 73760 | tf_op jit(solution)/shard_map/ppermute | solution.py:20
  244.6 6.7 %collective-permute-done.32 = bf16[4,25,576]{2,1,0:T(8,128)(2,1)S(1)} collective-permute-done((bf16[4,25,576]{2,1,0:T(8,128)(2,1)S(1)}, bf16[4,25,576]{2,1,0:T(8,128)(2,1)S(1)}, u32[]{:S(2)}, u32[]{:S(2)}) %collective-permute-start.32) | collective-permute-done | bytes 115232 | tf_op jit(solution)/shard_map/ppermute | solution.py:20
  257.4 2.5 collective-permute-start.53
  264.8 2.0 collective-permute-start.43
  268.1 3.2 %collective-permute-done.43 = bf16[2,24,768]{2,1,0:T(8,128)(2,1)S(1)} collective-permute-done((bf16[2,24,768]{2,1,0:T(8,128)(2,1)S(1)}, bf16[2,24,768]{2,1,0:T(8,128)(2,1)S(1)}, u32[]{:S(2)}, u32[]{:S(2)}) %collective-permute-start.43) | collective-permute-done | bytes 73760 | tf_op jit(solution)/shard_map/ppermute | solution.py:20
  274.1 2.2 collective-permute-start.37
  283.7 2.1 fusion.10
  285.8 2.7 pad_maximum_fusion.20
  291.5 2.8 collective-permute-done.61
  295.8 2.8 collective-permute-done.62
  299.0 4.0 %collective-permute-done.63 = f32[4,128]{0,1:T(8,128)S(1)} collective-permute-done((f32[4,128]{0,1:T(8,128)S(1)}, f32[4,128]{0,1:T(8,128)S(1)}, u32[]{:S(2)}, u32[]{:S(2)}) %collective-permute-start.63) | collective-permute-done | bytes 2080 | tf_op jit(solution)/shard_map/ppermute | solution.py:20
  305.9 2.8 collective-permute-done.64
  312.4 2.2 collective-permute-done.38
  (355 shorter events, 129.2 us)
Async XLA Ops:
  2.2 12.5 %collective-permute-start.7 = (bf16[16,192]{1,0:T(8,128)(2,1)}, bf16[16,192]{1,0:T(8,128)(2,1)S(1)}, u32[]{:S(2)}, u32[]{:S(2)}) collective-permute-start(bf16[16,192]{1,0:T(8,128)(2,1)} %pack.1), channel_id=1, source_target_pairs={{0,2},{1,3},{2,0},{3,1},{4,6},{5,7},{6,4},{7,5},{8,10},{9,11},{10,... | collective-permute-start | bytes 18440 | tf_op jit(solution)/shard_map/ppermute | solution.py:20
  5.2 12.8 %collective-permute-start.6 = (bf16[16,192]{1,0:T(8,128)(2,1)}, bf16[16,192]{1,0:T(8,128)(2,1)S(1)}, u32[]{:S(2)}, u32[]{:S(2)}) collective-permute-start(bf16[16,192]{1,0:T(8,128)(2,1)} %pack.1), channel_id=1, source_target_pairs={{0,1},{1,0},{2,3},{3,2},{4,5},{5,4},{6,7},{7,6},{8,9},{9,8},{10,11... | collective-permute-start | bytes 18440 | tf_op jit(solution)/shard_map/ppermute | solution.py:20
  5.2 29.9 %collective-permute-start = (bf16[256,768]{1,0:T(8,128)(2,1)}, bf16[256,768]{1,0:T(8,128)(2,1)}, u32[]{:S(2)}, u32[]{:S(2)}) collective-permute-start(bf16[256,768]{1,0:T(8,128)(2,1)} %param.19), channel_id=1, source_target_pairs={{0,1},{1,0},{2,3},{3,2},{4,5},{5,4},{6,7},{7,6},{8,9},{9,8},{10,11... | collective-permute-start | bytes 1179656 | tf_op jit(solution)/shard_map/ppermute | solution.py:20
  5.7 25.5 %collective-permute-start.1 = (bf16[256,768]{1,0:T(8,128)(2,1)}, bf16[256,768]{1,0:T(8,128)(2,1)}, u32[]{:S(2)}, u32[]{:S(2)}) collective-permute-start(bf16[256,768]{1,0:T(8,128)(2,1)} %param.19), channel_id=1, source_target_pairs={{0,2},{1,3},{2,0},{3,1},{4,6},{5,7},{6,4},{7,5},{8,10},{9,11},{10,... | collective-permute-start | bytes 1179656 | tf_op jit(solution)/shard_map/ppermute | solution.py:20
  9.4 13.3 %collective-permute-start.3 = (bf16[192,576]{1,0:T(8,128)(2,1)}, bf16[192,576]{1,0:T(8,128)(2,1)S(1)}, u32[]{:S(2)}, u32[]{:S(2)}) collective-permute-start(bf16[192,576]{1,0:T(8,128)(2,1)} %pad_maximum_fusion.13), channel_id=1, source_target_pairs={{0,1},{1,0},{2,3},{3,2},{4,5},{5,4},{6,7},{7,6},{8,9},{9,8},{10,11... | collective-permute-start | bytes 663560 | tf_op jit(solution)/shard_map/ppermute | solution.py:20
  33.1 35.7 %collective-permute-start.16 = (bf16[192,768]{1,0:T(8,128)(2,1)}, bf16[192,768]{1,0:T(8,128)(2,1)}, u32[]{:S(2)}, u32[]{:S(2)}) collective-permute-start(bf16[192,768]{1,0:T(8,128)(2,1)} %wp_ref.1), channel_id=1, source_target_pairs={{0,2},{1,3},{2,0},{3,1},{4,6},{5,7},{6,4},{7,5},{8,10},{9,11},{10,... | collective-permute-start | bytes 884744 | tf_op jit(solution)/shard_map/ppermute | solution.py:20
  34.8 34.4 %collective-permute-start.15 = (bf16[192,768]{1,0:T(8,128)(2,1)}, bf16[192,768]{1,0:T(8,128)(2,1)}, u32[]{:S(2)}, u32[]{:S(2)}) collective-permute-start(bf16[192,768]{1,0:T(8,128)(2,1)} %wp_ref.1), channel_id=1, source_target_pairs={{0,1},{1,0},{2,3},{3,2},{4,5},{5,4},{6,7},{7,6},{8,9},{9,8},{10,11... | collective-permute-start | bytes 884744 | tf_op jit(solution)/shard_map/ppermute | solution.py:20
  34.8 52.6 %collective-permute-start.13 = (bf16[256,768]{1,0:T(8,128)(2,1)S(1)}, bf16[256,768]{1,0:T(8,128)(2,1)}, u32[]{:S(2)}, u32[]{:S(2)}) collective-permute-start(bf16[256,768]{1,0:T(8,128)(2,1)S(1)} %get-tuple-element.57.g0), channel_id=1, source_target_pairs={{0,2},{1,3},{2,0},{3,1},{4,6},{5,7},{6,4},{7,5},{8,10},{9,11},{10,... | collective-permute-start | bytes 1179656 | tf_op jit(solution)/shard_map/ppermute | solution.py:20
  66.2 27.0 %collective-permute-start.10 = (bf16[1024,192]{1,0:T(8,128)(2,1)}, bf16[1024,192]{1,0:T(8,128)(2,1)}, u32[]{:S(2)}, u32[]{:S(2)}) collective-permute-start(bf16[1024,192]{1,0:T(8,128)(2,1)} %get-tuple-element.56.m0), channel_id=1, source_target_pairs={{0,2},{1,3},{2,0},{3,1},{4,6},{5,7},{6,4},{7,5},{8,10},{9,11},{10,... | collective-permute-start | bytes 1179656 | tf_op jit(solution)/shard_map/ppermute | solution.py:20
  68.8 18.0 %collective-permute-start.20 = (bf16[192,768]{1,0:T(8,128)(2,1)S(1)}, bf16[192,768]{1,0:T(8,128)(2,1)S(1)}, u32[]{:S(2)}, u32[]{:S(2)}) collective-permute-start(bf16[192,768]{1,0:T(8,128)(2,1)S(1)} %get-tuple-element.138), channel_id=1, source_target_pairs={{0,3},{1,2},{2,1},{3,0},{4,7},{5,6},{6,5},{7,4},{8,11},{9,10},{10,... | collective-permute-start | bytes 884744 | tf_op jit(solution)/shard_map/ppermute | solution.py:20
  69.2 24.0 %collective-permute-start.19 = (bf16[192,768]{1,0:T(8,128)(2,1)S(1)}, bf16[192,768]{1,0:T(8,128)(2,1)S(1)}, u32[]{:S(2)}, u32[]{:S(2)}) collective-permute-start(bf16[192,768]{1,0:T(8,128)(2,1)S(1)} %get-tuple-element.139), channel_id=1, source_target_pairs={{0,2},{1,3},{2,0},{3,1},{4,6},{5,7},{6,4},{7,5},{8,10},{9,11},{10,... | collective-permute-start | bytes 884744 | tf_op jit(solution)/shard_map/ppermute | solution.py:20
  74.5 20.7 %collective-permute-start.12 = (bf16[256,768]{1,0:T(8,128)(2,1)S(1)}, bf16[256,768]{1,0:T(8,128)(2,1)S(1)}, u32[]{:S(2)}, u32[]{:S(2)}) collective-permute-start(bf16[256,768]{1,0:T(8,128)(2,1)S(1)} %get-tuple-element.57.g0), channel_id=1, source_target_pairs={{0,1},{1,0},{2,3},{3,2},{4,5},{5,4},{6,7},{7,6},{8,9},{9,8},{10,11... | collective-permute-start | bytes 1179656 | tf_op jit(solution)/shard_map/ppermute | solution.py:20
  117.8 15.6 %collective-permute-start.45 = (bf16[1,384,768]{2,1,0:T(8,128)(2,1)}, bf16[1,384,768]{2,1,0:T(8,128)(2,1)}, u32[]{:S(2)}, u32[]{:S(2)}) collective-permute-start(bf16[1,384,768]{2,1,0:T(8,128)(2,1)} %select_convert_fusion.1), channel_id=1, source_target_pairs={{0,4},{4,0},{8,12},{12,8},{16,20},{20,16},{24,28},{28,24},{1,5},{5... | collective-permute-start | bytes 1769480 | tf_op jit(solution)/shard_map/ppermute | solution.py:20
  127.3 12.4 %collective-permute-start.22 = (bf16[256,768]{1,0:T(8,128)(2,1)S(1)}, bf16[256,768]{1,0:T(8,128)(2,1)S(1)}, u32[]{:S(2)}, u32[]{:S(2)}) collective-permute-start(bf16[256,768]{1,0:T(8,128)(2,1)S(1)} %fusion.19), channel_id=1, source_target_pairs={{0,2},{1,3},{2,0},{3,1},{4,6},{5,7},{6,4},{7,5},{8,10},{9,11},{10,... | collective-permute-start | bytes 1179656 | tf_op jit(solution)/shard_map/ppermute | solution.py:20
  138.2 15.8 %collective-permute-start.46 = (bf16[4,96,768]{2,1,0:T(8,128)(2,1)}, bf16[4,96,768]{2,1,0:T(8,128)(2,1)}, u32[]{:S(2)}, u32[]{:S(2)}) collective-permute-start(bf16[4,96,768]{2,1,0:T(8,128)(2,1)} %select_convert_fusion), channel_id=1, source_target_pairs={{0,4},{4,0},{8,12},{12,8},{16,20},{20,16},{24,28},{28,24},{1,5},{5... | collective-permute-start | bytes 1769480 | tf_op jit(solution)/shard_map/ppermute | solution.py:20
  144.6 12.5 %collective-permute-start.23 = (bf16[256,768]{1,0:T(8,128)(2,1)S(1)}, bf16[256,768]{1,0:T(8,128)(2,1)}, u32[]{:S(2)}, u32[]{:S(2)}) collective-permute-start(bf16[256,768]{1,0:T(8,128)(2,1)S(1)} %get-tuple-element.118), channel_id=1, source_target_pairs={{0,1},{1,0},{2,3},{3,2},{4,5},{5,4},{6,7},{7,6},{8,9},{9,8},{10,11... | collective-permute-start | bytes 1179656 | tf_op jit(solution)/shard_map/ppermute | solution.py:20
  156.3 46.2 %collective-permute-start.47 = (bf16[4,48,768]{2,1,0:T(8,128)(2,1)}, bf16[4,48,768]{2,1,0:T(8,128)(2,1)}, u32[]{:S(2)}, u32[]{:S(2)}) collective-permute-start(bf16[4,48,768]{2,1,0:T(8,128)(2,1)} %select_convert_fusion.4), channel_id=1, source_target_pairs={{0,8},{4,12},{8,0},{12,4},{16,24},{20,28},{24,16},{28,20},{1,9},{5... | collective-permute-start | bytes 884744 | tf_op jit(solution)/shard_map/ppermute | solution.py:20
  160.2 62.2 %collective-permute-start.39 = (bf16[1,96,768]{2,1,0:T(8,128)(2,1)}, bf16[1,96,768]{2,1,0:T(8,128)(2,1)}, u32[]{:S(2)}, u32[]{:S(2)}) collective-permute-start(bf16[1,96,768]{2,1,0:T(8,128)(2,1)} %select_convert_fusion.9), channel_id=1, source_target_pairs={{0,4},{4,0},{8,12},{12,8},{16,20},{20,16},{24,28},{28,24},{1,5},{5... | collective-permute-start | bytes 442376 | tf_op jit(solution)/shard_map/ppermute | solution.py:20
  197.4 13.3 %collective-permute-start.57 = (bf16[1,96,768]{2,1,0:T(8,128)(2,1)S(1)}, bf16[1,96,768]{2,1,0:T(8,128)(2,1)S(1)}, u32[]{:S(2)}, u32[]{:S(2)}) collective-permute-start(bf16[1,96,768]{2,1,0:T(8,128)(2,1)S(1)} %add_convert_fusion.2), channel_id=1, source_target_pairs={{0,16},{4,20},{8,24},{12,28},{16,0},{20,4},{24,8},{28,12},{1,17},{... | collective-permute-start | bytes 442376 | tf_op jit(solution)/shard_map/ppermute | solution.py:20
  200.9 17.8 %collective-permute-start.30 = (bf16[4,100,576]{2,0,1:T(4,128)(2,1)S(1)}, bf16[4,100,576]{2,0,1:T(4,128)(2,1)S(1)}, u32[]{:S(2)}, u32[]{:S(2)}) collective-permute-start(bf16[4,100,576]{2,0,1:T(4,128)(2,1)S(1)} %copy.39), channel_id=1, source_target_pairs={{0,4},{4,0},{8,12},{12,8},{16,20},{20,16},{24,28},{28,24},{1,5},{5... | collective-permute-start | bytes 1382408 | tf_op jit(solution)/shard_map/ppermute | solution.py:20
  217.3 25.6 %collective-permute-start.28 = (bf16[512,768]{1,0:T(8,128)(2,1)S(1)}, bf16[512,768]{1,0:T(8,128)(2,1)S(1)}, u32[]{:S(2)}, u32[]{:S(2)}) collective-permute-start(bf16[512,768]{1,0:T(8,128)(2,1)S(1)} %pad_maximum_fusion.7), channel_id=1, source_target_pairs={{0,1},{1,0},{2,3},{3,2},{4,5},{5,4},{6,7},{7,6},{8,9},{9,8},{10,11... | collective-permute-start | bytes 2359304 | tf_op jit(solution)/shard_map/ppermute | solution.py:20
  218.5 36.9 %collective-permute-start.26 = (bf16[512,768]{1,0:T(8,128)(2,1)S(1)}, bf16[512,768]{1,0:T(8,128)(2,1)S(1)}, u32[]{:S(2)}, u32[]{:S(2)}) collective-permute-start(bf16[512,768]{1,0:T(8,128)(2,1)S(1)} %pad_maximum_fusion.6), channel_id=1, source_target_pairs={{0,1},{1,0},{2,3},{3,2},{4,5},{5,4},{6,7},{7,6},{8,9},{9,8},{10,11... | collective-permute-start | bytes 2359304 | tf_op jit(solution)/shard_map/ppermute | solution.py:20
  218.5 13.0 %collective-permute-start.58 = (bf16[2,96,768]{2,1,0:T(8,128)(2,1)S(1)}, bf16[2,96,768]{2,1,0:T(8,128)(2,1)S(1)}, u32[]{:S(2)}, u32[]{:S(2)}) collective-permute-start(bf16[2,96,768]{2,1,0:T(8,128)(2,1)S(1)} %maximum_select_fusion.9), channel_id=1, source_target_pairs={{0,8},{4,12},{8,0},{12,4},{16,24},{20,28},{24,16},{28,20},{1,9},{5... | collective-permute-start | bytes 884744 | tf_op jit(solution)/shard_map/ppermute | solution.py:20
  218.7 23.4 %collective-permute-start.52 = (bf16[1,24,3072]{2,1,0:T(8,128)(2,1)S(1)}, bf16[1,24,3072]{2,1,0:T(8,128)(2,1)S(1)}, u32[]{:S(2)}, u32[]{:S(2)}) collective-permute-start(bf16[1,24,3072]{2,1,0:T(8,128)(2,1)S(1)} %maximum_bitcast_fusion), channel_id=1, source_target_pairs={{0,16},{4,20},{8,24},{12,28},{16,0},{20,4},{24,8},{28,12},{1,17},{... | collective-permute-start | bytes 442376 | tf_op jit(solution)/shard_map/ppermute | solution.py:20
  224.4 14.4 %collective-permute-start.31 = (bf16[4,50,576]{2,1,0:T(8,128)(2,1)S(1)}, bf16[4,50,576]{2,1,0:T(8,128)(2,1)S(1)}, u32[]{:S(2)}, u32[]{:S(2)}) collective-permute-start(bf16[4,50,576]{2,1,0:T(8,128)(2,1)S(1)} %select_convert_fusion.5), channel_id=1, source_target_pairs={{0,8},{4,12},{8,0},{12,4},{16,24},{20,28},{24,16},{28,20},{1,9},{5... | collective-permute-start | bytes 691208 | tf_op jit(solution)/shard_map/ppermute | solution.py:20
  255.4 22.2 %collective-permute-start.59 = (bf16[4,96,768]{2,1,0:T(8,128)(2,1)}, bf16[4,96,768]{2,1,0:T(8,128)(2,1)}, u32[]{:S(2)}, u32[]{:S(2)}) collective-permute-start(bf16[4,96,768]{2,1,0:T(8,128)(2,1)} %maximum_select_fusion.5), channel_id=1, source_target_pairs={{0,4},{4,0},{8,12},{12,8},{16,20},{20,16},{24,28},{28,24},{1,5},{5... | collective-permute-start | bytes 1769480 | tf_op jit(solution)/shard_map/ppermute | solution.py:20
  257.4 16.6 %collective-permute-start.53 = (bf16[2,24,3072]{2,1,0:T(8,128)(2,1)}, bf16[2,24,3072]{2,1,0:T(8,128)(2,1)}, u32[]{:S(2)}, u32[]{:S(2)}) collective-permute-start(bf16[2,24,3072]{2,1,0:T(8,128)(2,1)} %maximum_select_fusion.8), channel_id=1, source_target_pairs={{0,8},{4,12},{8,0},{12,4},{16,24},{20,28},{24,16},{28,20},{1,9},{5... | collective-permute-start | bytes 884744 | tf_op jit(solution)/shard_map/ppermute | solution.py:20
  259.9 22.0 %collective-permute-start.29 = (bf16[256,768]{1,0:T(8,128)(2,1)}, bf16[256,768]{1,0:T(8,128)(2,1)}, u32[]{:S(2)}, u32[]{:S(2)}) collective-permute-start(bf16[256,768]{1,0:T(8,128)(2,1)} %fusion.13), channel_id=1, source_target_pairs={{0,2},{1,3},{2,0},{3,1},{4,6},{5,7},{6,4},{7,5},{8,10},{9,11},{10,... | collective-permute-start | bytes 1179656 | tf_op jit(solution)/shard_map/ppermute | solution.py:20
  271.3 12.4 %collective-permute-start.27 = (bf16[256,768]{1,0:T(8,128)(2,1)S(1)}, bf16[256,768]{1,0:T(8,128)(2,1)S(1)}, u32[]{:S(2)}, u32[]{:S(2)}) collective-permute-start(bf16[256,768]{1,0:T(8,128)(2,1)S(1)} %fusion.16), channel_id=1, source_target_pairs={{0,2},{1,3},{2,0},{3,1},{4,6},{5,7},{6,4},{7,5},{8,10},{9,11},{10,... | collective-permute-start | bytes 1179656 | tf_op jit(solution)/shard_map/ppermute | solution.py:20
  273.1 22.7 %collective-permute-start.44 = (bf16[4,24,768]{2,1,0:T(8,128)(2,1)S(1)}, bf16[4,24,768]{2,1,0:T(8,128)(2,1)S(1)}, u32[]{:S(2)}, u32[]{:S(2)}) collective-permute-start(bf16[4,24,768]{2,1,0:T(8,128)(2,1)S(1)} %maximum_select_fusion.10), channel_id=1, source_target_pairs={{0,4},{4,0},{8,12},{12,8},{16,20},{20,16},{24,28},{28,24},{1,5},{5... | collective-permute-start | bytes 442376 | tf_op jit(solution)/shard_map/ppermute | solution.py:20
  274.1 21.6 %collective-permute-start.37 = (bf16[2,25,2304]{2,1,0:T(8,128)(2,1)S(1)}, bf16[2,25,2304]{2,1,0:T(8,128)(2,1)S(1)}, u32[]{:S(2)}, u32[]{:S(2)}) collective-permute-start(bf16[2,25,2304]{2,1,0:T(8,128)(2,1)S(1)} %maximum_select_fusion.6), channel_id=1, source_target_pairs={{0,8},{4,12},{8,0},{12,4},{16,24},{20,28},{24,16},{28,20},{1,9},{5... | collective-permute-start | bytes 691208 | tf_op jit(solution)/shard_map/ppermute | solution.py:20
  277.6 32.8 %collective-permute-start.54 = (bf16[4,24,3072]{2,1,0:T(8,128)(2,1)S(1)}, bf16[4,24,3072]{2,1,0:T(8,128)(2,1)S(1)}, u32[]{:S(2)}, u32[]{:S(2)}) collective-permute-start(bf16[4,24,3072]{2,1,0:T(8,128)(2,1)S(1)} %maximum_select_fusion.4), channel_id=1, source_target_pairs={{0,4},{4,0},{8,12},{12,8},{16,20},{20,16},{24,28},{28,24},{1,5},{5... | collective-permute-start | bytes 1769480 | tf_op jit(solution)/shard_map/ppermute | solution.py:20
  (81 other events, 540.7 us)

commit v2 on v1

--- a/solution.py
+++ b/solution.py
@@ -119,7 +119,7 @@
 def back_body(
     count, rank_ref, z_ref, wp_ref, p_ref, raw_ref, q_ref, k_ref, v_ref, x_ref, w_ref, vec_ref,
     head_ref, early_ref, out_ref, da_ref, sum_ref, bias_ref, heads_ref, dw_ref, g_ref, dk_ref,
-    dv_ref, dq_ref,
+    dv_ref, dq_ref, dkt_ref, dvt_ref,
 ):
     heads, rows, size = q_ref.shape
     scaling = size**-0.5
@@ -142,8 +142,11 @@
             delta = jnp.sum(probs * grad_probs, axis=-1, keepdims=True)
             grad_scores = (probs * (grad_probs - delta)).astype(BF16)
             dq_ref[at] = dot(grad_scores, k_ref[h])
-            dk_ref[...] += left_cross(grad_scores, q_ref[h, at])
-            dv_ref[...] += left_cross(low, grad)
+            dk_ref[...] += left_cross(q_ref[h, at], grad_scores)
+            dv_ref[...] += left_cross(grad, low)
+
+        dkt_ref[...] = dk_ref[...].T
+        dvt_ref[...] = dv_ref[...].T
 
         @pl.loop(0, steps)
         def _(step):
@@ -155,7 +158,7 @@
             g_ref[at, h * size : (h + 1) * size] = norm_back(
                 grad * head_ref[0:1], unit, scale
             ).astype(BF16)
-            grad = dk_ref[at]
+            grad = dkt_ref[at]
             unit, scale = norm_parts(raw_ref[heads + h, at])
             heads_ref[2:3] += jnp.sum(grad * unit, axis=0, keepdims=True)
             first = (heads + h) * size
@@ -163,7 +166,7 @@
                 BF16
             )
             first = (2 * heads + h) * size
-            g_ref[at, first : first + size] = dv_ref[at].astype(BF16)
+            g_ref[at, first : first + size] = dvt_ref[at].astype(BF16)
 
     @pl.loop(0, steps)
     def _(step):
@@ -226,6 +229,8 @@
             pltpu.VMEM((8, size), F32),
             pltpu.VMEM((width, 3 * part), F32),
             pltpu.VMEM((rows, 3 * part), BF16),
+            pltpu.VMEM((size, rows), F32),
+            pltpu.VMEM((size, rows), F32),
             pltpu.VMEM((rows, size), F32),
             pltpu.VMEM((rows, size), F32),
             pltpu.VMEM((rows, size), F32),
@@ -432,11 +437,12 @@
     def spread(pieces):
         return [pieces[0], near(pieces[1]), far(pieces[2]), swap(pieces[3], "fsdp", fs_size, 3)]
 
-    def collect(low):
+    def collect(low, mark=None):
         low = [low[r * count : (r + 1) * count] for r in range(4)]
         other = near(jnp.concatenate([low[1], low[3]], axis=0)).astype(F32)
         first = low[0].astype(F32) + other[:count]
         sent = (low[2].astype(F32) + other[count:]).astype(BF16)
+        sent = sent if mark is None else after(sent, mark)
         return first + far(sent).astype(F32), sent
 
     def at(r):
@@ -497,8 +503,9 @@
         count, tokens_all, w_qkv, vectors_one, b_qkv[None], head_vectors, ids
     )
     vectors = jnp.concatenate([b_proj[None], gain_two[None], shift_two[None]])
+    mixed_pieces = gather(mixed_own)
     branch_own, mlp_part, grad_two_part, total_down, total_up, sums_middle = middle(
-        count, gather(mixed_own), tokens_all, grad_mlp_pieces, w_proj_pieces, w_up, fc2_weight, vectors,
+        count, mixed_pieces, tokens_all, grad_mlp_pieces, w_proj_pieces, w_up, fc2_weight, vectors,
         fc1_bias.astype(F32)[None],
     )
     inputs = tokens.astype(F32)
@@ -551,27 +558,7 @@
     grad_branch_own = grad_hidden.astype(BF16)
     grad_branch_low = jnp.concatenate(gather(grad_branch_own), axis=0)
     total_proj = left_cross(mixed_own, grad_branch_low)
-    own_sums = [sums_middle[1], sums_middle[2], jnp.sum(grad_branch_own.astype(F32), axis=0)]
-    own_sums = jnp.stack(own_sums).reshape(3, fs_size, rows_own)
-    bias_up = jnp.where(jnp.arange(fs_size)[:, None] == rank, sums_middle[0][None], 0.0)
-    bias_down = jnp.sum(grad_out, axis=0).reshape(fs_size, rows_own)
-    early_rows = jnp.concatenate(
-        [own_sums[0], own_sums[1], own_sums[2], bias_up, bias_down], axis=1
-    )
-    early_rows = jnp.pad(early_rows, ((0, 0), (0, 9 * part - early_rows.shape[1])))
-    early_rows = early_rows.reshape(fs_size, 3, 3 * part)
-    total_last, grad_one_part = back(
-        count, dp_size, rank, grad_branch_low, proj_weight, probs, raw, queries, keys, values,
-        tokens_all, w_qkv, vectors_one, head_vectors, early_rows,
-    )
-    share_last, seen, lead = halve(total_last, tail=dp_size)
-    grad_normed_one, _ = collect(after(grad_one_part, lead))
-    unit_one, scale_one = norm_parts(inputs)
-    tokens_grad = grad_hidden + norm_back(
-        grad_normed_one * gain_one, unit_one, scale_one
-    )
-
-    branch_mlp = collect(after(mlp_part, lead))[0] + b_down
+    branch_mlp = collect(mlp_part, grad_normed_two)[0] + b_down
     result = hidden_one + branch_mlp
     rms_sums = jnp.stack(
         [
@@ -582,12 +569,27 @@
         ]
     )
 
-    rms_sums = jnp.broadcast_to(rms_sums[:, None], (4, 128))
-    for bit in (1, 2):
-        rms_sums = rms_sums + swap(rms_sums, "fsdp", fs_size, bit)
-    for bit in rounds:
-        rms_sums = rms_sums + swap(rms_sums, "dp", dp_size, bit)
-    sums = rms_sums[:, 0]
+    own_sums = [sums_middle[1], sums_middle[2], jnp.sum(grad_branch_own.astype(F32), axis=0)]
+    own_sums = jnp.stack(own_sums).reshape(3, fs_size, rows_own)
+    bias_up = jnp.where(jnp.arange(fs_size)[:, None] == rank, sums_middle[0][None], 0.0)
+    bias_down = jnp.sum(grad_out, axis=0).reshape(fs_size, rows_own)
+    early_rows = jnp.concatenate(
+        [own_sums[0], own_sums[1], own_sums[2], bias_up, bias_down]
+        + [jnp.broadcast_to(rms_sums[None], (fs_size, 4))],
+        axis=1,
+    )
+    early_rows = jnp.pad(early_rows, ((0, 0), (0, 9 * part - early_rows.shape[1])))
+    early_rows = early_rows.reshape(fs_size, 3, 3 * part)
+    total_last, grad_one_part = back(
+        count, dp_size, rank, grad_branch_low, proj_weight, probs, raw, queries, keys, values,
+        tokens_all, w_qkv, vectors_one, head_vectors, early_rows,
+    )
+    share_last, seen, lead = halve(total_last, tail=dp_size)
+    grad_normed_one, _ = collect(after(grad_one_part, lead))
+    unit_one, scale_one = norm_parts(inputs)
+    tokens_grad = grad_hidden + norm_back(
+        grad_normed_one * gain_one, unit_one, scale_one
+    )
 
     count_rounds = len(rounds)
     pieces_last = to_rows(share_last)
@@ -617,6 +619,7 @@
     finals += [flat[2 * rows_own : 3 * rows_own], flat[:rows_own], flat[rows_own : 2 * rows_own]]
     finals += [flat[3 * rows_own : 3 * rows_own + hidden_own]]
     finals += [flat[3 * rows_own + hidden_own : 4 * rows_own + hidden_own]]
+    sums = flat[4 * rows_own + hidden_own :]
     return (
         result.astype(BF16),
         tokens_grad,

time: 321 us -> 307 us (0.956)
  waiting for transfers between devices: 82.4 us -> 94.1 us
  other arithmetic: 59.5 us -> 47.9 us
  starting transfers between devices: 58.2 us -> 48.6 us
  local copies, waits for them, and re-layouts: 34.6 us -> 30.7 us
    ppermute x65 -> x60, waiting for transfers between devices: 82.4 us -> 94.1 us  [swap(): return lax.ppermute(value, axis, [(i, i ^ bit) for i in range(size)])]
    ppermute x65 -> x60, starting transfers between devices: 58.2 us -> 48.6 us  [swap(): return lax.ppermute(value, axis, [(i, i ^ bit) for i in range(size)])]
    select_n x11, other arithmetic: 6.12 us -> 2.09 us  [unite(): jnp.where(upper, jnp.concatenate([other, share], axis=0), jnp.concatenate...]
    convert_element_type x12, other arithmetic: 6.16 us -> 2.9 us  [halve(): sent = jnp.where(upper, low, high).astype(BF16)]
    unnamed x100 -> x82, local copies, waits for them, and re-layouts: 7.4 us -> 7.78 us
  transfers between devices with their start and end apart: 65 -> 60, of which waited for: 21 -> 24; matrix products, arithmetic and copies ran while one was open for 26% -> 21% of each run, Pallas kernels for 19% -> 21%
where the time goes in v2:
time: 307 us; the launch traced here: 306 us
  waiting for transfers between devices  94.1 us (31%)
  Pallas kernels  81.6 us (27%)
  starting transfers between devices  48.6 us (16%)
  other arithmetic  47.9 us (16%)
  local copies, waits for them, and re-layouts  30.7 us (10%)
    ppermute x60, waiting for transfers between devices, swap(): return lax.ppermute(value, axis, [(i, i ^ bit) for i in range(size)])  94.1 us
    ppermute x60, starting transfers between devices, swap(): return lax.ppermute(value, axis, [(i, i ^ bit) for i in range(size)])  48.6 us
    pallas_call x1, Pallas kernels, back(): pl.pallas_call(functools.partial(back_body, count), in_specs=[pl.BlockSpe...  32.6 us
    pallas_call x1, Pallas kernels, front(): pl.pallas_call(functools.partial(front_body, count), out_shape=[jax.Shape...  27.7 us
    pallas_call x1, Pallas kernels, middle(): pl.pallas_call(middle_body, grid=(steps,), in_specs=[shifted(r) for r in...  18.2 us
    unnamed x82, local copies, waits for them, and re-layouts  7.78 us
  transfers between devices with their start and end apart: 60, of which 24 were waited for; matrix products, arithmetic and copies ran while one was open for 21% of the time, Pallas kernels for 21%

profile of v2, /device:TPU:0, one launch (start us, length us, event | category | flops | bytes accessed | tf_op | source)
XLA Modules:
  0.0 306.2 jit_solution(17396682300522098631)
XLA Ops:
  1.2 2.6 collective-permute-start.1
  5.4 2.8 constant_dynamic-slice_fusion.14
  9.1 1.9 collective-permute-start.4
  11.4 1.9 pad_maximum_fusion.15
  21.7 4.2 %collective-permute-done.5 = bf16[192,576]{1,0:T(8,128)(2,1)S(1)} collective-permute-done((bf16[192,576]{1,0:T(8,128)(2,1)}, bf16[192,576]{1,0:T(8,128)(2,1)S(1)}, u32[]{:S(2)}, u32[]{:S(2)}) %collective-permute-start.5) | collective-permute-done | bytes 221216 | tf_op jit(solution)/shard_map/ppermute | solution.py:20
  35.1 27.7 %front.1 = (bf16[1024,192]{1,0:T(8,128)(2,1)}, bf16[3,1024,1024]{2,1,0:T(8,128)(2,1)}, f32[6,1024,64]{2,1,0:T(8,128)}, bf16[3,1024,64]{2,1,0:T(8,128)(2,1)}, bf1...) custom-call(bf16[1024,768]{1,0:T(8,128)(2,1)} %copy-done.6, bf16[768,576]{1,0:T(8,128)(2,1)} %pad_maximum_fusion.4.w_ref, ...), custom_call_target="tpu_custom_call" | custom-call | flops 1711276032 | bytes 11894784 | tf_op jit(solution)/shard_map/front/pallas_call | solution.py:100
  70.2 13.9 %collective-permute-done.19 = bf16[192,768]{1,0:T(8,128)(2,1)S(1)} collective-permute-done((bf16[192,768]{1,0:T(8,128)(2,1)S(1)}, bf16[192,768]{1,0:T(8,128)(2,1)S(1)}, u32[]{:S(2)}, u32[]{:S(2)}) %collective-permute-start.19) | collective-permute-done | bytes 294944 | tf_op jit(solution)/shard_map/ppermute | solution.py:20
  84.2 3.8 %collective-permute-done.20 = bf16[192,768]{1,0:T(8,128)(2,1)S(1)} collective-permute-done((bf16[192,768]{1,0:T(8,128)(2,1)S(1)}, bf16[192,768]{1,0:T(8,128)(2,1)S(1)}, u32[]{:S(2)}, u32[]{:S(2)}) %collective-permute-start.20) | collective-permute-done | bytes 294944 | tf_op jit(solution)/shard_map/ppermute | solution.py:20
  93.6 18.2 %middle.1 = (f32[256,768]{1,0:T(8,128)}, bf16[1024,768]{1,0:T(8,128)(2,1)}, bf16[1024,768]{1,0:T(8,128)(2,1)}, f32[768,768]{1,0:T(8,128)}, f32[768,768]{1,0:T(8,128)}, /*index=5*/f32[8,768]{1,0:T(8,128)}) custom-call(bf16[1024,192]{1,0:T(8,128)(2,1)} %get-tuple-element.56.m0, bf16[1024,192]{1,0:T(8,128)(2,1)} %collective-permute-done.9.m1, ...), custom_call_target="tpu_custom_call" | custom-call | flops 8455716864 | bytes 16121856 | tf_op jit(solution)/shard_map/middle/pallas_call | solution.py:365
  126.1 7.5 %collective-permute-done.45 = bf16[1,384,768]{2,1,0:T(8,128)(2,1)} collective-permute-done((bf16[1,384,768]{2,1,0:T(8,128)(2,1)}, bf16[1,384,768]{2,1,0:T(8,128)(2,1)}, u32[]{:S(2)}, u32[]{:S(2)}) %collective-permute-start.45) | collective-permute-done | bytes 589856 | tf_op jit(solution)/shard_map/ppermute | solution.py:20
  141.5 6.0 %collective-permute-done.24 = bf16[256,768]{1,0:T(8,128)(2,1)S(1)} collective-permute-done((bf16[256,768]{1,0:T(8,128)(2,1)S(1)}, bf16[256,768]{1,0:T(8,128)(2,1)S(1)}, u32[]{:S(2)}, u32[]{:S(2)}) %collective-permute-start.24) | collective-permute-done | bytes 393248 | tf_op jit(solution)/shard_map/ppermute | solution.py:20
  148.8 2.1 convert_reduce_fusion.2
  152.9 2.7 pad_maximum_fusion.20
  158.8 2.1 collective-permute-done.26
  162.0 2.7 collective-permute-start.56
  164.7 2.6 pad_maximum_fusion.z_ref
  167.3 32.6 %back.1 = (f32[4,200,576]{2,1,0:T(8,128)}, bf16[1024,768]{1,0:T(8,128)(2,1)}) custom-call(s32[1]{0:T(128)} %bitcast.7.rank_ref, bf16[1024,768]{1,0:T(8,128)(2,1)} %pad_maximum_fusion.z_ref, bf16[192,768]{1,0:T(8,128)(2,1)} %wp_ref.1, bf16[3,1024,1024]{2,1,0:T(8,128)(2,1)} %get-tuple-element.64.p_ref, f32[6,1024,64]{2,1,0:T(8,128)} %get-tuple-element.65.raw_ref, ...), custom_call_target="tpu_custom_call" | custom-call | flops 3724541952 | bytes 18382848 | tf_op jit(solution)/shard_map/back/pallas_call | solution.py:218
  208.3 2.3 collective-permute-start.57
  210.6 1.9 convolution_bitcast_fusion
  212.5 8.1 %collective-permute-done.48 = bf16[4,24,768]{2,1,0:T(8,128)(2,1)S(1)} collective-permute-done((bf16[4,24,768]{2,1,0:T(8,128)(2,1)S(1)}, bf16[4,24,768]{2,1,0:T(8,128)(2,1)S(1)}, u32[]{:S(2)}, u32[]{:S(2)}) %collective-permute-start.48) | collective-permute-done | bytes 147488 | tf_op jit(solution)/shard_map/ppermute | solution.py:20
  227.2 1.9 collective-permute-start.31
  229.5 8.3 %collective-permute-done.58 = bf16[2,96,768]{2,1,0:T(8,128)(2,1)S(1)} collective-permute-done((bf16[2,96,768]{2,1,0:T(8,128)(2,1)S(1)}, bf16[2,96,768]{2,1,0:T(8,128)(2,1)S(1)}, u32[]{:S(2)}, u32[]{:S(2)}) %collective-permute-start.58) | collective-permute-done | bytes 294944 | tf_op jit(solution)/shard_map/ppermute | solution.py:20
  238.8 4.9 %collective-permute-done.31 = bf16[4,50,576]{2,1,0:T(8,128)(2,1)S(1)} collective-permute-done((bf16[4,50,576]{2,1,0:T(8,128)(2,1)S(1)}, bf16[4,50,576]{2,1,0:T(8,128)(2,1)S(1)}, u32[]{:S(2)}, u32[]{:S(2)}) %collective-permute-start.31) | collective-permute-done | bytes 230432 | tf_op jit(solution)/shard_map/ppermute | solution.py:20
  244.6 2.5 collective-permute-start.41
  247.5 6.5 %collective-permute-done.32 = bf16[4,25,576]{2,1,0:T(8,128)(2,1)S(1)} collective-permute-done((bf16[4,25,576]{2,1,0:T(8,128)(2,1)S(1)}, bf16[4,25,576]{2,1,0:T(8,128)(2,1)S(1)}, u32[]{:S(2)}, u32[]{:S(2)}) %collective-permute-start.32) | collective-permute-done | bytes 115232 | tf_op jit(solution)/shard_map/ppermute | solution.py:20
  256.6 2.3 collective-permute-done.34.p2
  263.7 2.3 collective-permute-start.43
  266.0 5.0 %collective-permute-done.36 = bf16[1,25,2304]{2,1,0:T(8,128)(2,1)S(1)} collective-permute-done((bf16[1,25,2304]{2,1,0:T(8,128)(2,1)}, bf16[1,25,2304]{2,1,0:T(8,128)(2,1)S(1)}, u32[]{:S(2)}, u32[]{:S(2)}) %collective-permute-start.36) | collective-permute-done | bytes 115232 | tf_op jit(solution)/shard_map/ppermute | solution.py:20
  275.2 1.7 bitcast_convert_fusion
  282.7 8.2 %collective-permute-done.54 = bf16[4,24,3072]{2,1,0:T(8,128)(2,1)S(1)} collective-permute-done((bf16[4,24,3072]{2,1,0:T(8,128)(2,1)S(1)}, bf16[4,24,3072]{2,1,0:T(8,128)(2,1)S(1)}, u32[]{:S(2)}, u32[]{:S(2)}) %collective-permute-start.54) | collective-permute-done | bytes 589856 | tf_op jit(solution)/shard_map/ppermute | solution.py:20
  291.1 1.7 bitcast_convert_fusion.1
  292.8 6.7 %collective-permute-done.38 = bf16[4,25,2304]{2,0,1:T(4,128)(2,1)S(1)} collective-permute-done((bf16[4,25,2304]{2,0,1:T(4,128)(2,1)S(1)}, bf16[4,25,2304]{2,0,1:T(4,128)(2,1)S(1)}, u32[]{:S(2)}, u32[]{:S(2)}) %collective-permute-start.38) | collective-permute-done | bytes 460832 | tf_op jit(solution)/shard_map/ppermute | solution.py:20
  (321 shorter events, 105.3 us)
Async XLA Ops:
  0.7 31.2 %collective-permute-start = (bf16[256,768]{1,0:T(8,128)(2,1)}, bf16[256,768]{1,0:T(8,128)(2,1)}, u32[]{:S(2)}, u32[]{:S(2)}) collective-permute-start(bf16[256,768]{1,0:T(8,128)(2,1)} %param.19), channel_id=1, source_target_pairs={{0,1},{1,0},{2,3},{3,2},{4,5},{5,4},{6,7},{7,6},{8,9},{9,8},{10,11... | collective-permute-start | bytes 1179656 | tf_op jit(solution)/shard_map/ppermute | solution.py:20
  1.2 25.8 %collective-permute-start.1 = (bf16[256,768]{1,0:T(8,128)(2,1)}, bf16[256,768]{1,0:T(8,128)(2,1)}, u32[]{:S(2)}, u32[]{:S(2)}) collective-permute-start(bf16[256,768]{1,0:T(8,128)(2,1)} %param.19), channel_id=1, source_target_pairs={{0,2},{1,3},{2,0},{3,1},{4,6},{5,7},{6,4},{7,5},{8,10},{9,11},{10,... | collective-permute-start | bytes 1179656 | tf_op jit(solution)/shard_map/ppermute | solution.py:20
  5.3 12.5 %collective-permute-start.6 = (bf16[16,192]{1,0:T(8,128)(2,1)}, bf16[16,192]{1,0:T(8,128)(2,1)S(1)}, u32[]{:S(2)}, u32[]{:S(2)}) collective-permute-start(bf16[16,192]{1,0:T(8,128)(2,1)} %pack.1), channel_id=1, source_target_pairs={{0,1},{1,0},{2,3},{3,2},{4,5},{5,4},{6,7},{7,6},{8,9},{9,8},{10,11... | collective-permute-start | bytes 18440 | tf_op jit(solution)/shard_map/ppermute | solution.py:20
  9.1 12.6 %collective-permute-start.4 = (bf16[192,576]{1,0:T(8,128)(2,1)}, bf16[192,576]{1,0:T(8,128)(2,1)S(1)}, u32[]{:S(2)}, u32[]{:S(2)}) collective-permute-start(bf16[192,576]{1,0:T(8,128)(2,1)} %pad_maximum_fusion.14), channel_id=1, source_target_pairs={{0,2},{1,3},{2,0},{3,1},{4,6},{5,7},{6,4},{7,5},{8,10},{9,11},{10,... | collective-permute-start | bytes 663560 | tf_op jit(solution)/shard_map/ppermute | solution.py:20
  29.6 36.5 %collective-permute-start.15 = (bf16[192,768]{1,0:T(8,128)(2,1)}, bf16[192,768]{1,0:T(8,128)(2,1)S(1)}, u32[]{:S(2)}, u32[]{:S(2)}) collective-permute-start(bf16[192,768]{1,0:T(8,128)(2,1)} %wp_ref.1), channel_id=1, source_target_pairs={{0,1},{1,0},{2,3},{3,2},{4,5},{5,4},{6,7},{7,6},{8,9},{9,8},{10,11... | collective-permute-start | bytes 884744 | tf_op jit(solution)/shard_map/ppermute | solution.py:20
  29.8 37.0 %collective-permute-start.16 = (bf16[192,768]{1,0:T(8,128)(2,1)}, bf16[192,768]{1,0:T(8,128)(2,1)}, u32[]{:S(2)}, u32[]{:S(2)}) collective-permute-start(bf16[192,768]{1,0:T(8,128)(2,1)} %wp_ref.1), channel_id=1, source_target_pairs={{0,2},{1,3},{2,0},{3,1},{4,6},{5,7},{6,4},{7,5},{8,10},{9,11},{10,... | collective-permute-start | bytes 884744 | tf_op jit(solution)/shard_map/ppermute | solution.py:20
  30.8 58.3 %collective-permute-start.13 = (bf16[256,768]{1,0:T(8,128)(2,1)S(1)}, bf16[256,768]{1,0:T(8,128)(2,1)}, u32[]{:S(2)}, u32[]{:S(2)}) collective-permute-start(bf16[256,768]{1,0:T(8,128)(2,1)S(1)} %get-tuple-element.57.g0), channel_id=1, source_target_pairs={{0,2},{1,3},{2,0},{3,1},{4,6},{5,7},{6,4},{7,5},{8,10},{9,11},{10,... | collective-permute-start | bytes 1179656 | tf_op jit(solution)/shard_map/ppermute | solution.py:20
  62.8 26.7 %collective-permute-start.10 = (bf16[1024,192]{1,0:T(8,128)(2,1)}, bf16[1024,192]{1,0:T(8,128)(2,1)}, u32[]{:S(2)}, u32[]{:S(2)}) collective-permute-start(bf16[1024,192]{1,0:T(8,128)(2,1)} %get-tuple-element.56.m0), channel_id=1, source_target_pairs={{0,2},{1,3},{2,0},{3,1},{4,6},{5,7},{6,4},{7,5},{8,10},{9,11},{10,... | collective-permute-start | bytes 1179656 | tf_op jit(solution)/shard_map/ppermute | solution.py:20
  65.0 19.2 %collective-permute-start.19 = (bf16[192,768]{1,0:T(8,128)(2,1)S(1)}, bf16[192,768]{1,0:T(8,128)(2,1)S(1)}, u32[]{:S(2)}, u32[]{:S(2)}) collective-permute-start(bf16[192,768]{1,0:T(8,128)(2,1)S(1)} %get-tuple-element.140), channel_id=1, source_target_pairs={{0,2},{1,3},{2,0},{3,1},{4,6},{5,7},{6,4},{7,5},{8,10},{9,11},{10,... | collective-permute-start | bytes 884744 | tf_op jit(solution)/shard_map/ppermute | solution.py:20
  66.9 21.2 %collective-permute-start.20 = (bf16[192,768]{1,0:T(8,128)(2,1)S(1)}, bf16[192,768]{1,0:T(8,128)(2,1)S(1)}, u32[]{:S(2)}, u32[]{:S(2)}) collective-permute-start(bf16[192,768]{1,0:T(8,128)(2,1)S(1)} %get-tuple-element.139), channel_id=1, source_target_pairs={{0,3},{1,2},{2,1},{3,0},{4,7},{5,6},{6,5},{7,4},{8,11},{9,10},{10,... | collective-permute-start | bytes 884744 | tf_op jit(solution)/shard_map/ppermute | solution.py:20
  66.9 22.2 %collective-permute-start.18 = (bf16[192,768]{1,0:T(8,128)(2,1)S(1)}, bf16[192,768]{1,0:T(8,128)(2,1)S(1)}, u32[]{:S(2)}, u32[]{:S(2)}) collective-permute-start(bf16[192,768]{1,0:T(8,128)(2,1)S(1)} %get-tuple-element.138), channel_id=1, source_target_pairs={{0,1},{1,0},{2,3},{3,2},{4,5},{5,4},{6,7},{7,6},{8,9},{9,8},{10,11... | collective-permute-start | bytes 884744 | tf_op jit(solution)/shard_map/ppermute | solution.py:20
  117.6 16.0 %collective-permute-start.45 = (bf16[1,384,768]{2,1,0:T(8,128)(2,1)}, bf16[1,384,768]{2,1,0:T(8,128)(2,1)}, u32[]{:S(2)}, u32[]{:S(2)}) collective-permute-start(bf16[1,384,768]{2,1,0:T(8,128)(2,1)} %select_convert_fusion.1), channel_id=1, source_target_pairs={{0,4},{4,0},{8,12},{12,8},{16,20},{20,16},{24,28},{28,24},{1,5},{5... | collective-permute-start | bytes 1769480 | tf_op jit(solution)/shard_map/ppermute | solution.py:20
  124.7 11.2 %collective-permute-start.23 = (bf16[256,768]{1,0:T(8,128)(2,1)S(1)}, bf16[256,768]{1,0:T(8,128)(2,1)S(1)}, u32[]{:S(2)}, u32[]{:S(2)}) collective-permute-start(bf16[256,768]{1,0:T(8,128)(2,1)S(1)} %fusion.16), channel_id=1, source_target_pairs={{0,2},{1,3},{2,0},{3,1},{4,6},{5,7},{6,4},{7,5},{8,10},{9,11},{10,... | collective-permute-start | bytes 1179656 | tf_op jit(solution)/shard_map/ppermute | solution.py:20
  138.4 14.3 %collective-permute-start.46 = (bf16[4,96,768]{2,1,0:T(8,128)(2,1)S(1)}, bf16[4,96,768]{2,1,0:T(8,128)(2,1)S(1)}, u32[]{:S(2)}, u32[]{:S(2)}) collective-permute-start(bf16[4,96,768]{2,1,0:T(8,128)(2,1)S(1)} %select_convert_fusion), channel_id=1, source_target_pairs={{0,4},{4,0},{8,12},{12,8},{16,20},{20,16},{24,28},{28,24},{1,5},{5... | collective-permute-start | bytes 1769480 | tf_op jit(solution)/shard_map/ppermute | solution.py:20
  139.9 18.9 %collective-permute-start.55 = (bf16[1,192,768]{2,1,0:T(8,128)(2,1)}, bf16[1,192,768]{2,1,0:T(8,128)(2,1)}, u32[]{:S(2)}, u32[]{:S(2)}) collective-permute-start(bf16[1,192,768]{2,1,0:T(8,128)(2,1)} %select_convert_fusion.3), channel_id=1, source_target_pairs={{0,8},{4,12},{8,0},{12,4},{16,24},{20,28},{24,16},{28,20},{1,9},{5... | collective-permute-start | bytes 884744 | tf_op jit(solution)/shard_map/ppermute | solution.py:20
  152.2 12.5 %collective-permute-start.25 = (bf16[256,768]{1,0:T(8,128)(2,1)}, bf16[256,768]{1,0:T(8,128)(2,1)}, u32[]{:S(2)}, u32[]{:S(2)}) collective-permute-start(bf16[256,768]{1,0:T(8,128)(2,1)} %get-tuple-element.119), channel_id=1, source_target_pairs={{0,1},{1,0},{2,3},{3,2},{4,5},{5,4},{6,7},{7,6},{8,9},{9,8},{10,11... | collective-permute-start | bytes 1179656 | tf_op jit(solution)/shard_map/ppermute | solution.py:20
  157.2 48.3 %collective-permute-start.47 = (bf16[4,48,768]{2,1,0:T(8,128)(2,1)}, bf16[4,48,768]{2,1,0:T(8,128)(2,1)}, u32[]{:S(2)}, u32[]{:S(2)}) collective-permute-start(bf16[4,48,768]{2,1,0:T(8,128)(2,1)} %select_convert_fusion.4), channel_id=1, source_target_pairs={{0,8},{4,12},{8,0},{12,4},{16,24},{20,28},{24,16},{28,20},{1,9},{5... | collective-permute-start | bytes 884744 | tf_op jit(solution)/shard_map/ppermute | solution.py:20
  162.0 45.3 %collective-permute-start.56 = (bf16[1,96,768]{2,1,0:T(8,128)(2,1)S(1)}, bf16[1,96,768]{2,1,0:T(8,128)(2,1)}, u32[]{:S(2)}, u32[]{:S(2)}) collective-permute-start(bf16[1,96,768]{2,1,0:T(8,128)(2,1)S(1)} %select_convert_fusion.7), channel_id=1, source_target_pairs={{0,16},{4,20},{8,24},{12,28},{16,0},{20,4},{24,8},{28,12},{1,17},{... | collective-permute-start | bytes 442376 | tf_op jit(solution)/shard_map/ppermute | solution.py:20
  204.0 43.3 %collective-permute-start.28 = (bf16[512,768]{1,0:T(8,128)(2,1)S(1)}, bf16[512,768]{1,0:T(8,128)(2,1)S(1)}, u32[]{:S(2)}, u32[]{:S(2)}) collective-permute-start(bf16[512,768]{1,0:T(8,128)(2,1)S(1)} %pad_maximum_fusion.7), channel_id=1, source_target_pairs={{0,1},{1,0},{2,3},{3,2},{4,5},{5,4},{6,7},{7,6},{8,9},{9,8},{10,11... | collective-permute-start | bytes 2359304 | tf_op jit(solution)/shard_map/ppermute | solution.py:20
  204.3 22.5 %collective-permute-start.30 = (bf16[4,100,576]{2,0,1:T(4,128)(2,1)S(1)}, bf16[4,100,576]{2,0,1:T(4,128)(2,1)S(1)}, u32[]{:S(2)}, u32[]{:S(2)}) collective-permute-start(bf16[4,100,576]{2,0,1:T(4,128)(2,1)S(1)} %copy.39), channel_id=1, source_target_pairs={{0,4},{4,0},{8,12},{12,8},{16,20},{20,16},{24,28},{28,24},{1,5},{5... | collective-permute-start | bytes 1382408 | tf_op jit(solution)/shard_map/ppermute | solution.py:20
  206.6 14.0 %collective-permute-start.48 = (bf16[4,24,768]{2,1,0:T(8,128)(2,1)S(1)}, bf16[4,24,768]{2,1,0:T(8,128)(2,1)S(1)}, u32[]{:S(2)}, u32[]{:S(2)}) collective-permute-start(bf16[4,24,768]{2,1,0:T(8,128)(2,1)S(1)} %select_convert_fusion.8), channel_id=1, source_target_pairs={{0,16},{4,20},{8,24},{12,28},{16,0},{20,4},{24,8},{28,12},{1,17},{... | collective-permute-start | bytes 442376 | tf_op jit(solution)/shard_map/ppermute | solution.py:20
  208.3 14.5 %collective-permute-start.57 = (bf16[1,96,768]{2,1,0:T(8,128)(2,1)S(1)}, bf16[1,96,768]{2,1,0:T(8,128)(2,1)S(1)}, u32[]{:S(2)}, u32[]{:S(2)}) collective-permute-start(bf16[1,96,768]{2,1,0:T(8,128)(2,1)S(1)} %add_convert_fusion.2), channel_id=1, source_target_pairs={{0,16},{4,20},{8,24},{12,28},{16,0},{20,4},{24,8},{28,12},{1,17},{... | collective-permute-start | bytes 442376 | tf_op jit(solution)/shard_map/ppermute | solution.py:20
  224.8 13.0 %collective-permute-start.58 = (bf16[2,96,768]{2,1,0:T(8,128)(2,1)S(1)}, bf16[2,96,768]{2,1,0:T(8,128)(2,1)S(1)}, u32[]{:S(2)}, u32[]{:S(2)}) collective-permute-start(bf16[2,96,768]{2,1,0:T(8,128)(2,1)S(1)} %maximum_select_fusion.9), channel_id=1, source_target_pairs={{0,8},{4,12},{8,0},{12,4},{16,24},{20,28},{24,16},{28,20},{1,9},{5... | collective-permute-start | bytes 884744 | tf_op jit(solution)/shard_map/ppermute | solution.py:20
  226.3 20.8 %collective-permute-start.52 = (bf16[1,24,3072]{2,1,0:T(8,128)(2,1)S(1)}, bf16[1,24,3072]{2,1,0:T(8,128)(2,1)S(1)}, u32[]{:S(2)}, u32[]{:S(2)}) collective-permute-start(bf16[1,24,3072]{2,1,0:T(8,128)(2,1)S(1)} %maximum_bitcast_fusion), channel_id=1, source_target_pairs={{0,16},{4,20},{8,24},{12,28},{16,0},{20,4},{24,8},{28,12},{1,17},{... | collective-permute-start | bytes 442376 | tf_op jit(solution)/shard_map/ppermute | solution.py:20
  227.2 16.5 %collective-permute-start.31 = (bf16[4,50,576]{2,1,0:T(8,128)(2,1)S(1)}, bf16[4,50,576]{2,1,0:T(8,128)(2,1)S(1)}, u32[]{:S(2)}, u32[]{:S(2)}) collective-permute-start(bf16[4,50,576]{2,1,0:T(8,128)(2,1)S(1)} %select_convert_fusion.5), channel_id=1, source_target_pairs={{0,8},{4,12},{8,0},{12,4},{16,24},{20,28},{24,16},{28,20},{1,9},{5... | collective-permute-start | bytes 691208 | tf_op jit(solution)/shard_map/ppermute | solution.py:20
  229.4 15.1 %collective-permute-start.40 = (bf16[1,48,768]{2,1,0:T(8,128)(2,1)S(1)}, bf16[1,48,768]{2,1,0:T(8,128)(2,1)S(1)}, u32[]{:S(2)}, u32[]{:S(2)}) collective-permute-start(bf16[1,48,768]{2,1,0:T(8,128)(2,1)S(1)} %select_convert_fusion.10), channel_id=1, source_target_pairs={{0,8},{4,12},{8,0},{12,4},{16,24},{20,28},{24,16},{28,20},{1,9},{5... | collective-permute-start | bytes 221192 | tf_op jit(solution)/shard_map/ppermute | solution.py:20
  237.9 35.8 %collective-permute-start.59 = (bf16[4,96,768]{2,1,0:T(8,128)(2,1)S(1)}, bf16[4,96,768]{2,1,0:T(8,128)(2,1)}, u32[]{:S(2)}, u32[]{:S(2)}) collective-permute-start(bf16[4,96,768]{2,1,0:T(8,128)(2,1)S(1)} %maximum_select_fusion.5), channel_id=1, source_target_pairs={{0,4},{4,0},{8,12},{12,8},{16,20},{20,16},{24,28},{28,24},{1,5},{5... | collective-permute-start | bytes 1769480 | tf_op jit(solution)/shard_map/ppermute | solution.py:20
  244.6 10.8 %collective-permute-start.41 = (bf16[1,24,768]{2,1,0:T(8,128)(2,1)S(1)}, bf16[1,24,768]{2,1,0:T(8,128)(2,1)S(1)}, u32[]{:S(2)}, u32[]{:S(2)}) collective-permute-start(bf16[1,24,768]{2,1,0:T(8,128)(2,1)S(1)} %select_convert_fusion.11), channel_id=1, source_target_pairs={{0,16},{4,20},{8,24},{12,28},{16,0},{20,4},{24,8},{28,12},{1,17},{... | collective-permute-start | bytes 110600 | tf_op jit(solution)/shard_map/ppermute | solution.py:20
  247.1 25.6 %collective-permute-start.53 = (bf16[2,24,3072]{2,1,0:T(8,128)(2,1)S(1)}, bf16[2,24,3072]{2,1,0:T(8,128)(2,1)S(1)}, u32[]{:S(2)}, u32[]{:S(2)}) collective-permute-start(bf16[2,24,3072]{2,1,0:T(8,128)(2,1)S(1)} %maximum_select_fusion.8), channel_id=1, source_target_pairs={{0,8},{4,12},{8,0},{12,4},{16,24},{20,28},{24,16},{28,20},{1,9},{5... | collective-permute-start | bytes 884744 | tf_op jit(solution)/shard_map/ppermute | solution.py:20
  262.8 14.0 %collective-permute-start.29 = (bf16[256,768]{1,0:T(8,128)(2,1)S(1)}, bf16[256,768]{1,0:T(8,128)(2,1)S(1)}, u32[]{:S(2)}, u32[]{:S(2)}) collective-permute-start(bf16[256,768]{1,0:T(8,128)(2,1)S(1)} %fusion.13), channel_id=1, source_target_pairs={{0,2},{1,3},{2,0},{3,1},{4,6},{5,7},{6,4},{7,5},{8,10},{9,11},{10,... | collective-permute-start | bytes 1179656 | tf_op jit(solution)/shard_map/ppermute | solution.py:20
  272.8 18.1 %collective-permute-start.54 = (bf16[4,24,3072]{2,1,0:T(8,128)(2,1)S(1)}, bf16[4,24,3072]{2,1,0:T(8,128)(2,1)S(1)}, u32[]{:S(2)}, u32[]{:S(2)}) collective-permute-start(bf16[4,24,3072]{2,1,0:T(8,128)(2,1)S(1)} %maximum_select_fusion.4), channel_id=1, source_target_pairs={{0,4},{4,0},{8,12},{12,8},{16,20},{20,16},{24,28},{28,24},{1,5},{5... | collective-permute-start | bytes 1769480 | tf_op jit(solution)/shard_map/ppermute | solution.py:20
  280.5 19.0 %collective-permute-start.38 = (bf16[4,25,2304]{2,0,1:T(4,128)(2,1)S(1)}, bf16[4,25,2304]{2,0,1:T(4,128)(2,1)S(1)}, u32[]{:S(2)}, u32[]{:S(2)}) collective-permute-start(bf16[4,25,2304]{2,0,1:T(4,128)(2,1)S(1)} %copy.41), channel_id=1, source_target_pairs={{0,4},{4,0},{8,12},{12,8},{16,20},{20,16},{24,28},{28,24},{1,5},{5... | collective-permute-start | bytes 1382408 | tf_op jit(solution)/shard_map/ppermute | solution.py:20
  (67 other events, 468.6 us)

commit v3 on v1

--- a/solution.py
+++ b/solution.py
@@ -119,7 +119,7 @@
 def back_body(
     count, rank_ref, z_ref, wp_ref, p_ref, raw_ref, q_ref, k_ref, v_ref, x_ref, w_ref, vec_ref,
     head_ref, early_ref, out_ref, da_ref, sum_ref, bias_ref, heads_ref, dw_ref, g_ref, dk_ref,
-    dv_ref, dq_ref,
+    dv_ref, dq_ref, dkt_ref, dvt_ref,
 ):
     heads, rows, size = q_ref.shape
     scaling = size**-0.5
@@ -142,8 +142,11 @@
             delta = jnp.sum(probs * grad_probs, axis=-1, keepdims=True)
             grad_scores = (probs * (grad_probs - delta)).astype(BF16)
             dq_ref[at] = dot(grad_scores, k_ref[h])
-            dk_ref[...] += left_cross(grad_scores, q_ref[h, at])
-            dv_ref[...] += left_cross(low, grad)
+            dk_ref[...] += left_cross(q_ref[h, at], grad_scores)
+            dv_ref[...] += left_cross(grad, low)
+
+        dkt_ref[...] = dk_ref[...].T
+        dvt_ref[...] = dv_ref[...].T
 
         @pl.loop(0, steps)
         def _(step):
@@ -155,7 +158,7 @@
             g_ref[at, h * size : (h + 1) * size] = norm_back(
                 grad * head_ref[0:1], unit, scale
             ).astype(BF16)
-            grad = dk_ref[at]
+            grad = dkt_ref[at]
             unit, scale = norm_parts(raw_ref[heads + h, at])
             heads_ref[2:3] += jnp.sum(grad * unit, axis=0, keepdims=True)
             first = (heads + h) * size
@@ -163,7 +166,7 @@
                 BF16
             )
             first = (2 * heads + h) * size
-            g_ref[at, first : first + size] = dv_ref[at].astype(BF16)
+            g_ref[at, first : first + size] = dvt_ref[at].astype(BF16)
 
     @pl.loop(0, steps)
     def _(step):
@@ -226,6 +229,8 @@
             pltpu.VMEM((8, size), F32),
             pltpu.VMEM((width, 3 * part), F32),
             pltpu.VMEM((rows, 3 * part), BF16),
+            pltpu.VMEM((size, rows), F32),
+            pltpu.VMEM((size, rows), F32),
             pltpu.VMEM((rows, size), F32),
             pltpu.VMEM((rows, size), F32),
             pltpu.VMEM((rows, size), F32),
@@ -432,11 +437,12 @@
     def spread(pieces):
         return [pieces[0], near(pieces[1]), far(pieces[2]), swap(pieces[3], "fsdp", fs_size, 3)]
 
-    def collect(low):
+    def collect(low, mark=None):
         low = [low[r * count : (r + 1) * count] for r in range(4)]
         other = near(jnp.concatenate([low[1], low[3]], axis=0)).astype(F32)
         first = low[0].astype(F32) + other[:count]
         sent = (low[2].astype(F32) + other[count:]).astype(BF16)
+        sent = sent if mark is None else after(sent, mark)
         return first + far(sent).astype(F32), sent
 
     def at(r):
@@ -474,21 +480,24 @@
     def after(value, other):
         return lax.optimization_barrier((value, other))[0]
 
-    w_proj_pieces = gather(after(proj_weight, w_qkv))
     up_pieces = [
-        lax.dynamic_slice_in_dim(after(fc1_weight, w_qkv), at(r) * hidden_own, hidden_own, 1)
-        for r in range(4)
+        lax.dynamic_slice_in_dim(fc1_weight, at(r) * hidden_own, hidden_own, 1) for r in range(4)
     ]
-    up_pieces[1] = near(up_pieces[1])
-    up_pieces[2] = far(up_pieces[2])
-    up_pieces[3] = swap(up_pieces[3], "fsdp", fs_size, 3)
-    w_up = ordered(up_pieces, 0)
     weights_valid = valid_mask.astype(F32)[:, None]
     grad_mlp_own = (cotangent.astype(F32) * weights_valid).astype(BF16)
-    grad_mlp_pieces = gather(after(grad_mlp_own, w_qkv))
-    ids = jnp.concatenate(
-        [lax.dynamic_slice_in_dim(segment_ids, at(r) * count, count) for r in range(4)]
-    )
+    late = jnp.concatenate([proj_weight, grad_mlp_own, up_pieces[2]], axis=0)
+    both = proj_weight.shape[0] + count
+    late = far(after(late, w_qkv))
+    up_pieces[3] = swap(after(up_pieces[3], w_qkv), "fsdp", fs_size, 3)
+    up_pieces[1] = near(after(up_pieces[1], w_qkv))
+    up_pieces[2] = late[both:]
+    first = near(jnp.concatenate([proj_weight, grad_mlp_own], axis=0))
+    last = near(late[:both])
+    cut = proj_weight.shape[0]
+    w_proj_pieces = [proj_weight, first[:cut], late[:cut], last[:cut]]
+    grad_mlp_pieces = [grad_mlp_own, first[cut:], late[cut:both], last[cut:]]
+    w_up = ordered(up_pieces, 0)
+    ids = ordered([segment_ids[i * count : (i + 1) * count] for i in range(4)], 0)
 
     b_qkv = jnp.concatenate(own_columns(b_qkv_all, rank))
     vectors_one = jnp.concatenate([gain_one[None], shift_one[None]])
@@ -497,8 +506,9 @@
         count, tokens_all, w_qkv, vectors_one, b_qkv[None], head_vectors, ids
     )
     vectors = jnp.concatenate([b_proj[None], gain_two[None], shift_two[None]])
+    mixed_pieces = gather(mixed_own)
     branch_own, mlp_part, grad_two_part, total_down, total_up, sums_middle = middle(
-        count, gather(mixed_own), tokens_all, grad_mlp_pieces, w_proj_pieces, w_up, fc2_weight, vectors,
+        count, mixed_pieces, tokens_all, grad_mlp_pieces, w_proj_pieces, w_up, fc2_weight, vectors,
         fc1_bias.astype(F32)[None],
     )
     inputs = tokens.astype(F32)
@@ -545,7 +555,10 @@
         return spread([lax.dynamic_index_in_dim(share, at(r), 0, False) for r in range(4)])
 
     grad_normed_two, mark_two = collect(grad_two_part)
-    grad_out = grad_mlp_own.astype(F32)
+    total_down = after(total_down, mark_two)
+    sums_middle = after(sums_middle, mark_two)
+    mlp_part = after(mlp_part, mark_two)
+    grad_out = after(grad_mlp_own, mark_two).astype(F32)
     unit_two, scale_two = norm_parts(hidden_one)
     grad_hidden = grad_out + norm_back(grad_normed_two * gain_two, unit_two, scale_two)
     grad_branch_own = grad_hidden.astype(BF16)
@@ -571,7 +584,7 @@
         grad_normed_one * gain_one, unit_one, scale_one
     )
 
-    branch_mlp = collect(after(mlp_part, lead))[0] + b_down
+    branch_mlp = collect(mlp_part, lead)[0] + b_down
     result = hidden_one + branch_mlp
     rms_sums = jnp.stack(
         [
@@ -585,9 +598,8 @@
     rms_sums = jnp.broadcast_to(rms_sums[:, None], (4, 128))
     for bit in (1, 2):
         rms_sums = rms_sums + swap(rms_sums, "fsdp", fs_size, bit)
-    for bit in rounds:
-        rms_sums = rms_sums + swap(rms_sums, "dp", dp_size, bit)
-    sums = rms_sums[:, 0]
+    rms_rows = jnp.pad(rms_sums[:, 0], (0, width - 4))[None]
+    rms_rows = jnp.pad(rms_rows, ((0, dp_size - 1), (0, 0)))
 
     count_rounds = len(rounds)
     pieces_last = to_rows(share_last)
@@ -595,18 +607,21 @@
     last, seen_back = unite(arrange(share_rows, rank, pieces_last))
     seen = [*seen, pieces_last[3], *seen_back]
 
-    early = [mark_two, grad_branch_own] + [grad_branch_low] * (count_rounds - 2)
+    early = [grad_normed_two, grad_branch_own] + [grad_branch_low] * (count_rounds - 2)
     share_down, seen_down, _ = halve(total_down[None], early)
     grad_down, _ = unite(share_down[0], [lead, seen[0], seen[1]])
     grad_down = grad_down.astype(F32).reshape(hidden_own, width)
     total_up = after(total_up, seen_down[0])
-    late = [grad_branch_own] + [lead] * (count_rounds - 1)
+    late = [grad_branch_own, lead] + [seen[0]] * (count_rounds - 2)
     share_up, _, _ = halve(total_up.reshape(fs_size, rows_own, hidden_own), late)
-    grad_up, _ = unite(ordered(to_rows(share_up), 1), [seen[1], seen[2], seen[count_rounds]])
+    pieces_up = to_rows(share_up)
+    pieces_up[3] = after(pieces_up[3], seen[1])
+    grad_up, _ = unite(ordered(pieces_up, 1), [seen[2], seen[3]])
     grad_up = grad_up.astype(F32).reshape(rows_own, hidden)
-    share_proj, _, _ = halve(total_proj[None], seen[:count_rounds])
-    grad_proj, _ = unite(share_proj[0], seen[count_rounds:])
-    grad_proj = grad_proj.astype(F32).reshape(rows_own, width)
+    total_proj = after(jnp.concatenate([total_proj, rms_rows], axis=0), seen[0])
+    share_proj, _, _ = halve(total_proj[None], seen[1 : count_rounds + 1], tail=dp_size)
+    grad_proj, _ = unite(share_proj[0], seen[count_rounds + 1 : -1])
+    grad_proj = grad_proj.astype(F32)
     last = last.astype(F32)
     grad_qkv = last[:, :share_rows].reshape(rows_own, 3 * width)
     table = last[:, share_rows, : 3 * part]
@@ -617,6 +632,7 @@
     finals += [flat[2 * rows_own : 3 * rows_own], flat[:rows_own], flat[rows_own : 2 * rows_own]]
     finals += [flat[3 * rows_own : 3 * rows_own + hidden_own]]
     finals += [flat[3 * rows_own + hidden_own : 4 * rows_own + hidden_own]]
+    sums = grad_proj[0, share_rows, :4]
     return (
         result.astype(BF16),
         tokens_grad,
@@ -627,7 +643,7 @@
         finals[3],
         finals[4],
         finals[5],
-        grad_proj,
+        grad_proj[:, :share_rows].reshape(rows_own, width),
         finals[6],
         finals[7],
         finals[8],

time: 321 us -> 324 us (level)
  local copies, waits for them, and re-layouts: 34.6 us -> 42.8 us
  waiting for transfers between devices: 82.4 us -> 90 us
  starting transfers between devices: 58.2 us -> 50.9 us
  other arithmetic: 59.5 us -> 54.3 us
    slice x0 -> x7, local copies, waits for them, and re-layouts: none -> 9.48 us  [the longest x3 4.32 us: on_device(): grad_mlp_pieces = [grad_mlp_own, first[cut:], late[cut:both], last[cut:]]]
    ppermute x65 -> x58, waiting for transfers between devices: 82.4 us -> 90 us  [swap(): return lax.ppermute(value, axis, [(i, i ^ bit) for i in range(size)])]
    ppermute x65 -> x58, starting transfers between devices: 58.2 us -> 50.9 us  [swap(): return lax.ppermute(value, axis, [(i, i ^ bit) for i in range(size)])]
    concatenate x3, other arithmetic: 4.43 us -> 1.03 us  [on_device(): jnp.concatenate(own_columns(qkv_weight, at(r)), axis=1)]
    select_n x5 -> x8, other arithmetic: 0.87 us -> 4.23 us  [ordered(): lax.select_n(at(i), *[pieces[j] for j in range(4)])]
    unnamed x100 -> x112, local copies, waits for them, and re-layouts: 7.4 us -> 4.52 us
  transfers between devices with their start and end apart: 65 -> 58, of which waited for: 21 -> 22; matrix products, arithmetic and copies ran while one was open for 26% -> 28% of each run, Pallas kernels for 19% -> 19%
where the time goes in v3:
time: 324 us; the launch traced here: 323 us
  waiting for transfers between devices  90 us (28%)
  Pallas kernels  81.4 us (25%)
  other arithmetic  54.3 us (17%)
  starting transfers between devices  50.9 us (16%)
  local copies, waits for them, and re-layouts  42.8 us (13%)
    ppermute x58, waiting for transfers between devices, swap(): return lax.ppermute(value, axis, [(i, i ^ bit) for i in range(size)])  90 us
    ppermute x58, starting transfers between devices, swap(): return lax.ppermute(value, axis, [(i, i ^ bit) for i in range(size)])  50.9 us
    pallas_call x1, Pallas kernels, back(): pl.pallas_call(functools.partial(back_body, count), in_specs=[pl.BlockSpe...  32.5 us
    pallas_call x1, Pallas kernels, front(): pl.pallas_call(functools.partial(front_body, count), out_shape=[jax.Shape...  27.7 us
    pallas_call x1, Pallas kernels, middle(): pl.pallas_call(middle_body, grid=(steps,), in_specs=[shifted(r) for r in...  18.1 us
  transfers between devices with their start and end apart: 58, of which 22 were waited for; matrix products, arithmetic and copies ran while one was open for 28% of the time, Pallas kernels for 19%

profile of v3, /device:TPU:0, one launch (start us, length us, event | category | flops | bytes accessed | tf_op | source)
XLA Modules:
  0.0 322.6 jit_solution(7892910742180390809)
XLA Ops:
  2.2 3.0 collective-permute-start.7
  5.7 2.9 constant_dynamic-slice_fusion.14
  17.0 2.0 collective-permute-start.4
  22.1 3.7 %collective-permute-done.4 = bf16[192,576]{1,0:T(8,128)(2,1)S(1)} collective-permute-done((bf16[192,576]{1,0:T(8,128)(2,1)S(1)}, bf16[192,576]{1,0:T(8,128)(2,1)S(1)}, u32[]{:S(2)}, u32[]{:S(2)}) %collective-permute-start.4) | collective-permute-done | bytes 221216 | tf_op jit(solution)/shard_map/ppermute | solution.py:20
  25.8 3.9 %collective-permute-done.5 = bf16[192,576]{1,0:T(8,128)(2,1)S(1)} collective-permute-done((bf16[192,576]{1,0:T(8,128)(2,1)S(1)}, bf16[192,576]{1,0:T(8,128)(2,1)S(1)}, u32[]{:S(2)}, u32[]{:S(2)}) %collective-permute-start.5) | collective-permute-done | bytes 221216 | tf_op jit(solution)/shard_map/ppermute | solution.py:20
  39.4 27.7 %front.1 = (bf16[1024,192]{1,0:T(8,128)(2,1)}, bf16[3,1024,1024]{2,1,0:T(8,128)(2,1)}, f32[6,1024,64]{2,1,0:T(8,128)}, bf16[3,1024,64]{2,1,0:T(8,128)(2,1)}, bf1...) custom-call(bf16[1024,768]{1,0:T(8,128)(2,1)} %copy-done.14, bf16[768,576]{1,0:T(8,128)(2,1)} %pad_maximum_fusion.4.w_ref, ...), custom_call_target="tpu_custom_call" | custom-call | flops 1711276032 | bytes 11894784 | tf_op jit(solution)/shard_map/front/pallas_call | solution.py:100
  79.9 2.4 collective-permute-done.10.m2
  83.1 2.9 collective-permute-done.16
  91.7 18.1 %middle.1 = (f32[256,768]{1,0:T(8,128)}, bf16[1024,768]{1,0:T(8,128)(2,1)}, bf16[1024,768]{1,0:T(8,128)(2,1)}, f32[768,768]{1,0:T(8,128)}, f32[768,768]{1,0:T(8,128)}, /*index=5*/f32[8,768]{1,0:T(8,128)}) custom-call(bf16[1024,192]{1,0:T(8,128)(2,1)} %get-tuple-element.60.m0, bf16[1024,192]{1,0:T(8,128)(2,1)} %collective-permute-done.9.m1, ...), custom_call_target="tpu_custom_call" | custom-call | flops 8455716864 | bytes 16121856 | tf_op jit(solution)/shard_map/middle/pallas_call | solution.py:365
  118.5 2.7 select_convert_fusion.1
  124.1 2.8 collective-permute-done.19
  128.3 2.0 convert_reduce_fusion.2
  143.2 2.1 fusion.17
  145.3 2.6 collective-permute-done.53
  148.7 2.8 collective-permute-start.54
  151.4 4.4 %collective-permute-done.44 = bf16[4,96,768]{2,1,0:T(8,128)(2,1)S(1)} collective-permute-done((bf16[4,96,768]{2,1,0:T(8,128)(2,1)S(1)}, bf16[4,96,768]{2,1,0:T(8,128)(2,1)S(1)}, u32[]{:S(2)}, u32[]{:S(2)}) %collective-permute-start.44) | collective-permute-done | bytes 589856 | tf_op jit(solution)/shard_map/ppermute | solution.py:20
  160.2 32.5 %back.1 = (f32[4,200,576]{2,1,0:T(8,128)}, bf16[1024,768]{1,0:T(8,128)(2,1)}) custom-call(s32[1]{0:T(128)} %bitcast.7.rank_ref, bf16[1024,768]{1,0:T(8,128)(2,1)} %copy-done, bf16[192,768]{1,0:T(8,128)(2,1)} %wp_ref.1, bf16[3,1024,1024]{2,1,0:T(8,128)(2,1)} %get-tuple-element.69.p_ref, f32[6,1024,64]{2,1,0:T(8,128)} %get-tuple-element.70.raw_ref, ...), custom_call_target="tpu_custom_call" | custom-call | flops 3724541952 | bytes 18382848 | tf_op jit(solution)/shard_map/back/pallas_call | solution.py:218
  195.4 2.7 collective-permute-start.55
  201.8 2.8 collective-permute-done.55
  206.0 3.6 %collective-permute-done.23 = bf16[256,768]{1,0:T(8,128)(2,1)S(1)} collective-permute-done((bf16[256,768]{1,0:T(8,128)(2,1)S(1)}, bf16[256,768]{1,0:T(8,128)(2,1)S(1)}, u32[]{:S(2)}, u32[]{:S(2)}) %collective-permute-start.23) | collective-permute-done | bytes 393248 | tf_op jit(solution)/shard_map/ppermute | solution.py:20
  209.7 2.1 fusion.10
  211.8 2.7 pad_maximum_fusion.28
  220.6 4.4 %collective-permute-done.46 = bf16[4,24,768]{2,1,0:T(8,128)(2,1)S(1)} collective-permute-done((bf16[4,24,768]{2,1,0:T(8,128)(2,1)S(1)}, bf16[4,24,768]{2,1,0:T(8,128)(2,1)S(1)}, u32[]{:S(2)}, u32[]{:S(2)}) %collective-permute-start.46) | collective-permute-done | bytes 147488 | tf_op jit(solution)/shard_map/ppermute | solution.py:20
  227.3 8.9 %collective-permute-done.27 = bf16[4,50,576]{2,1,0:T(8,128)(2,1)S(1)} collective-permute-done((bf16[4,50,576]{2,1,0:T(8,128)(2,1)S(1)}, bf16[4,50,576]{2,1,0:T(8,128)(2,1)S(1)}, u32[]{:S(2)}, u32[]{:S(2)}) %collective-permute-start.27) | collective-permute-done | bytes 230432 | tf_op jit(solution)/shard_map/ppermute | solution.py:20
  238.6 3.0 collective-permute-start.28
  241.6 12.7 %collective-permute-done.37 = bf16[1,100,768]{2,1,0:T(8,128)(2,1)S(1)} collective-permute-done((bf16[1,100,768]{2,1,0:T(8,128)(2,1)S(1)}, bf16[1,100,768]{2,1,0:T(8,128)(2,1)S(1)}, u32[]{:S(2)}, u32[]{:S(2)}) %collective-permute-start.37) | collective-permute-done | bytes 153632 | tf_op jit(solution)/shard_map/ppermute | solution.py:20
  255.9 3.0 collective-permute-done.38
  267.0 2.3 collective-permute-start.32
  272.3 4.9 %collective-permute-done.32 = bf16[1,25,2304]{2,1,0:T(8,128)(2,1)S(1)} collective-permute-done((bf16[1,25,2304]{2,1,0:T(8,128)(2,1)}, bf16[1,25,2304]{2,1,0:T(8,128)(2,1)S(1)}, u32[]{:S(2)}, u32[]{:S(2)}) %collective-permute-start.32) | collective-permute-done | bytes 115232 | tf_op jit(solution)/shard_map/ppermute | solution.py:20
  278.4 2.7 collective-permute-done.40
  281.2 2.1 collective-permute-start.41
  293.9 17.7 %collective-permute-done.42 = bf16[4,25,768]{2,1,0:T(8,128)(2,1)S(1)} collective-permute-done((bf16[4,25,768]{2,1,0:T(8,128)(2,1)S(1)}, bf16[4,25,768]{2,1,0:T(8,128)(2,1)S(1)}, u32[]{:S(2)}, u32[]{:S(2)}) %collective-permute-start.42) | collective-permute-done | bytes 153632 | tf_op jit(solution)/shard_map/ppermute | solution.py:20
  (369 shorter events, 126.7 us)
Async XLA Ops:
  2.2 12.6 %collective-permute-start.7 = (bf16[16,192]{1,0:T(8,128)(2,1)}, bf16[16,192]{1,0:T(8,128)(2,1)S(1)}, u32[]{:S(2)}, u32[]{:S(2)}) collective-permute-start(bf16[16,192]{1,0:T(8,128)(2,1)} %pack.1), channel_id=1, source_target_pairs={{0,2},{1,3},{2,0},{3,1},{4,6},{5,7},{6,4},{7,5},{8,10},{9,11},{10,... | collective-permute-start | bytes 18440 | tf_op jit(solution)/shard_map/ppermute | solution.py:20
  5.2 31.0 %collective-permute-start = (bf16[256,768]{1,0:T(8,128)(2,1)}, bf16[256,768]{1,0:T(8,128)(2,1)}, u32[]{:S(2)}, u32[]{:S(2)}) collective-permute-start(bf16[256,768]{1,0:T(8,128)(2,1)} %param.19), channel_id=1, source_target_pairs={{0,1},{1,0},{2,3},{3,2},{4,5},{5,4},{6,7},{7,6},{8,9},{9,8},{10,11... | collective-permute-start | bytes 1179656 | tf_op jit(solution)/shard_map/ppermute | solution.py:20
  5.7 26.5 %collective-permute-start.1 = (bf16[256,768]{1,0:T(8,128)(2,1)}, bf16[256,768]{1,0:T(8,128)(2,1)}, u32[]{:S(2)}, u32[]{:S(2)}) collective-permute-start(bf16[256,768]{1,0:T(8,128)(2,1)} %param.19), channel_id=1, source_target_pairs={{0,2},{1,3},{2,0},{3,1},{4,6},{5,7},{6,4},{7,5},{8,10},{9,11},{10,... | collective-permute-start | bytes 1179656 | tf_op jit(solution)/shard_map/ppermute | solution.py:20
  9.4 12.5 %collective-permute-start.3 = (bf16[192,576]{1,0:T(8,128)(2,1)}, bf16[192,576]{1,0:T(8,128)(2,1)}, u32[]{:S(2)}, u32[]{:S(2)}) collective-permute-start(bf16[192,576]{1,0:T(8,128)(2,1)} %pad_maximum_fusion.17), channel_id=1, source_target_pairs={{0,1},{1,0},{2,3},{3,2},{4,5},{5,4},{6,7},{7,6},{8,9},{9,8},{10,11... | collective-permute-start | bytes 663560 | tf_op jit(solution)/shard_map/ppermute | solution.py:20
  22.0 53.9 %collective-permute-start.12 = (bf16[448,768]{1,0:T(8,128)(2,1)}, bf16[448,768]{1,0:T(8,128)(2,1)}, u32[]{:S(2)}, u32[]{:S(2)}) collective-permute-start(bf16[448,768]{1,0:T(8,128)(2,1)} %pad_maximum_fusion.9), channel_id=1, source_target_pairs={{0,1},{1,0},{2,3},{3,2},{4,5},{5,4},{6,7},{7,6},{8,9},{9,8},{10,11... | collective-permute-start | bytes 2064392 | tf_op jit(solution)/shard_map/ppermute | solution.py:20
  33.8 38.5 %collective-permute-start.13 = (bf16[640,768]{1,0:T(8,128)(2,1)}, bf16[640,768]{1,0:T(8,128)(2,1)S(1)}, u32[]{:S(2)}, u32[]{:S(2)}) collective-permute-start(bf16[640,768]{1,0:T(8,128)(2,1)} %pad_maximum_fusion.5), channel_id=1, source_target_pairs={{0,2},{1,3},{2,0},{3,1},{4,6},{5,7},{6,4},{7,5},{8,10},{9,11},{10,... | collective-permute-start | bytes 2949128 | tf_op jit(solution)/shard_map/ppermute | solution.py:20
  67.2 15.1 %collective-permute-start.10 = (bf16[1024,192]{1,0:T(8,128)(2,1)}, bf16[1024,192]{1,0:T(8,128)(2,1)}, u32[]{:S(2)}, u32[]{:S(2)}) collective-permute-start(bf16[1024,192]{1,0:T(8,128)(2,1)} %get-tuple-element.60.m0), channel_id=1, source_target_pairs={{0,2},{1,3},{2,0},{3,1},{4,6},{5,7},{6,4},{7,5},{8,10},{9,11},{10,... | collective-permute-start | bytes 1179656 | tf_op jit(solution)/shard_map/ppermute | solution.py:20
  68.6 14.5 %collective-permute-start.15 = (bf16[192,768]{1,0:T(8,128)(2,1)}, bf16[192,768]{1,0:T(8,128)(2,1)S(1)}, u32[]{:S(2)}, u32[]{:S(2)}) collective-permute-start(bf16[192,768]{1,0:T(8,128)(2,1)} %get-tuple-element.62), channel_id=1, source_target_pairs={{0,1},{1,0},{2,3},{3,2},{4,5},{5,4},{6,7},{7,6},{8,9},{9,8},{10,11... | collective-permute-start | bytes 884744 | tf_op jit(solution)/shard_map/ppermute | solution.py:20
  68.6 17.4 %collective-permute-start.16 = (bf16[192,768]{1,0:T(8,128)(2,1)}, bf16[192,768]{1,0:T(8,128)(2,1)S(1)}, u32[]{:S(2)}, u32[]{:S(2)}) collective-permute-start(bf16[192,768]{1,0:T(8,128)(2,1)} %get-tuple-element.63), channel_id=1, source_target_pairs={{0,3},{1,2},{2,1},{3,0},{4,7},{5,6},{6,5},{7,4},{8,11},{9,10},{10,... | collective-permute-start | bytes 884744 | tf_op jit(solution)/shard_map/ppermute | solution.py:20
  73.2 15.0 %collective-permute-start.14 = (bf16[448,768]{1,0:T(8,128)(2,1)}, bf16[448,768]{1,0:T(8,128)(2,1)}, u32[]{:S(2)}, u32[]{:S(2)}) collective-permute-start(bf16[448,768]{1,0:T(8,128)(2,1)} %slice.475), channel_id=1, source_target_pairs={{0,1},{1,0},{2,3},{3,2},{4,5},{5,4},{6,7},{7,6},{8,9},{9,8},{10,11... | collective-permute-start | bytes 2064392 | tf_op jit(solution)/shard_map/ppermute | solution.py:20
  79.4 12.3 %collective-permute-start.9 = (bf16[1024,192]{1,0:T(8,128)(2,1)}, bf16[1024,192]{1,0:T(8,128)(2,1)}, u32[]{:S(2)}, u32[]{:S(2)}) collective-permute-start(bf16[1024,192]{1,0:T(8,128)(2,1)} %get-tuple-element.60.m0), channel_id=1, source_target_pairs={{0,1},{1,0},{2,3},{3,2},{4,5},{5,4},{6,7},{7,6},{8,9},{9,8},{10,11... | collective-permute-start | bytes 1179656 | tf_op jit(solution)/shard_map/ppermute | solution.py:20
  121.2 15.8 %collective-permute-start.43 = (bf16[1,384,768]{2,1,0:T(8,128)(2,1)}, bf16[1,384,768]{2,1,0:T(8,128)(2,1)}, u32[]{:S(2)}, u32[]{:S(2)}) collective-permute-start(bf16[1,384,768]{2,1,0:T(8,128)(2,1)} %select_convert_fusion.1), channel_id=1, source_target_pairs={{0,4},{4,0},{8,12},{12,8},{16,20},{20,16},{24,28},{28,24},{1,5},{5... | collective-permute-start | bytes 1769480 | tf_op jit(solution)/shard_map/ppermute | solution.py:20
  124.0 18.0 %collective-permute-start.18 = (bf16[512,768]{1,0:T(8,128)(2,1)}, bf16[512,768]{1,0:T(8,128)(2,1)}, u32[]{:S(2)}, u32[]{:S(2)}) collective-permute-start(bf16[512,768]{1,0:T(8,128)(2,1)} %pad_maximum_fusion.7), channel_id=1, source_target_pairs={{0,1},{1,0},{2,3},{3,2},{4,5},{5,4},{6,7},{7,6},{8,9},{9,8},{10,11... | collective-permute-start | bytes 2359304 | tf_op jit(solution)/shard_map/ppermute | solution.py:20
  130.3 15.0 %collective-permute-start.21 = (bf16[256,768]{1,0:T(8,128)(2,1)}, bf16[256,768]{1,0:T(8,128)(2,1)}, u32[]{:S(2)}, u32[]{:S(2)}) collective-permute-start(bf16[256,768]{1,0:T(8,128)(2,1)} %get-tuple-element.124), channel_id=1, source_target_pairs={{0,2},{1,3},{2,0},{3,1},{4,6},{5,7},{6,4},{7,5},{8,10},{9,11},{10,... | collective-permute-start | bytes 1179656 | tf_op jit(solution)/shard_map/ppermute | solution.py:20
  130.6 26.9 %collective-permute-start.20 = (bf16[256,768]{1,0:T(8,128)(2,1)}, bf16[256,768]{1,0:T(8,128)(2,1)}, u32[]{:S(2)}, u32[]{:S(2)}) collective-permute-start(bf16[256,768]{1,0:T(8,128)(2,1)} %get-tuple-element.124), channel_id=1, source_target_pairs={{0,1},{1,0},{2,3},{3,2},{4,5},{5,4},{6,7},{7,6},{8,9},{9,8},{10,11... | collective-permute-start | bytes 1179656 | tf_op jit(solution)/shard_map/ppermute | solution.py:20
  140.4 15.5 %collective-permute-start.44 = (bf16[4,96,768]{2,1,0:T(8,128)(2,1)S(1)}, bf16[4,96,768]{2,1,0:T(8,128)(2,1)S(1)}, u32[]{:S(2)}, u32[]{:S(2)}) collective-permute-start(bf16[4,96,768]{2,1,0:T(8,128)(2,1)S(1)} %select_convert_fusion), channel_id=1, source_target_pairs={{0,4},{4,0},{8,12},{12,8},{16,20},{20,16},{24,28},{28,24},{1,5},{5... | collective-permute-start | bytes 1769480 | tf_op jit(solution)/shard_map/ppermute | solution.py:20
  148.7 46.6 %collective-permute-start.54 = (bf16[1,96,768]{2,1,0:T(8,128)(2,1)}, bf16[1,96,768]{2,1,0:T(8,128)(2,1)S(1)}, u32[]{:S(2)}, u32[]{:S(2)}) collective-permute-start(bf16[1,96,768]{2,1,0:T(8,128)(2,1)} %select_convert_fusion.8), channel_id=1, source_target_pairs={{0,16},{4,20},{8,24},{12,28},{16,0},{20,4},{24,8},{28,12},{1,17},{... | collective-permute-start | bytes 442376 | tf_op jit(solution)/shard_map/ppermute | solution.py:20
  156.9 48.1 %collective-permute-start.45 = (bf16[4,48,768]{2,1,0:T(8,128)(2,1)}, bf16[4,48,768]{2,1,0:T(8,128)(2,1)}, u32[]{:S(2)}, u32[]{:S(2)}) collective-permute-start(bf16[4,48,768]{2,1,0:T(8,128)(2,1)} %select_convert_fusion.4), channel_id=1, source_target_pairs={{0,8},{4,12},{8,0},{12,4},{16,24},{20,28},{24,16},{28,20},{1,9},{5... | collective-permute-start | bytes 884744 | tf_op jit(solution)/shard_map/ppermute | solution.py:20
  198.4 21.9 %collective-permute-start.26 = (bf16[4,100,576]{2,0,1:T(4,128)(2,1)S(1)}, bf16[4,100,576]{2,0,1:T(4,128)(2,1)S(1)}, u32[]{:S(2)}, u32[]{:S(2)}) collective-permute-start(bf16[4,100,576]{2,0,1:T(4,128)(2,1)S(1)} %copy.39), channel_id=1, source_target_pairs={{0,4},{4,0},{8,12},{12,8},{16,20},{20,16},{24,28},{28,24},{1,5},{5... | collective-permute-start | bytes 1382408 | tf_op jit(solution)/shard_map/ppermute | solution.py:20
  201.7 53.3 %collective-permute-start.24 = (bf16[512,768]{1,0:T(8,128)(2,1)S(1)}, bf16[512,768]{1,0:T(8,128)(2,1)S(1)}, u32[]{:S(2)}, u32[]{:S(2)}) collective-permute-start(bf16[512,768]{1,0:T(8,128)(2,1)S(1)} %pad_maximum_fusion.8), channel_id=1, source_target_pairs={{0,1},{1,0},{2,3},{3,2},{4,5},{5,4},{6,7},{7,6},{8,9},{9,8},{10,11... | collective-permute-start | bytes 2359304 | tf_op jit(solution)/shard_map/ppermute | solution.py:20
  204.6 15.9 %collective-permute-start.56 = (bf16[2,96,768]{2,1,0:T(8,128)(2,1)S(1)}, bf16[2,96,768]{2,1,0:T(8,128)(2,1)S(1)}, u32[]{:S(2)}, u32[]{:S(2)}) collective-permute-start(bf16[2,96,768]{2,1,0:T(8,128)(2,1)S(1)} %maximum_select_fusion.9), channel_id=1, source_target_pairs={{0,8},{4,12},{8,0},{12,4},{16,24},{20,28},{24,16},{28,20},{1,9},{5... | collective-permute-start | bytes 884744 | tf_op jit(solution)/shard_map/ppermute | solution.py:20
  225.1 12.5 %collective-permute-start.49 = (bf16[24,768]{1,0:T(8,128)(2,1)S(1)}, bf16[24,768]{1,0:T(8,128)(2,1)S(1)}, u32[]{:S(2)}, u32[]{:S(2)}) collective-permute-start(bf16[24,768]{1,0:T(8,128)(2,1)S(1)} %get-tuple-element.192), channel_id=1, source_target_pairs={{0,3},{1,2},{2,1},{3,0},{4,7},{5,6},{6,5},{7,4},{8,11},{9,10},{10,... | collective-permute-start | bytes 110600 | tf_op jit(solution)/shard_map/ppermute | solution.py:20
  225.9 12.5 %collective-permute-start.48 = (bf16[24,768]{1,0:T(8,128)(2,1)S(1)}, bf16[24,768]{1,0:T(8,128)(2,1)S(1)}, u32[]{:S(2)}, u32[]{:S(2)}) collective-permute-start(bf16[24,768]{1,0:T(8,128)(2,1)S(1)} %get-tuple-element.193), channel_id=1, source_target_pairs={{0,2},{1,3},{2,0},{3,1},{4,6},{5,7},{6,4},{7,5},{8,10},{9,11},{10,... | collective-permute-start | bytes 110600 | tf_op jit(solution)/shard_map/ppermute | solution.py:20
  236.1 47.1 %collective-permute-start.57 = (bf16[4,96,768]{2,1,0:T(8,128)(2,1)S(1)}, bf16[4,96,768]{2,1,0:T(8,128)(2,1)S(1)}, u32[]{:S(2)}, u32[]{:S(2)}) collective-permute-start(bf16[4,96,768]{2,1,0:T(8,128)(2,1)S(1)} %maximum_select_fusion.5), channel_id=1, source_target_pairs={{0,4},{4,0},{8,12},{12,8},{16,20},{20,16},{24,28},{28,24},{1,5},{5... | collective-permute-start | bytes 1769480 | tf_op jit(solution)/shard_map/ppermute | solution.py:20
  237.6 16.7 %collective-permute-start.37 = (bf16[1,100,768]{2,1,0:T(8,128)(2,1)S(1)}, bf16[1,100,768]{2,1,0:T(8,128)(2,1)S(1)}, u32[]{:S(2)}, u32[]{:S(2)}) collective-permute-start(bf16[1,100,768]{2,1,0:T(8,128)(2,1)S(1)} %select_convert_fusion.7), channel_id=1, source_target_pairs={{0,4},{4,0},{8,12},{12,8},{16,20},{20,16},{24,28},{28,24},{1,5},{5... | collective-permute-start | bytes 460808 | tf_op jit(solution)/shard_map/ppermute | solution.py:20
  238.5 30.8 %collective-permute-start.50 = (bf16[1,24,3072]{2,1,0:T(8,128)(2,1)S(1)}, bf16[1,24,3072]{2,1,0:T(8,128)(2,1)}, u32[]{:S(2)}, u32[]{:S(2)}) collective-permute-start(bf16[1,24,3072]{2,1,0:T(8,128)(2,1)S(1)} %maximum_bitcast_fusion), channel_id=1, source_target_pairs={{0,16},{4,20},{8,24},{12,28},{16,0},{20,4},{24,8},{28,12},{1,17},{... | collective-permute-start | bytes 442376 | tf_op jit(solution)/shard_map/ppermute | solution.py:20
  238.6 20.3 %collective-permute-start.28 = (bf16[4,25,576]{2,1,0:T(8,128)(2,1)S(1)}, bf16[4,25,576]{2,1,0:T(8,128)(2,1)S(1)}, u32[]{:S(2)}, u32[]{:S(2)}) collective-permute-start(bf16[4,25,576]{2,1,0:T(8,128)(2,1)S(1)} %select_convert_fusion.6), channel_id=1, source_target_pairs={{0,16},{4,20},{8,24},{12,28},{16,0},{20,4},{24,8},{28,12},{1,17},{... | collective-permute-start | bytes 345608 | tf_op jit(solution)/shard_map/ppermute | solution.py:20
  263.1 23.4 %collective-permute-start.25 = (bf16[256,768]{1,0:T(8,128)(2,1)}, bf16[256,768]{1,0:T(8,128)(2,1)}, u32[]{:S(2)}, u32[]{:S(2)}) collective-permute-start(bf16[256,768]{1,0:T(8,128)(2,1)} %fusion.13), channel_id=1, source_target_pairs={{0,2},{1,3},{2,0},{3,1},{4,6},{5,7},{6,4},{7,5},{8,10},{9,11},{10,... | collective-permute-start | bytes 1179656 | tf_op jit(solution)/shard_map/ppermute | solution.py:20
  270.3 14.8 %collective-permute-start.51 = (bf16[2,24,3072]{2,1,0:T(8,128)(2,1)S(1)}, bf16[2,24,3072]{2,1,0:T(8,128)(2,1)S(1)}, u32[]{:S(2)}, u32[]{:S(2)}) collective-permute-start(bf16[2,24,3072]{2,1,0:T(8,128)(2,1)S(1)} %maximum_select_fusion.8), channel_id=1, source_target_pairs={{0,8},{4,12},{8,0},{12,4},{16,24},{20,28},{24,16},{28,20},{1,9},{5... | collective-permute-start | bytes 884744 | tf_op jit(solution)/shard_map/ppermute | solution.py:20
  285.2 34.2 %collective-permute-start.52 = (bf16[4,24,3072]{2,1,0:T(8,128)(2,1)S(1)}, bf16[4,24,3072]{2,1,0:T(8,128)(2,1)}, u32[]{:S(2)}, u32[]{:S(2)}) collective-permute-start(bf16[4,24,3072]{2,1,0:T(8,128)(2,1)S(1)} %maximum_select_fusion.4), channel_id=1, source_target_pairs={{0,4},{4,0},{8,12},{12,8},{16,20},{20,16},{24,28},{28,24},{1,5},{5... | collective-permute-start | bytes 1769480 | tf_op jit(solution)/shard_map/ppermute | solution.py:20
  290.6 23.8 %collective-permute-start.34 = (bf16[4,25,2304]{2,0,1:T(4,128)(2,1)S(1)}, bf16[4,25,2304]{2,0,1:T(4,128)(2,1)S(1)}, u32[]{:S(2)}, u32[]{:S(2)}) collective-permute-start(bf16[4,25,2304]{2,0,1:T(4,128)(2,1)S(1)} %copy.41), channel_id=1, source_target_pairs={{0,4},{4,0},{8,12},{12,8},{16,20},{20,16},{24,28},{28,24},{1,5},{5... | collective-permute-start | bytes 1382408 | tf_op jit(solution)/shard_map/ppermute | solution.py:20
  291.9 19.7 %collective-permute-start.42 = (bf16[4,25,768]{2,1,0:T(8,128)(2,1)S(1)}, bf16[4,25,768]{2,1,0:T(8,128)(2,1)S(1)}, u32[]{:S(2)}, u32[]{:S(2)}) collective-permute-start(bf16[4,25,768]{2,1,0:T(8,128)(2,1)S(1)} %maximum_select_fusion.10), channel_id=1, source_target_pairs={{0,4},{4,0},{8,12},{12,8},{16,20},{20,16},{24,28},{28,24},{1,5},{5... | collective-permute-start | bytes 460808 | tf_op jit(solution)/shard_map/ppermute | solution.py:20
  (80 other events, 531.5 us)

commit v4 on v2

--- a/solution.py
+++ b/solution.py
@@ -443,7 +443,8 @@
         first = low[0].astype(F32) + other[:count]
         sent = (low[2].astype(F32) + other[count:]).astype(BF16)
         sent = sent if mark is None else after(sent, mark)
-        return first + far(sent).astype(F32), sent
+        other = far(sent)
+        return first + other.astype(F32), sent
 
     def at(r):
         return rank ^ r
@@ -527,7 +528,8 @@
             upper = (place & bit) != 0
             sent = jnp.where(upper, low, high).astype(BF16)
             lead = sent if order == 0 else lead
-            other = held_back(swap(sent, "dp", dp_size, bit), marks, order)
+            other = swap(sent, "dp", dp_size, bit)
+            other = held_back(other, marks, order)
             seen.append(other)
             total = jnp.where(upper, high, low).astype(F32) + other.astype(F32)
             first, second = total[:, :size], total[:, size:]
@@ -537,7 +539,8 @@
         share = share.astype(BF16)[None]
         seen = []
         for order, bit in enumerate(reversed(rounds)):
-            other = held_back(swap(share, "dp", dp_size, bit), marks, order)
+            other = swap(share, "dp", dp_size, bit)
+            other = held_back(other, marks, order)
             seen.append(other)
             upper = (place & bit) != 0
             share = jnp.where(
@@ -552,13 +555,41 @@
         return spread([lax.dynamic_index_in_dim(share, at(r), 0, False) for r in range(4)])
 
     grad_normed_two, mark_two = collect(grad_two_part)
-    grad_out = grad_mlp_own.astype(F32)
+    total_down = after(total_down, mark_two)
+    sums_middle = after(sums_middle, mark_two)
+    grad_out = after(grad_mlp_own, mark_two).astype(F32)
     unit_two, scale_two = norm_parts(hidden_one)
     grad_hidden = grad_out + norm_back(grad_normed_two * gain_two, unit_two, scale_two)
     grad_branch_own = grad_hidden.astype(BF16)
     grad_branch_low = jnp.concatenate(gather(grad_branch_own), axis=0)
     total_proj = left_cross(mixed_own, grad_branch_low)
-    branch_mlp = collect(mlp_part, grad_normed_two)[0] + b_down
+    own_sums = [sums_middle[1], sums_middle[2], jnp.sum(grad_branch_own.astype(F32), axis=0)]
+    own_sums = jnp.stack(own_sums).reshape(3, fs_size, rows_own)
+    bias_up = jnp.where(jnp.arange(fs_size)[:, None] == rank, sums_middle[0][None], 0.0)
+    bias_down = jnp.sum(grad_out, axis=0).reshape(fs_size, rows_own)
+    early_rows = jnp.concatenate(
+        [own_sums[0], own_sums[1], own_sums[2], bias_up, bias_down], axis=1
+    )
+    early_rows = jnp.pad(early_rows, ((0, 0), (0, 9 * part - early_rows.shape[1])))
+    early_rows = early_rows.reshape(fs_size, 3, 3 * part)
+    total_last, grad_one_part = back(
+        count, dp_size, rank, grad_branch_low, proj_weight, probs, raw, queries, keys, values,
+        tokens_all, w_qkv, vectors_one, head_vectors, early_rows,
+    )
+    share_last, seen, lead = halve(total_last, tail=dp_size)
+    grad_normed_one, _ = collect(after(grad_one_part, lead))
+    unit_one, scale_one = norm_parts(inputs)
+    tokens_grad = grad_hidden + norm_back(
+        grad_normed_one * gain_one, unit_one, scale_one
+    )
+
+    count_rounds = len(rounds)
+    pieces_last = to_rows(share_last)
+    share_rows = rows_own // dp_size
+    last, seen_back = unite(arrange(share_rows, rank, pieces_last))
+    seen = [*seen, pieces_last[3], *seen_back]
+
+    branch_mlp = collect(after(mlp_part, lead))[0] + b_down
     result = hidden_one + branch_mlp
     rms_sums = jnp.stack(
         [
@@ -569,42 +600,22 @@
         ]
     )
 
-    own_sums = [sums_middle[1], sums_middle[2], jnp.sum(grad_branch_own.astype(F32), axis=0)]
-    own_sums = jnp.stack(own_sums).reshape(3, fs_size, rows_own)
-    bias_up = jnp.where(jnp.arange(fs_size)[:, None] == rank, sums_middle[0][None], 0.0)
-    bias_down = jnp.sum(grad_out, axis=0).reshape(fs_size, rows_own)
-    early_rows = jnp.concatenate(
-        [own_sums[0], own_sums[1], own_sums[2], bias_up, bias_down]
-        + [jnp.broadcast_to(rms_sums[None], (fs_size, 4))],
-        axis=1,
-    )
-    early_rows = jnp.pad(early_rows, ((0, 0), (0, 9 * part - early_rows.shape[1])))
-    early_rows = early_rows.reshape(fs_size, 3, 3 * part)
-    total_last, grad_one_part = back(
-        count, dp_size, rank, grad_branch_low, proj_weight, probs, raw, queries, keys, values,
-        tokens_all, w_qkv, vectors_one, head_vectors, early_rows,
-    )
-    share_last, seen, lead = halve(total_last, tail=dp_size)
-    grad_normed_one, _ = collect(after(grad_one_part, lead))
-    unit_one, scale_one = norm_parts(inputs)
-    tokens_grad = grad_hidden + norm_back(
-        grad_normed_one * gain_one, unit_one, scale_one
-    )
-
-    count_rounds = len(rounds)
-    pieces_last = to_rows(share_last)
-    share_rows = rows_own // dp_size
-    last, seen_back = unite(arrange(share_rows, rank, pieces_last))
-    seen = [*seen, pieces_last[3], *seen_back]
-
-    early = [mark_two, grad_branch_own] + [grad_branch_low] * (count_rounds - 2)
+    rms_sums = jnp.broadcast_to(rms_sums[:, None], (4, 128))
+    hops = [("fsdp", fs_size, 1), ("fsdp", fs_size, 2)] + [("dp", dp_size, bit) for bit in rounds]
+    for order, (axis, size, bit) in enumerate(hops):
+        other = swap(rms_sums, axis, size, bit)
+        rms_sums = rms_sums + after(other, seen[min(order + 1, len(seen) - 2)])
+    sums = rms_sums[:, 0]
+
+    early = [grad_branch_own, grad_branch_own] + [grad_branch_low] * (count_rounds - 2)
     share_down, seen_down, _ = halve(total_down[None], early)
-    grad_down, _ = unite(share_down[0], [lead, seen[0], seen[1]])
+    grad_down, _ = unite(share_down[0], [seen[0], seen[0], seen[1]])
     grad_down = grad_down.astype(F32).reshape(hidden_own, width)
     total_up = after(total_up, seen_down[0])
-    late = [grad_branch_own] + [lead] * (count_rounds - 1)
+    late = [grad_branch_own, lead] + [seen[0]] * (count_rounds - 2)
     share_up, _, _ = halve(total_up.reshape(fs_size, rows_own, hidden_own), late)
-    grad_up, _ = unite(ordered(to_rows(share_up), 1), [seen[1], seen[2], seen[count_rounds]])
+    pieces_up = to_rows(share_up)
+    grad_up, _ = unite(ordered(pieces_up, 1), [seen[1], seen[2], seen[count_rounds]])
     grad_up = grad_up.astype(F32).reshape(rows_own, hidden)
     share_proj, _, _ = halve(total_proj[None], seen[:count_rounds])
     grad_proj, _ = unite(share_proj[0], seen[count_rounds:])
@@ -619,7 +630,6 @@
     finals += [flat[2 * rows_own : 3 * rows_own], flat[:rows_own], flat[rows_own : 2 * rows_own]]
     finals += [flat[3 * rows_own : 3 * rows_own + hidden_own]]
     finals += [flat[3 * rows_own + hidden_own : 4 * rows_own + hidden_own]]
-    sums = flat[4 * rows_own + hidden_own :]
     return (
         result.astype(BF16),
         tokens_grad,

time: 307 us -> 310 us (level)
  starting transfers between devices: 48.6 us -> 61.8 us
  local copies, waits for them, and re-layouts: 30.7 us -> 26.1 us
  other arithmetic: 47.9 us -> 44.3 us
    ppermute x60 -> x65, starting transfers between devices: 48.6 us -> 61.8 us  [swap(): return lax.ppermute(value, axis, [(i, i ^ bit) for i in range(size)])]
    unnamed x82 -> x88, local copies, waits for them, and re-layouts: 7.78 us -> 5.86 us
    ppermute x60 -> x65, waiting for transfers between devices: 94.1 us -> 92.5 us  [swap(): return lax.ppermute(value, axis, [(i, i ^ bit) for i in range(size)])]
  transfers between devices with their start and end apart: 60 -> 65, of which waited for: 24 -> 25; matrix products, arithmetic and copies ran while one was open for 21% -> 20% of each run, Pallas kernels for 21% -> 20%
where the time goes in v4:
time: 310 us
  waiting for transfers between devices  92.5 us (30%)
  Pallas kernels  81.6 us (26%)
  starting transfers between devices  61.8 us (20%)
  other arithmetic  44.3 us (14%)
  local copies, waits for them, and re-layouts  26.1 us (8%)
    ppermute x65, waiting for transfers between devices, swap(): return lax.ppermute(value, axis, [(i, i ^ bit) for i in range(size)])  92.5 us
    ppermute x65, starting transfers between devices, swap(): return lax.ppermute(value, axis, [(i, i ^ bit) for i in range(size)])  61.8 us
    pallas_call x1, Pallas kernels, back(): pl.pallas_call(functools.partial(back_body, count), in_specs=[pl.BlockSpe...  32.5 us
    pallas_call x1, Pallas kernels, front(): pl.pallas_call(functools.partial(front_body, count), out_shape=[jax.Shape...  27.8 us
    pallas_call x1, Pallas kernels, middle(): pl.pallas_call(middle_body, grid=(steps,), in_specs=[shifted(r) for r in...  18.2 us
  transfers between devices with their start and end apart: 65, of which 25 were waited for; matrix products, arithmetic and copies ran while one was open for 20% of the time, Pallas kernels for 20%

profile of v4, /device:TPU:0, one launch (start us, length us, event | category | flops | bytes accessed | tf_op | source)
XLA Modules:
  0.0 309.6 jit_solution(13122903670100522637)
XLA Ops:
  2.2 3.0 collective-permute-start.7
  5.7 2.8 constant_dynamic-slice_fusion.14
  10.3 1.9 pad_maximum_fusion.15
  17.3 2.0 collective-permute-start.4
  22.0 4.4 %collective-permute-done.4 = bf16[192,576]{1,0:T(8,128)(2,1)S(1)} collective-permute-done((bf16[192,576]{1,0:T(8,128)(2,1)}, bf16[192,576]{1,0:T(8,128)(2,1)S(1)}, u32[]{:S(2)}, u32[]{:S(2)}) %collective-permute-start.4) | collective-permute-done | bytes 221216 | tf_op jit(solution)/shard_map/ppermute | solution.py:20
  26.3 4.0 %collective-permute-done.5 = bf16[192,576]{1,0:T(8,128)(2,1)S(1)} collective-permute-done((bf16[192,576]{1,0:T(8,128)(2,1)}, bf16[192,576]{1,0:T(8,128)(2,1)S(1)}, u32[]{:S(2)}, u32[]{:S(2)}) %collective-permute-start.5) | collective-permute-done | bytes 221216 | tf_op jit(solution)/shard_map/ppermute | solution.py:20
  37.7 27.8 %front.1 = (bf16[1024,192]{1,0:T(8,128)(2,1)}, bf16[3,1024,1024]{2,1,0:T(8,128)(2,1)}, f32[6,1024,64]{2,1,0:T(8,128)}, bf16[3,1024,64]{2,1,0:T(8,128)(2,1)}, bf1...) custom-call(bf16[1024,768]{1,0:T(8,128)(2,1)} %copy-done.7, bf16[768,576]{1,0:T(8,128)(2,1)} %pad_maximum_fusion.4.w_ref, ...), custom_call_target="tpu_custom_call" | custom-call | flops 1711276032 | bytes 11894784 | tf_op jit(solution)/shard_map/front/pallas_call | solution.py:100
  72.0 14.1 %collective-permute-done.20 = bf16[192,768]{1,0:T(8,128)(2,1)S(1)} collective-permute-done((bf16[192,768]{1,0:T(8,128)(2,1)S(1)}, bf16[192,768]{1,0:T(8,128)(2,1)S(1)}, u32[]{:S(2)}, u32[]{:S(2)}) %collective-permute-start.20) | collective-permute-done | bytes 294944 | tf_op jit(solution)/shard_map/ppermute | solution.py:20
  86.7 5.8 %collective-permute-done.19 = bf16[192,768]{1,0:T(8,128)(2,1)S(1)} collective-permute-done((bf16[192,768]{1,0:T(8,128)(2,1)S(1)}, bf16[192,768]{1,0:T(8,128)(2,1)S(1)}, u32[]{:S(2)}, u32[]{:S(2)}) %collective-permute-start.19) | collective-permute-done | bytes 294944 | tf_op jit(solution)/shard_map/ppermute | solution.py:20
  96.2 18.2 %middle.1 = (f32[256,768]{1,0:T(8,128)}, bf16[1024,768]{1,0:T(8,128)(2,1)}, bf16[1024,768]{1,0:T(8,128)(2,1)}, f32[768,768]{1,0:T(8,128)}, f32[768,768]{1,0:T(8,128)}, /*index=5*/f32[8,768]{1,0:T(8,128)}) custom-call(bf16[1024,192]{1,0:T(8,128)(2,1)} %get-tuple-element.64.m0, bf16[1024,192]{1,0:T(8,128)(2,1)} %copy-done.38, ...), custom_call_target="tpu_custom_call" | custom-call | flops 8455716864 | bytes 16121856 | tf_op jit(solution)/shard_map/middle/pallas_call | solution.py:365
  122.7 6.8 %collective-permute-done.22 = bf16[256,768]{1,0:T(8,128)(2,1)S(1)} collective-permute-done((bf16[256,768]{1,0:T(8,128)(2,1)S(1)}, bf16[256,768]{1,0:T(8,128)(2,1)S(1)}, u32[]{:S(2)}, u32[]{:S(2)}) %collective-permute-start.22) | collective-permute-done | bytes 393248 | tf_op jit(solution)/shard_map/ppermute | solution.py:20
  132.9 2.4 collective-permute-done.45
  138.5 2.5 select_convert_fusion
  144.8 2.7 collective-permute-start.56
  149.1 2.4 pad_maximum_fusion.z_ref
  151.5 32.5 %back.1 = (f32[4,200,576]{2,1,0:T(8,128)}, bf16[1024,768]{1,0:T(8,128)(2,1)}) custom-call(s32[1]{0:T(128)} %bitcast.7.rank_ref, bf16[1024,768]{1,0:T(8,128)(2,1)} %pad_maximum_fusion.z_ref, bf16[192,768]{1,0:T(8,128)(2,1)} %wp_ref.1, bf16[3,1024,1024]{2,1,0:T(8,128)(2,1)} %get-tuple-element.72.p_ref, f32[6,1024,64]{2,1,0:T(8,128)} %get-tuple-element.73.raw_ref, ...), custom_call_target="tpu_custom_call" | custom-call | flops 3724541952 | bytes 18382848 | tf_op jit(solution)/shard_map/back/pallas_call | solution.py:218
  193.1 8.2 %collective-permute-done.47 = bf16[4,48,768]{2,1,0:T(8,128)(2,1)S(1)} collective-permute-done((bf16[4,48,768]{2,1,0:T(8,128)(2,1)S(1)}, bf16[4,48,768]{2,1,0:T(8,128)(2,1)S(1)}, u32[]{:S(2)}, u32[]{:S(2)}) %collective-permute-start.47) | collective-permute-done | bytes 294944 | tf_op jit(solution)/shard_map/ppermute | solution.py:20
  202.8 8.3 %collective-permute-done.48 = bf16[4,24,768]{2,1,0:T(8,128)(2,1)S(1)} collective-permute-done((bf16[4,24,768]{2,1,0:T(8,128)(2,1)S(1)}, bf16[4,24,768]{2,1,0:T(8,128)(2,1)S(1)}, u32[]{:S(2)}, u32[]{:S(2)}) %collective-permute-start.48) | collective-permute-done | bytes 147488 | tf_op jit(solution)/shard_map/ppermute | solution.py:20
  220.8 8.3 %collective-permute-done.31 = bf16[4,50,576]{2,1,0:T(8,128)(2,1)S(1)} collective-permute-done((bf16[4,50,576]{2,1,0:T(8,128)(2,1)S(1)}, bf16[4,50,576]{2,1,0:T(8,128)(2,1)S(1)}, u32[]{:S(2)}, u32[]{:S(2)}) %collective-permute-start.31) | collective-permute-done | bytes 230432 | tf_op jit(solution)/shard_map/ppermute | solution.py:20
  230.2 2.7 collective-permute-done.52
  232.9 3.4 %collective-permute-start.32 = (bf16[4,25,576]{2,1,0:T(8,128)(2,1)S(1)}, bf16[4,25,576]{2,1,0:T(8,128)(2,1)S(1)}, u32[]{:S(2)}, u32[]{:S(2)}) collective-permute-start(bf16[4,25,576]{2,1,0:T(8,128)(2,1)S(1)} %select_convert_fusion.6), channel_id=1, source_target_pairs={{0,16},{4,20},{8,24},{12,28},{16,0},{20,4},{24,8},{28,12},{1,17},{... | collective-permute-start | bytes 345608 | tf_op jit(solution)/shard_map/ppermute | solution.py:20
  237.3 6.6 %collective-permute-done.32 = bf16[4,25,576]{2,1,0:T(8,128)(2,1)S(1)} collective-permute-done((bf16[4,25,576]{2,1,0:T(8,128)(2,1)S(1)}, bf16[4,25,576]{2,1,0:T(8,128)(2,1)S(1)}, u32[]{:S(2)}, u32[]{:S(2)}) %collective-permute-start.32) | collective-permute-done | bytes 115232 | tf_op jit(solution)/shard_map/ppermute | solution.py:20
  247.4 2.4 collective-permute-start.53
  256.4 2.1 collective-permute-start.43
  262.0 2.9 collective-permute-done.36
  271.4 2.1 fusion.10
  273.5 2.7 pad_maximum_fusion.20
  279.7 2.3 collective-permute-done.61
  283.8 2.5 collective-permute-done.62
  286.3 2.6 collective-permute-start.63
  289.0 2.2 collective-permute-done.63
  291.2 2.6 collective-permute-start.64
  (343 shorter events, 112.8 us)
Async XLA Ops:
  2.2 12.5 %collective-permute-start.7 = (bf16[16,192]{1,0:T(8,128)(2,1)}, bf16[16,192]{1,0:T(8,128)(2,1)S(1)}, u32[]{:S(2)}, u32[]{:S(2)}) collective-permute-start(bf16[16,192]{1,0:T(8,128)(2,1)} %pack.1), channel_id=1, source_target_pairs={{0,2},{1,3},{2,0},{3,1},{4,6},{5,7},{6,4},{7,5},{8,10},{9,11},{10,... | collective-permute-start | bytes 18440 | tf_op jit(solution)/shard_map/ppermute | solution.py:20
  5.2 12.1 %collective-permute-start.6 = (bf16[16,192]{1,0:T(8,128)(2,1)}, bf16[16,192]{1,0:T(8,128)(2,1)S(1)}, u32[]{:S(2)}, u32[]{:S(2)}) collective-permute-start(bf16[16,192]{1,0:T(8,128)(2,1)} %pack.1), channel_id=1, source_target_pairs={{0,1},{1,0},{2,3},{3,2},{4,5},{5,4},{6,7},{7,6},{8,9},{9,8},{10,11... | collective-permute-start | bytes 18440 | tf_op jit(solution)/shard_map/ppermute | solution.py:20
  5.2 29.2 %collective-permute-start = (bf16[256,768]{1,0:T(8,128)(2,1)}, bf16[256,768]{1,0:T(8,128)(2,1)}, u32[]{:S(2)}, u32[]{:S(2)}) collective-permute-start(bf16[256,768]{1,0:T(8,128)(2,1)} %param.19), channel_id=1, source_target_pairs={{0,1},{1,0},{2,3},{3,2},{4,5},{5,4},{6,7},{7,6},{8,9},{9,8},{10,11... | collective-permute-start | bytes 1179656 | tf_op jit(solution)/shard_map/ppermute | solution.py:20
  5.7 24.8 %collective-permute-start.1 = (bf16[256,768]{1,0:T(8,128)(2,1)}, bf16[256,768]{1,0:T(8,128)(2,1)}, u32[]{:S(2)}, u32[]{:S(2)}) collective-permute-start(bf16[256,768]{1,0:T(8,128)(2,1)} %param.19), channel_id=1, source_target_pairs={{0,2},{1,3},{2,0},{3,1},{4,6},{5,7},{6,4},{7,5},{8,10},{9,11},{10,... | collective-permute-start | bytes 1179656 | tf_op jit(solution)/shard_map/ppermute | solution.py:20
  9.4 12.6 %collective-permute-start.3 = (bf16[192,576]{1,0:T(8,128)(2,1)}, bf16[192,576]{1,0:T(8,128)(2,1)S(1)}, u32[]{:S(2)}, u32[]{:S(2)}) collective-permute-start(bf16[192,576]{1,0:T(8,128)(2,1)} %pad_maximum_fusion.13), channel_id=1, source_target_pairs={{0,1},{1,0},{2,3},{3,2},{4,5},{5,4},{6,7},{7,6},{8,9},{9,8},{10,11... | collective-permute-start | bytes 663560 | tf_op jit(solution)/shard_map/ppermute | solution.py:20
  32.4 35.7 %collective-permute-start.16 = (bf16[192,768]{1,0:T(8,128)(2,1)}, bf16[192,768]{1,0:T(8,128)(2,1)}, u32[]{:S(2)}, u32[]{:S(2)}) collective-permute-start(bf16[192,768]{1,0:T(8,128)(2,1)} %wp_ref.1), channel_id=1, source_target_pairs={{0,2},{1,3},{2,0},{3,1},{4,6},{5,7},{6,4},{7,5},{8,10},{9,11},{10,... | collective-permute-start | bytes 884744 | tf_op jit(solution)/shard_map/ppermute | solution.py:20
  34.1 34.4 %collective-permute-start.15 = (bf16[192,768]{1,0:T(8,128)(2,1)}, bf16[192,768]{1,0:T(8,128)(2,1)}, u32[]{:S(2)}, u32[]{:S(2)}) collective-permute-start(bf16[192,768]{1,0:T(8,128)(2,1)} %wp_ref.1), channel_id=1, source_target_pairs={{0,1},{1,0},{2,3},{3,2},{4,5},{5,4},{6,7},{7,6},{8,9},{9,8},{10,11... | collective-permute-start | bytes 884744 | tf_op jit(solution)/shard_map/ppermute | solution.py:20
  34.1 52.6 %collective-permute-start.13 = (bf16[256,768]{1,0:T(8,128)(2,1)S(1)}, bf16[256,768]{1,0:T(8,128)(2,1)}, u32[]{:S(2)}, u32[]{:S(2)}) collective-permute-start(bf16[256,768]{1,0:T(8,128)(2,1)S(1)} %multiply_convert_fusion.g0), channel_id=1, source_target_pairs={{0,2},{1,3},{2,0},{3,1},{4,6},{5,7},{6,4},{7,5},{8,10},{9,11},{10,... | collective-permute-start | bytes 1179656 | tf_op jit(solution)/shard_map/ppermute | solution.py:20
  65.5 27.0 %collective-permute-start.10 = (bf16[1024,192]{1,0:T(8,128)(2,1)}, bf16[1024,192]{1,0:T(8,128)(2,1)}, u32[]{:S(2)}, u32[]{:S(2)}) collective-permute-start(bf16[1024,192]{1,0:T(8,128)(2,1)} %get-tuple-element.64.m0), channel_id=1, source_target_pairs={{0,2},{1,3},{2,0},{3,1},{4,6},{5,7},{6,4},{7,5},{8,10},{9,11},{10,... | collective-permute-start | bytes 1179656 | tf_op jit(solution)/shard_map/ppermute | solution.py:20
  68.1 18.0 %collective-permute-start.20 = (bf16[192,768]{1,0:T(8,128)(2,1)S(1)}, bf16[192,768]{1,0:T(8,128)(2,1)S(1)}, u32[]{:S(2)}, u32[]{:S(2)}) collective-permute-start(bf16[192,768]{1,0:T(8,128)(2,1)S(1)} %get-tuple-element.152), channel_id=1, source_target_pairs={{0,3},{1,2},{2,1},{3,0},{4,7},{5,6},{6,5},{7,4},{8,11},{9,10},{10,... | collective-permute-start | bytes 884744 | tf_op jit(solution)/shard_map/ppermute | solution.py:20
  68.5 24.0 %collective-permute-start.19 = (bf16[192,768]{1,0:T(8,128)(2,1)S(1)}, bf16[192,768]{1,0:T(8,128)(2,1)S(1)}, u32[]{:S(2)}, u32[]{:S(2)}) collective-permute-start(bf16[192,768]{1,0:T(8,128)(2,1)S(1)} %get-tuple-element.153), channel_id=1, source_target_pairs={{0,2},{1,3},{2,0},{3,1},{4,6},{5,7},{6,4},{7,5},{8,10},{9,11},{10,... | collective-permute-start | bytes 884744 | tf_op jit(solution)/shard_map/ppermute | solution.py:20
  72.0 22.4 %collective-permute-start.12 = (bf16[256,768]{1,0:T(8,128)(2,1)S(1)}, bf16[256,768]{1,0:T(8,128)(2,1)S(1)}, u32[]{:S(2)}, u32[]{:S(2)}) collective-permute-start(bf16[256,768]{1,0:T(8,128)(2,1)S(1)} %multiply_convert_fusion.g0), channel_id=1, source_target_pairs={{0,1},{1,0},{2,3},{3,2},{4,5},{5,4},{6,7},{7,6},{8,9},{9,8},{10,11... | collective-permute-start | bytes 1179656 | tf_op jit(solution)/shard_map/ppermute | solution.py:20
  118.3 11.2 %collective-permute-start.22 = (bf16[256,768]{1,0:T(8,128)(2,1)S(1)}, bf16[256,768]{1,0:T(8,128)(2,1)S(1)}, u32[]{:S(2)}, u32[]{:S(2)}) collective-permute-start(bf16[256,768]{1,0:T(8,128)(2,1)S(1)} %fusion.21), channel_id=1, source_target_pairs={{0,2},{1,3},{2,0},{3,1},{4,6},{5,7},{6,4},{7,5},{8,10},{9,11},{10,... | collective-permute-start | bytes 1179656 | tf_op jit(solution)/shard_map/ppermute | solution.py:20
  120.2 15.2 %collective-permute-start.45 = (bf16[1,384,768]{2,1,0:T(8,128)(2,1)S(1)}, bf16[1,384,768]{2,1,0:T(8,128)(2,1)S(1)}, u32[]{:S(2)}, u32[]{:S(2)}) collective-permute-start(bf16[1,384,768]{2,1,0:T(8,128)(2,1)S(1)} %select_convert_fusion.1), channel_id=1, source_target_pairs={{0,4},{4,0},{8,12},{12,8},{16,20},{20,16},{24,28},{28,24},{1,5},{5... | collective-permute-start | bytes 1769480 | tf_op jit(solution)/shard_map/ppermute | solution.py:20
  131.2 11.4 %collective-permute-start.24 = (bf16[256,768]{1,0:T(8,128)(2,1)S(1)}, bf16[256,768]{1,0:T(8,128)(2,1)}, u32[]{:S(2)}, u32[]{:S(2)}) collective-permute-start(bf16[256,768]{1,0:T(8,128)(2,1)S(1)} %get-tuple-element.132), channel_id=1, source_target_pairs={{0,2},{1,3},{2,0},{3,1},{4,6},{5,7},{6,4},{7,5},{8,10},{9,11},{10,... | collective-permute-start | bytes 1179656 | tf_op jit(solution)/shard_map/ppermute | solution.py:20
  141.0 48.5 %collective-permute-start.46 = (bf16[4,96,768]{2,1,0:T(8,128)(2,1)}, bf16[4,96,768]{2,1,0:T(8,128)(2,1)}, u32[]{:S(2)}, u32[]{:S(2)}) collective-permute-start(bf16[4,96,768]{2,1,0:T(8,128)(2,1)} %select_convert_fusion), channel_id=1, source_target_pairs={{0,4},{4,0},{8,12},{12,8},{16,20},{20,16},{24,28},{28,24},{1,5},{5... | collective-permute-start | bytes 1769480 | tf_op jit(solution)/shard_map/ppermute | solution.py:20
  144.8 44.3 %collective-permute-start.56 = (bf16[1,96,768]{2,1,0:T(8,128)(2,1)S(1)}, bf16[1,96,768]{2,1,0:T(8,128)(2,1)S(1)}, u32[]{:S(2)}, u32[]{:S(2)}) collective-permute-start(bf16[1,96,768]{2,1,0:T(8,128)(2,1)S(1)} %select_convert_fusion.7), channel_id=1, source_target_pairs={{0,16},{4,20},{8,24},{12,28},{16,0},{20,4},{24,8},{28,12},{1,17},{... | collective-permute-start | bytes 442376 | tf_op jit(solution)/shard_map/ppermute | solution.py:20
  186.6 14.9 %collective-permute-start.39 = (bf16[1,96,768]{2,1,0:T(8,128)(2,1)S(1)}, bf16[1,96,768]{2,1,0:T(8,128)(2,1)S(1)}, u32[]{:S(2)}, u32[]{:S(2)}) collective-permute-start(bf16[1,96,768]{2,1,0:T(8,128)(2,1)S(1)} %select_convert_fusion.9), channel_id=1, source_target_pairs={{0,4},{4,0},{8,12},{12,8},{16,20},{20,16},{24,28},{28,24},{1,5},{5... | collective-permute-start | bytes 442376 | tf_op jit(solution)/shard_map/ppermute | solution.py:20
  188.5 14.0 %collective-permute-start.30 = (bf16[4,100,576]{2,0,1:T(4,128)(2,1)S(1)}, bf16[4,100,576]{2,0,1:T(4,128)(2,1)S(1)}, u32[]{:S(2)}, u32[]{:S(2)}) collective-permute-start(bf16[4,100,576]{2,0,1:T(4,128)(2,1)S(1)} %copy.39), channel_id=1, source_target_pairs={{0,4},{4,0},{8,12},{12,8},{16,20},{20,16},{24,28},{28,24},{1,5},{5... | collective-permute-start | bytes 1382408 | tf_op jit(solution)/shard_map/ppermute | solution.py:20
  189.1 13.7 %collective-permute-start.57 = (bf16[1,96,768]{2,1,0:T(8,128)(2,1)S(1)}, bf16[1,96,768]{2,1,0:T(8,128)(2,1)S(1)}, u32[]{:S(2)}, u32[]{:S(2)}) collective-permute-start(bf16[1,96,768]{2,1,0:T(8,128)(2,1)S(1)} %add_convert_fusion.2), channel_id=1, source_target_pairs={{0,16},{4,20},{8,24},{12,28},{16,0},{20,4},{24,8},{28,12},{1,17},{... | collective-permute-start | bytes 442376 | tf_op jit(solution)/shard_map/ppermute | solution.py:20
  192.9 44.3 %collective-permute-start.28 = (bf16[512,768]{1,0:T(8,128)(2,1)S(1)}, bf16[512,768]{1,0:T(8,128)(2,1)S(1)}, u32[]{:S(2)}, u32[]{:S(2)}) collective-permute-start(bf16[512,768]{1,0:T(8,128)(2,1)S(1)} %pad_maximum_fusion.7), channel_id=1, source_target_pairs={{0,1},{1,0},{2,3},{3,2},{4,5},{5,4},{6,7},{7,6},{8,9},{9,8},{10,11... | collective-permute-start | bytes 2359304 | tf_op jit(solution)/shard_map/ppermute | solution.py:20
  201.3 46.1 %collective-permute-start.26 = (bf16[512,768]{1,0:T(8,128)(2,1)S(1)}, bf16[512,768]{1,0:T(8,128)(2,1)S(1)}, u32[]{:S(2)}, u32[]{:S(2)}) collective-permute-start(bf16[512,768]{1,0:T(8,128)(2,1)S(1)} %pad_maximum_fusion.6), channel_id=1, source_target_pairs={{0,1},{1,0},{2,3},{3,2},{4,5},{5,4},{6,7},{7,6},{8,9},{9,8},{10,11... | collective-permute-start | bytes 2359304 | tf_op jit(solution)/shard_map/ppermute | solution.py:20
  215.9 13.1 %collective-permute-start.31 = (bf16[4,50,576]{2,1,0:T(8,128)(2,1)S(1)}, bf16[4,50,576]{2,1,0:T(8,128)(2,1)S(1)}, u32[]{:S(2)}, u32[]{:S(2)}) collective-permute-start(bf16[4,50,576]{2,1,0:T(8,128)(2,1)S(1)} %select_convert_fusion.5), channel_id=1, source_target_pairs={{0,8},{4,12},{8,0},{12,4},{16,24},{20,28},{24,16},{28,20},{1,9},{5... | collective-permute-start | bytes 691208 | tf_op jit(solution)/shard_map/ppermute | solution.py:20
  216.8 20.3 %collective-permute-start.58 = (bf16[2,96,768]{2,1,0:T(8,128)(2,1)S(1)}, bf16[2,96,768]{2,1,0:T(8,128)(2,1)S(1)}, u32[]{:S(2)}, u32[]{:S(2)}) collective-permute-start(bf16[2,96,768]{2,1,0:T(8,128)(2,1)S(1)} %maximum_select_fusion.9), channel_id=1, source_target_pairs={{0,8},{4,12},{8,0},{12,4},{16,24},{20,28},{24,16},{28,20},{1,9},{5... | collective-permute-start | bytes 884744 | tf_op jit(solution)/shard_map/ppermute | solution.py:20
  219.7 13.2 %collective-permute-start.52 = (bf16[1,24,3072]{2,1,0:T(8,128)(2,1)S(1)}, bf16[1,24,3072]{2,1,0:T(8,128)(2,1)S(1)}, u32[]{:S(2)}, u32[]{:S(2)}) collective-permute-start(bf16[1,24,3072]{2,1,0:T(8,128)(2,1)S(1)} %maximum_bitcast_fusion), channel_id=1, source_target_pairs={{0,16},{4,20},{8,24},{12,28},{16,0},{20,4},{24,8},{28,12},{1,17},{... | collective-permute-start | bytes 442376 | tf_op jit(solution)/shard_map/ppermute | solution.py:20
  244.0 12.4 %collective-permute-start.42 = (bf16[1,24,768]{2,1,0:T(8,128)(2,1)S(1)}, bf16[1,24,768]{2,1,0:T(8,128)(2,1)S(1)}, u32[]{:S(2)}, u32[]{:S(2)}) collective-permute-start(bf16[1,24,768]{2,1,0:T(8,128)(2,1)S(1)} %add_convert_fusion.4), channel_id=1, source_target_pairs={{0,16},{4,20},{8,24},{12,28},{16,0},{20,4},{24,8},{28,12},{1,17},{... | collective-permute-start | bytes 110600 | tf_op jit(solution)/shard_map/ppermute | solution.py:20
  247.4 18.1 %collective-permute-start.53 = (bf16[2,24,3072]{2,1,0:T(8,128)(2,1)}, bf16[2,24,3072]{2,1,0:T(8,128)(2,1)}, u32[]{:S(2)}, u32[]{:S(2)}) collective-permute-start(bf16[2,24,3072]{2,1,0:T(8,128)(2,1)} %maximum_select_fusion.8), channel_id=1, source_target_pairs={{0,8},{4,12},{8,0},{12,4},{16,24},{20,28},{24,16},{28,20},{1,9},{5... | collective-permute-start | bytes 884744 | tf_op jit(solution)/shard_map/ppermute | solution.py:20
  251.1 47.3 %collective-permute-start.59 = (bf16[4,96,768]{2,1,0:T(8,128)(2,1)S(1)}, bf16[4,96,768]{2,1,0:T(8,128)(2,1)}, u32[]{:S(2)}, u32[]{:S(2)}) collective-permute-start(bf16[4,96,768]{2,1,0:T(8,128)(2,1)S(1)} %maximum_select_fusion.5), channel_id=1, source_target_pairs={{0,4},{4,0},{8,12},{12,8},{16,20},{20,16},{24,28},{28,24},{1,5},{5... | collective-permute-start | bytes 1769480 | tf_op jit(solution)/shard_map/ppermute | solution.py:20
  251.9 16.0 %collective-permute-start.29 = (bf16[256,768]{1,0:T(8,128)(2,1)}, bf16[256,768]{1,0:T(8,128)(2,1)}, u32[]{:S(2)}, u32[]{:S(2)}) collective-permute-start(bf16[256,768]{1,0:T(8,128)(2,1)} %fusion.13), channel_id=1, source_target_pairs={{0,2},{1,3},{2,0},{3,1},{4,6},{5,7},{6,4},{7,5},{8,10},{9,11},{10,... | collective-permute-start | bytes 1179656 | tf_op jit(solution)/shard_map/ppermute | solution.py:20
  264.9 18.9 %collective-permute-start.44 = (bf16[4,24,768]{2,1,0:T(8,128)(2,1)S(1)}, bf16[4,24,768]{2,1,0:T(8,128)(2,1)S(1)}, u32[]{:S(2)}, u32[]{:S(2)}) collective-permute-start(bf16[4,24,768]{2,1,0:T(8,128)(2,1)S(1)} %maximum_select_fusion.10), channel_id=1, source_target_pairs={{0,4},{4,0},{8,12},{12,8},{16,20},{20,16},{24,28},{28,24},{1,5},{5... | collective-permute-start | bytes 442376 | tf_op jit(solution)/shard_map/ppermute | solution.py:20
  265.6 18.1 %collective-permute-start.37 = (bf16[2,25,2304]{2,1,0:T(8,128)(2,1)S(1)}, bf16[2,25,2304]{2,1,0:T(8,128)(2,1)S(1)}, u32[]{:S(2)}, u32[]{:S(2)}) collective-permute-start(bf16[2,25,2304]{2,1,0:T(8,128)(2,1)S(1)} %maximum_select_fusion.6), channel_id=1, source_target_pairs={{0,8},{4,12},{8,0},{12,4},{16,24},{20,28},{24,16},{28,20},{1,9},{5... | collective-permute-start | bytes 691208 | tf_op jit(solution)/shard_map/ppermute | solution.py:20
  267.9 33.8 %collective-permute-start.54 = (bf16[4,24,3072]{2,1,0:T(8,128)(2,1)S(1)}, bf16[4,24,3072]{2,1,0:T(8,128)(2,1)S(1)}, u32[]{:S(2)}, u32[]{:S(2)}) collective-permute-start(bf16[4,24,3072]{2,1,0:T(8,128)(2,1)S(1)} %maximum_select_fusion.4), channel_id=1, source_target_pairs={{0,4},{4,0},{8,12},{12,8},{16,20},{20,16},{24,28},{28,24},{1,5},{5... | collective-permute-start | bytes 1769480 | tf_op jit(solution)/shard_map/ppermute | solution.py:20
  (75 other events, 564.4 us)

commit v5 on v4

--- a/solution.py
+++ b/solution.py
@@ -437,13 +437,14 @@
     def spread(pieces):
         return [pieces[0], near(pieces[1]), far(pieces[2]), swap(pieces[3], "fsdp", fs_size, 3)]
 
-    def collect(low, mark=None):
+    def collect(low, mark=None, hold=None):
         low = [low[r * count : (r + 1) * count] for r in range(4)]
         other = near(jnp.concatenate([low[1], low[3]], axis=0)).astype(F32)
         first = low[0].astype(F32) + other[:count]
         sent = (low[2].astype(F32) + other[count:]).astype(BF16)
         sent = sent if mark is None else after(sent, mark)
         other = far(sent)
+        other = other if hold is None else after(other, hold)
         return first + other.astype(F32), sent
 
     def at(r):
@@ -577,7 +578,7 @@
         tokens_all, w_qkv, vectors_one, head_vectors, early_rows,
     )
     share_last, seen, lead = halve(total_last, tail=dp_size)
-    grad_normed_one, _ = collect(after(grad_one_part, lead))
+    grad_normed_one, _ = collect(after(grad_one_part, lead), hold=seen[2])
     unit_one, scale_one = norm_parts(inputs)
     tokens_grad = grad_hidden + norm_back(
         grad_normed_one * gain_one, unit_one, scale_one
@@ -589,7 +590,7 @@
     last, seen_back = unite(arrange(share_rows, rank, pieces_last))
     seen = [*seen, pieces_last[3], *seen_back]
 
-    branch_mlp = collect(after(mlp_part, lead))[0] + b_down
+    branch_mlp = collect(after(mlp_part, lead), hold=seen[2])[0] + b_down
     result = hidden_one + branch_mlp
     rms_sums = jnp.stack(
         [
@@ -604,18 +605,18 @@
     hops = [("fsdp", fs_size, 1), ("fsdp", fs_size, 2)] + [("dp", dp_size, bit) for bit in rounds]
     for order, (axis, size, bit) in enumerate(hops):
         other = swap(rms_sums, axis, size, bit)
-        rms_sums = rms_sums + after(other, seen[min(order + 1, len(seen) - 2)])
+        rms_sums = rms_sums + (after(other, seen[-2]) if order == 1 else other)
     sums = rms_sums[:, 0]
 
     early = [grad_branch_own, grad_branch_own] + [grad_branch_low] * (count_rounds - 2)
     share_down, seen_down, _ = halve(total_down[None], early)
-    grad_down, _ = unite(share_down[0], [seen[0], seen[0], seen[1]])
+    grad_down, _ = unite(share_down[0], [seen[0], seen[1]])
     grad_down = grad_down.astype(F32).reshape(hidden_own, width)
     total_up = after(total_up, seen_down[0])
-    late = [grad_branch_own, lead] + [seen[0]] * (count_rounds - 2)
+    late = [lead, seen[0]] + [seen[1]] * (count_rounds - 2)
     share_up, _, _ = halve(total_up.reshape(fs_size, rows_own, hidden_own), late)
     pieces_up = to_rows(share_up)
-    grad_up, _ = unite(ordered(pieces_up, 1), [seen[1], seen[2], seen[count_rounds]])
+    grad_up, _ = unite(ordered(pieces_up, 1), [seen[count_rounds], seen[count_rounds + 1]])
     grad_up = grad_up.astype(F32).reshape(rows_own, hidden)
     share_proj, _, _ = halve(total_proj[None], seen[:count_rounds])
     grad_proj, _ = unite(share_proj[0], seen[count_rounds:])

time: 310 us -> 308 us (level)
  starting transfers between devices: 61.8 us -> 58.1 us
    ppermute x65, starting transfers between devices: 61.8 us -> 58.1 us  [swap(): return lax.ppermute(value, axis, [(i, i ^ bit) for i in range(size)])]
    select_n x11, other arithmetic: 4.17 us -> 7.71 us  [unite(): jnp.where(upper, jnp.concatenate([other, share], axis=0), jnp.concatenate...]
  transfers between devices with their start and end apart: 65 -> 65, of which waited for: 25 -> 25; matrix products, arithmetic and copies ran while one was open for 20% -> 21% of each run, Pallas kernels for 20% -> 20%
where the time goes in v5:
time: 308 us; the launch traced here: 307 us
  waiting for transfers between devices  91.2 us (30%)
  Pallas kernels  81.6 us (26%)
  starting transfers between devices  58.1 us (19%)
  other arithmetic  46.6 us (15%)
  local copies, waits for them, and re-layouts  26.1 us (8%)
    ppermute x65, waiting for transfers between devices, swap(): return lax.ppermute(value, axis, [(i, i ^ bit) for i in range(size)])  91.2 us
    ppermute x65, starting transfers between devices, swap(): return lax.ppermute(value, axis, [(i, i ^ bit) for i in range(size)])  58.1 us
    pallas_call x1, Pallas kernels, back(): pl.pallas_call(functools.partial(back_body, count), in_specs=[pl.BlockSpe...  32.5 us
    pallas_call x1, Pallas kernels, front(): pl.pallas_call(functools.partial(front_body, count), out_shape=[jax.Shape...  27.8 us
    pallas_call x1, Pallas kernels, middle(): pl.pallas_call(middle_body, grid=(steps,), in_specs=[shifted(r) for r in...  18.2 us
    select_n x11, other arithmetic, unite(): jnp.where(upper, jnp.concatenate([other, share], axis=0), jnp.concatenate...  7.71 us
  transfers between devices with their start and end apart: 65, of which 25 were waited for; matrix products, arithmetic and copies ran while one was open for 21% of the time, Pallas kernels for 20%

profile of v5, /device:TPU:0, one launch (start us, length us, event | category | flops | bytes accessed | tf_op | source)
XLA Modules:
  0.0 306.8 jit_solution(5958725895101147268)
XLA Ops:
  2.2 3.0 collective-permute-start.7
  5.7 2.8 constant_dynamic-slice_fusion.14
  17.3 2.0 collective-permute-start.4
  22.0 4.4 %collective-permute-done.4 = bf16[192,576]{1,0:T(8,128)(2,1)S(1)} collective-permute-done((bf16[192,576]{1,0:T(8,128)(2,1)}, bf16[192,576]{1,0:T(8,128)(2,1)S(1)}, u32[]{:S(2)}, u32[]{:S(2)}) %collective-permute-start.4) | collective-permute-done | bytes 221216 | tf_op jit(solution)/shard_map/ppermute | solution.py:20
  26.3 4.0 %collective-permute-done.5 = bf16[192,576]{1,0:T(8,128)(2,1)S(1)} collective-permute-done((bf16[192,576]{1,0:T(8,128)(2,1)}, bf16[192,576]{1,0:T(8,128)(2,1)S(1)}, u32[]{:S(2)}, u32[]{:S(2)}) %collective-permute-start.5) | collective-permute-done | bytes 221216 | tf_op jit(solution)/shard_map/ppermute | solution.py:20
  37.7 27.8 %front.1 = (bf16[1024,192]{1,0:T(8,128)(2,1)}, bf16[3,1024,1024]{2,1,0:T(8,128)(2,1)}, f32[6,1024,64]{2,1,0:T(8,128)}, bf16[3,1024,64]{2,1,0:T(8,128)(2,1)}, bf1...) custom-call(bf16[1024,768]{1,0:T(8,128)(2,1)} %copy-done.8, bf16[768,576]{1,0:T(8,128)(2,1)} %pad_maximum_fusion.4.w_ref, ...), custom_call_target="tpu_custom_call" | custom-call | flops 1711276032 | bytes 11894784 | tf_op jit(solution)/shard_map/front/pallas_call | solution.py:100
  72.0 14.1 %collective-permute-done.20 = bf16[192,768]{1,0:T(8,128)(2,1)S(1)} collective-permute-done((bf16[192,768]{1,0:T(8,128)(2,1)S(1)}, bf16[192,768]{1,0:T(8,128)(2,1)S(1)}, u32[]{:S(2)}, u32[]{:S(2)}) %collective-permute-start.20) | collective-permute-done | bytes 294944 | tf_op jit(solution)/shard_map/ppermute | solution.py:20
  86.7 5.8 %collective-permute-done.19 = bf16[192,768]{1,0:T(8,128)(2,1)S(1)} collective-permute-done((bf16[192,768]{1,0:T(8,128)(2,1)S(1)}, bf16[192,768]{1,0:T(8,128)(2,1)S(1)}, u32[]{:S(2)}, u32[]{:S(2)}) %collective-permute-start.19) | collective-permute-done | bytes 294944 | tf_op jit(solution)/shard_map/ppermute | solution.py:20
  96.2 18.2 %middle.1 = (f32[256,768]{1,0:T(8,128)}, bf16[1024,768]{1,0:T(8,128)(2,1)}, bf16[1024,768]{1,0:T(8,128)(2,1)}, f32[768,768]{1,0:T(8,128)}, f32[768,768]{1,0:T(8,128)}, /*index=5*/f32[8,768]{1,0:T(8,128)}) custom-call(bf16[1024,192]{1,0:T(8,128)(2,1)} %get-tuple-element.60.m0, bf16[1024,192]{1,0:T(8,128)(2,1)} %copy-done.38, ...), custom_call_target="tpu_custom_call" | custom-call | flops 8455716864 | bytes 16121856 | tf_op jit(solution)/shard_map/middle/pallas_call | solution.py:365
  122.7 6.8 %collective-permute-done.22 = bf16[256,768]{1,0:T(8,128)(2,1)S(1)} collective-permute-done((bf16[256,768]{1,0:T(8,128)(2,1)S(1)}, bf16[256,768]{1,0:T(8,128)(2,1)S(1)}, u32[]{:S(2)}, u32[]{:S(2)}) %collective-permute-start.22) | collective-permute-done | bytes 393248 | tf_op jit(solution)/shard_map/ppermute | solution.py:20
  132.9 2.4 collective-permute-done.45
  138.5 2.5 select_convert_fusion
  144.8 2.7 collective-permute-start.56
  149.1 2.4 pad_maximum_fusion.z_ref
  151.5 32.5 %back.1 = (f32[4,200,576]{2,1,0:T(8,128)}, bf16[1024,768]{1,0:T(8,128)(2,1)}) custom-call(s32[1]{0:T(128)} %bitcast.7.rank_ref, bf16[1024,768]{1,0:T(8,128)(2,1)} %pad_maximum_fusion.z_ref, bf16[192,768]{1,0:T(8,128)(2,1)} %wp_ref.1, bf16[3,1024,1024]{2,1,0:T(8,128)(2,1)} %get-tuple-element.68.p_ref, f32[6,1024,64]{2,1,0:T(8,128)} %get-tuple-element.69.raw_ref, ...), custom_call_target="tpu_custom_call" | custom-call | flops 3724541952 | bytes 18382848 | tf_op jit(solution)/shard_map/back/pallas_call | solution.py:218
  193.7 8.7 %collective-permute-done.28 = bf16[4,100,576]{2,0,1:T(4,128)(2,1)S(1)} collective-permute-done((bf16[4,100,576]{2,0,1:T(4,128)(2,1)S(1)}, bf16[4,100,576]{2,0,1:T(4,128)(2,1)S(1)}, u32[]{:S(2)}, u32[]{:S(2)}) %collective-permute-start.28) | collective-permute-done | bytes 460832 | tf_op jit(solution)/shard_map/ppermute | solution.py:20
  206.0 3.5 %collective-permute-done.40 = bf16[1,48,768]{2,1,0:T(8,128)(2,1)S(1)} collective-permute-done((bf16[1,48,768]{2,1,0:T(8,128)(2,1)S(1)}, bf16[1,48,768]{2,1,0:T(8,128)(2,1)S(1)}, u32[]{:S(2)}, u32[]{:S(2)}) %collective-permute-start.40) | collective-permute-done | bytes 73760 | tf_op jit(solution)/shard_map/ppermute | solution.py:20
  209.5 5.0 %collective-permute-done.29 = bf16[4,50,576]{2,1,0:T(8,128)(2,1)S(1)} collective-permute-done((bf16[4,50,576]{2,1,0:T(8,128)(2,1)S(1)}, bf16[4,50,576]{2,1,0:T(8,128)(2,1)S(1)}, u32[]{:S(2)}, u32[]{:S(2)}) %collective-permute-start.29) | collective-permute-done | bytes 230432 | tf_op jit(solution)/shard_map/ppermute | solution.py:20
  222.6 9.3 %collective-permute-done.58 = bf16[2,96,768]{2,1,0:T(8,128)(2,1)S(1)} collective-permute-done((bf16[2,96,768]{2,1,0:T(8,128)(2,1)S(1)}, bf16[2,96,768]{2,1,0:T(8,128)(2,1)S(1)}, u32[]{:S(2)}, u32[]{:S(2)}) %collective-permute-start.58) | collective-permute-done | bytes 294944 | tf_op jit(solution)/shard_map/ppermute | solution.py:20
  234.1 3.0 collective-permute-start.42
  241.5 1.9 collective-permute-start.32
  245.7 2.8 collective-permute-start.36
  250.5 3.3 %collective-permute-done.43 = bf16[2,24,768]{2,1,0:T(8,128)(2,1)S(1)} collective-permute-done((bf16[2,24,768]{2,1,0:T(8,128)(2,1)S(1)}, bf16[2,24,768]{2,1,0:T(8,128)(2,1)S(1)}, u32[]{:S(2)}, u32[]{:S(2)}) %collective-permute-start.43) | collective-permute-done | bytes 73760 | tf_op jit(solution)/shard_map/ppermute | solution.py:20
  257.8 3.6 %collective-permute-done.53 = bf16[2,24,3072]{2,1,0:T(8,128)(2,1)S(1)} collective-permute-done((bf16[2,24,3072]{2,1,0:T(8,128)(2,1)S(1)}, bf16[2,24,3072]{2,1,0:T(8,128)(2,1)S(1)}, u32[]{:S(2)}, u32[]{:S(2)}) %collective-permute-start.53) | collective-permute-done | bytes 294944 | tf_op jit(solution)/shard_map/ppermute | solution.py:20
  263.3 2.2 collective-permute-start.54
  267.1 2.3 fusion.10
  269.4 2.7 pad_maximum_fusion.20
  275.1 2.7 collective-permute-done.61
  278.2 4.0 %collective-permute-done.62 = f32[4,128]{0,1:T(8,128)S(1)} collective-permute-done((f32[4,128]{0,1:T(8,128)S(1)}, f32[4,128]{0,1:T(8,128)S(1)}, u32[]{:S(2)}, u32[]{:S(2)}) %collective-permute-start.62) | collective-permute-done | bytes 2080 | tf_op jit(solution)/shard_map/ppermute | solution.py:20
  282.6 4.0 %collective-permute-done.63 = f32[4,128]{0,1:T(8,128)S(1)} collective-permute-done((f32[4,128]{0,1:T(8,128)S(1)}, f32[4,128]{0,1:T(8,128)S(1)}, u32[]{:S(2)}, u32[]{:S(2)}) %collective-permute-start.63) | collective-permute-done | bytes 2080 | tf_op jit(solution)/shard_map/ppermute | solution.py:20
  289.2 3.0 collective-permute-done.64
  303.0 2.0 maximum_select_fusion.1
  (343 shorter events, 109.8 us)
Async XLA Ops:
  2.2 12.5 %collective-permute-start.7 = (bf16[16,192]{1,0:T(8,128)(2,1)}, bf16[16,192]{1,0:T(8,128)(2,1)S(1)}, u32[]{:S(2)}, u32[]{:S(2)}) collective-permute-start(bf16[16,192]{1,0:T(8,128)(2,1)} %pack.1), channel_id=1, source_target_pairs={{0,2},{1,3},{2,0},{3,1},{4,6},{5,7},{6,4},{7,5},{8,10},{9,11},{10,... | collective-permute-start | bytes 18440 | tf_op jit(solution)/shard_map/ppermute | solution.py:20
  5.2 12.1 %collective-permute-start.6 = (bf16[16,192]{1,0:T(8,128)(2,1)}, bf16[16,192]{1,0:T(8,128)(2,1)S(1)}, u32[]{:S(2)}, u32[]{:S(2)}) collective-permute-start(bf16[16,192]{1,0:T(8,128)(2,1)} %pack.1), channel_id=1, source_target_pairs={{0,1},{1,0},{2,3},{3,2},{4,5},{5,4},{6,7},{7,6},{8,9},{9,8},{10,11... | collective-permute-start | bytes 18440 | tf_op jit(solution)/shard_map/ppermute | solution.py:20
  5.2 29.2 %collective-permute-start = (bf16[256,768]{1,0:T(8,128)(2,1)}, bf16[256,768]{1,0:T(8,128)(2,1)}, u32[]{:S(2)}, u32[]{:S(2)}) collective-permute-start(bf16[256,768]{1,0:T(8,128)(2,1)} %param.19), channel_id=1, source_target_pairs={{0,1},{1,0},{2,3},{3,2},{4,5},{5,4},{6,7},{7,6},{8,9},{9,8},{10,11... | collective-permute-start | bytes 1179656 | tf_op jit(solution)/shard_map/ppermute | solution.py:20
  5.7 24.8 %collective-permute-start.1 = (bf16[256,768]{1,0:T(8,128)(2,1)}, bf16[256,768]{1,0:T(8,128)(2,1)}, u32[]{:S(2)}, u32[]{:S(2)}) collective-permute-start(bf16[256,768]{1,0:T(8,128)(2,1)} %param.19), channel_id=1, source_target_pairs={{0,2},{1,3},{2,0},{3,1},{4,6},{5,7},{6,4},{7,5},{8,10},{9,11},{10,... | collective-permute-start | bytes 1179656 | tf_op jit(solution)/shard_map/ppermute | solution.py:20
  9.4 12.6 %collective-permute-start.3 = (bf16[192,576]{1,0:T(8,128)(2,1)}, bf16[192,576]{1,0:T(8,128)(2,1)S(1)}, u32[]{:S(2)}, u32[]{:S(2)}) collective-permute-start(bf16[192,576]{1,0:T(8,128)(2,1)} %pad_maximum_fusion.13), channel_id=1, source_target_pairs={{0,1},{1,0},{2,3},{3,2},{4,5},{5,4},{6,7},{7,6},{8,9},{9,8},{10,11... | collective-permute-start | bytes 663560 | tf_op jit(solution)/shard_map/ppermute | solution.py:20
  32.4 35.7 %collective-permute-start.16 = (bf16[192,768]{1,0:T(8,128)(2,1)}, bf16[192,768]{1,0:T(8,128)(2,1)}, u32[]{:S(2)}, u32[]{:S(2)}) collective-permute-start(bf16[192,768]{1,0:T(8,128)(2,1)} %wp_ref.1), channel_id=1, source_target_pairs={{0,2},{1,3},{2,0},{3,1},{4,6},{5,7},{6,4},{7,5},{8,10},{9,11},{10,... | collective-permute-start | bytes 884744 | tf_op jit(solution)/shard_map/ppermute | solution.py:20
  34.1 34.4 %collective-permute-start.15 = (bf16[192,768]{1,0:T(8,128)(2,1)}, bf16[192,768]{1,0:T(8,128)(2,1)}, u32[]{:S(2)}, u32[]{:S(2)}) collective-permute-start(bf16[192,768]{1,0:T(8,128)(2,1)} %wp_ref.1), channel_id=1, source_target_pairs={{0,1},{1,0},{2,3},{3,2},{4,5},{5,4},{6,7},{7,6},{8,9},{9,8},{10,11... | collective-permute-start | bytes 884744 | tf_op jit(solution)/shard_map/ppermute | solution.py:20
  34.1 52.6 %collective-permute-start.13 = (bf16[256,768]{1,0:T(8,128)(2,1)S(1)}, bf16[256,768]{1,0:T(8,128)(2,1)}, u32[]{:S(2)}, u32[]{:S(2)}) collective-permute-start(bf16[256,768]{1,0:T(8,128)(2,1)S(1)} %multiply_convert_fusion.g0), channel_id=1, source_target_pairs={{0,2},{1,3},{2,0},{3,1},{4,6},{5,7},{6,4},{7,5},{8,10},{9,11},{10,... | collective-permute-start | bytes 1179656 | tf_op jit(solution)/shard_map/ppermute | solution.py:20
  65.5 27.0 %collective-permute-start.10 = (bf16[1024,192]{1,0:T(8,128)(2,1)}, bf16[1024,192]{1,0:T(8,128)(2,1)}, u32[]{:S(2)}, u32[]{:S(2)}) collective-permute-start(bf16[1024,192]{1,0:T(8,128)(2,1)} %get-tuple-element.60.m0), channel_id=1, source_target_pairs={{0,2},{1,3},{2,0},{3,1},{4,6},{5,7},{6,4},{7,5},{8,10},{9,11},{10,... | collective-permute-start | bytes 1179656 | tf_op jit(solution)/shard_map/ppermute | solution.py:20
  68.1 18.0 %collective-permute-start.20 = (bf16[192,768]{1,0:T(8,128)(2,1)S(1)}, bf16[192,768]{1,0:T(8,128)(2,1)S(1)}, u32[]{:S(2)}, u32[]{:S(2)}) collective-permute-start(bf16[192,768]{1,0:T(8,128)(2,1)S(1)} %get-tuple-element.144), channel_id=1, source_target_pairs={{0,3},{1,2},{2,1},{3,0},{4,7},{5,6},{6,5},{7,4},{8,11},{9,10},{10,... | collective-permute-start | bytes 884744 | tf_op jit(solution)/shard_map/ppermute | solution.py:20
  68.5 24.0 %collective-permute-start.19 = (bf16[192,768]{1,0:T(8,128)(2,1)S(1)}, bf16[192,768]{1,0:T(8,128)(2,1)S(1)}, u32[]{:S(2)}, u32[]{:S(2)}) collective-permute-start(bf16[192,768]{1,0:T(8,128)(2,1)S(1)} %get-tuple-element.145), channel_id=1, source_target_pairs={{0,2},{1,3},{2,0},{3,1},{4,6},{5,7},{6,4},{7,5},{8,10},{9,11},{10,... | collective-permute-start | bytes 884744 | tf_op jit(solution)/shard_map/ppermute | solution.py:20
  72.0 22.4 %collective-permute-start.12 = (bf16[256,768]{1,0:T(8,128)(2,1)S(1)}, bf16[256,768]{1,0:T(8,128)(2,1)S(1)}, u32[]{:S(2)}, u32[]{:S(2)}) collective-permute-start(bf16[256,768]{1,0:T(8,128)(2,1)S(1)} %multiply_convert_fusion.g0), channel_id=1, source_target_pairs={{0,1},{1,0},{2,3},{3,2},{4,5},{5,4},{6,7},{7,6},{8,9},{9,8},{10,11... | collective-permute-start | bytes 1179656 | tf_op jit(solution)/shard_map/ppermute | solution.py:20
  120.2 15.2 %collective-permute-start.45 = (bf16[1,384,768]{2,1,0:T(8,128)(2,1)S(1)}, bf16[1,384,768]{2,1,0:T(8,128)(2,1)S(1)}, u32[]{:S(2)}, u32[]{:S(2)}) collective-permute-start(bf16[1,384,768]{2,1,0:T(8,128)(2,1)S(1)} %select_convert_fusion.1), channel_id=1, source_target_pairs={{0,4},{4,0},{8,12},{12,8},{16,20},{20,16},{24,28},{28,24},{1,5},{5... | collective-permute-start | bytes 1769480 | tf_op jit(solution)/shard_map/ppermute | solution.py:20
  131.2 11.4 %collective-permute-start.24 = (bf16[256,768]{1,0:T(8,128)(2,1)S(1)}, bf16[256,768]{1,0:T(8,128)(2,1)}, u32[]{:S(2)}, u32[]{:S(2)}) collective-permute-start(bf16[256,768]{1,0:T(8,128)(2,1)S(1)} %get-tuple-element.124), channel_id=1, source_target_pairs={{0,2},{1,3},{2,0},{3,1},{4,6},{5,7},{6,4},{7,5},{8,10},{9,11},{10,... | collective-permute-start | bytes 1179656 | tf_op jit(solution)/shard_map/ppermute | solution.py:20
  141.0 48.5 %collective-permute-start.46 = (bf16[4,96,768]{2,1,0:T(8,128)(2,1)}, bf16[4,96,768]{2,1,0:T(8,128)(2,1)}, u32[]{:S(2)}, u32[]{:S(2)}) collective-permute-start(bf16[4,96,768]{2,1,0:T(8,128)(2,1)} %select_convert_fusion), channel_id=1, source_target_pairs={{0,4},{4,0},{8,12},{12,8},{16,20},{20,16},{24,28},{28,24},{1,5},{5... | collective-permute-start | bytes 1769480 | tf_op jit(solution)/shard_map/ppermute | solution.py:20
  144.8 44.3 %collective-permute-start.56 = (bf16[1,96,768]{2,1,0:T(8,128)(2,1)S(1)}, bf16[1,96,768]{2,1,0:T(8,128)(2,1)S(1)}, u32[]{:S(2)}, u32[]{:S(2)}) collective-permute-start(bf16[1,96,768]{2,1,0:T(8,128)(2,1)S(1)} %select_convert_fusion.7), channel_id=1, source_target_pairs={{0,16},{4,20},{8,24},{12,28},{16,0},{20,4},{24,8},{28,12},{1,17},{... | collective-permute-start | bytes 442376 | tf_op jit(solution)/shard_map/ppermute | solution.py:20
  188.5 14.0 %collective-permute-start.28 = (bf16[4,100,576]{2,0,1:T(4,128)(2,1)S(1)}, bf16[4,100,576]{2,0,1:T(4,128)(2,1)S(1)}, u32[]{:S(2)}, u32[]{:S(2)}) collective-permute-start(bf16[4,100,576]{2,0,1:T(4,128)(2,1)S(1)} %copy.39), channel_id=1, source_target_pairs={{0,4},{4,0},{8,12},{12,8},{16,20},{20,16},{24,28},{28,24},{1,5},{5... | collective-permute-start | bytes 1382408 | tf_op jit(solution)/shard_map/ppermute | solution.py:20
  189.1 16.0 %collective-permute-start.57 = (bf16[1,96,768]{2,1,0:T(8,128)(2,1)S(1)}, bf16[1,96,768]{2,1,0:T(8,128)(2,1)S(1)}, u32[]{:S(2)}, u32[]{:S(2)}) collective-permute-start(bf16[1,96,768]{2,1,0:T(8,128)(2,1)S(1)} %add_convert_fusion.2), channel_id=1, source_target_pairs={{0,16},{4,20},{8,24},{12,28},{16,0},{20,4},{24,8},{28,12},{1,17},{... | collective-permute-start | bytes 442376 | tf_op jit(solution)/shard_map/ppermute | solution.py:20
  191.2 12.6 %collective-permute-start.47 = (bf16[4,48,768]{2,1,0:T(8,128)(2,1)S(1)}, bf16[4,48,768]{2,1,0:T(8,128)(2,1)S(1)}, u32[]{:S(2)}, u32[]{:S(2)}) collective-permute-start(bf16[4,48,768]{2,1,0:T(8,128)(2,1)S(1)} %select_convert_fusion.4), channel_id=1, source_target_pairs={{0,8},{4,12},{8,0},{12,4},{16,24},{20,28},{24,16},{28,20},{1,9},{5... | collective-permute-start | bytes 884744 | tf_op jit(solution)/shard_map/ppermute | solution.py:20
  193.0 38.9 %collective-permute-start.31 = (bf16[512,768]{1,0:T(8,128)(2,1)S(1)}, bf16[512,768]{1,0:T(8,128)(2,1)S(1)}, u32[]{:S(2)}, u32[]{:S(2)}) collective-permute-start(bf16[512,768]{1,0:T(8,128)(2,1)S(1)} %pad_maximum_fusion.7), channel_id=1, source_target_pairs={{0,1},{1,0},{2,3},{3,2},{4,5},{5,4},{6,7},{7,6},{8,9},{9,8},{10,11... | collective-permute-start | bytes 2359304 | tf_op jit(solution)/shard_map/ppermute | solution.py:20
  193.4 39.6 %collective-permute-start.26 = (bf16[512,768]{1,0:T(8,128)(2,1)S(1)}, bf16[512,768]{1,0:T(8,128)(2,1)S(1)}, u32[]{:S(2)}, u32[]{:S(2)}) collective-permute-start(bf16[512,768]{1,0:T(8,128)(2,1)S(1)} %pad_maximum_fusion.6), channel_id=1, source_target_pairs={{0,1},{1,0},{2,3},{3,2},{4,5},{5,4},{6,7},{7,6},{8,9},{9,8},{10,11... | collective-permute-start | bytes 2359304 | tf_op jit(solution)/shard_map/ppermute | solution.py:20
  218.5 13.3 %collective-permute-start.58 = (bf16[2,96,768]{2,1,0:T(8,128)(2,1)S(1)}, bf16[2,96,768]{2,1,0:T(8,128)(2,1)S(1)}, u32[]{:S(2)}, u32[]{:S(2)}) collective-permute-start(bf16[2,96,768]{2,1,0:T(8,128)(2,1)S(1)} %maximum_select_fusion.9), channel_id=1, source_target_pairs={{0,8},{4,12},{8,0},{12,4},{16,24},{20,28},{24,16},{28,20},{1,9},{5... | collective-permute-start | bytes 884744 | tf_op jit(solution)/shard_map/ppermute | solution.py:20
  219.6 14.5 %collective-permute-start.41 = (bf16[1,24,768]{2,1,0:T(8,128)(2,1)S(1)}, bf16[1,24,768]{2,1,0:T(8,128)(2,1)S(1)}, u32[]{:S(2)}, u32[]{:S(2)}) collective-permute-start(bf16[1,24,768]{2,1,0:T(8,128)(2,1)S(1)} %select_convert_fusion.11), channel_id=1, source_target_pairs={{0,16},{4,20},{8,24},{12,28},{16,0},{20,4},{24,8},{28,12},{1,17},{... | collective-permute-start | bytes 110600 | tf_op jit(solution)/shard_map/ppermute | solution.py:20
  220.8 12.5 %collective-permute-start.30 = (bf16[4,25,576]{2,1,0:T(8,128)(2,1)S(1)}, bf16[4,25,576]{2,1,0:T(8,128)(2,1)S(1)}, u32[]{:S(2)}, u32[]{:S(2)}) collective-permute-start(bf16[4,25,576]{2,1,0:T(8,128)(2,1)S(1)} %select_convert_fusion.6), channel_id=1, source_target_pairs={{0,16},{4,20},{8,24},{12,28},{16,0},{20,4},{24,8},{28,12},{1,17},{... | collective-permute-start | bytes 345608 | tf_op jit(solution)/shard_map/ppermute | solution.py:20
  231.8 17.6 %collective-permute-start.52 = (bf16[1,24,3072]{2,1,0:T(8,128)(2,1)S(1)}, bf16[1,24,3072]{2,1,0:T(8,128)(2,1)}, u32[]{:S(2)}, u32[]{:S(2)}) collective-permute-start(bf16[1,24,3072]{2,1,0:T(8,128)(2,1)S(1)} %maximum_bitcast_fusion), channel_id=1, source_target_pairs={{0,16},{4,20},{8,24},{12,28},{16,0},{20,4},{24,8},{28,12},{1,17},{... | collective-permute-start | bytes 442376 | tf_op jit(solution)/shard_map/ppermute | solution.py:20
  234.1 11.6 %collective-permute-start.42 = (bf16[1,24,768]{2,1,0:T(8,128)(2,1)S(1)}, bf16[1,24,768]{2,1,0:T(8,128)(2,1)}, u32[]{:S(2)}, u32[]{:S(2)}) collective-permute-start(bf16[1,24,768]{2,1,0:T(8,128)(2,1)S(1)} %add_convert_fusion.4), channel_id=1, source_target_pairs={{0,16},{4,20},{8,24},{12,28},{16,0},{20,4},{24,8},{28,12},{1,17},{... | collective-permute-start | bytes 110600 | tf_op jit(solution)/shard_map/ppermute | solution.py:20
  240.5 53.5 %collective-permute-start.59 = (bf16[4,96,768]{2,1,0:T(8,128)(2,1)S(1)}, bf16[4,96,768]{2,1,0:T(8,128)(2,1)}, u32[]{:S(2)}, u32[]{:S(2)}) collective-permute-start(bf16[4,96,768]{2,1,0:T(8,128)(2,1)S(1)} %maximum_select_fusion.5), channel_id=1, source_target_pairs={{0,4},{4,0},{8,12},{12,8},{16,20},{20,16},{24,28},{28,24},{1,5},{5... | collective-permute-start | bytes 1769480 | tf_op jit(solution)/shard_map/ppermute | solution.py:20
  241.5 21.7 %collective-permute-start.32 = (bf16[256,768]{1,0:T(8,128)(2,1)}, bf16[256,768]{1,0:T(8,128)(2,1)}, u32[]{:S(2)}, u32[]{:S(2)}) collective-permute-start(bf16[256,768]{1,0:T(8,128)(2,1)} %fusion.13), channel_id=1, source_target_pairs={{0,2},{1,3},{2,0},{3,1},{4,6},{5,7},{6,4},{7,5},{8,10},{9,11},{10,... | collective-permute-start | bytes 1179656 | tf_op jit(solution)/shard_map/ppermute | solution.py:20
  243.5 23.6 %collective-permute-start.27 = (bf16[256,768]{1,0:T(8,128)(2,1)}, bf16[256,768]{1,0:T(8,128)(2,1)}, u32[]{:S(2)}, u32[]{:S(2)}) collective-permute-start(bf16[256,768]{1,0:T(8,128)(2,1)} %fusion.16), channel_id=1, source_target_pairs={{0,2},{1,3},{2,0},{3,1},{4,6},{5,7},{6,4},{7,5},{8,10},{9,11},{10,... | collective-permute-start | bytes 1179656 | tf_op jit(solution)/shard_map/ppermute | solution.py:20
  255.2 22.9 %collective-permute-start.44 = (bf16[4,24,768]{2,1,0:T(8,128)(2,1)S(1)}, bf16[4,24,768]{2,1,0:T(8,128)(2,1)S(1)}, u32[]{:S(2)}, u32[]{:S(2)}) collective-permute-start(bf16[4,24,768]{2,1,0:T(8,128)(2,1)S(1)} %maximum_select_fusion.10), channel_id=1, source_target_pairs={{0,4},{4,0},{8,12},{12,8},{16,20},{20,16},{24,28},{28,24},{1,5},{5... | collective-permute-start | bytes 442376 | tf_op jit(solution)/shard_map/ppermute | solution.py:20
  261.4 13.7 %collective-permute-start.37 = (bf16[2,25,2304]{2,1,0:T(8,128)(2,1)S(1)}, bf16[2,25,2304]{2,1,0:T(8,128)(2,1)S(1)}, u32[]{:S(2)}, u32[]{:S(2)}) collective-permute-start(bf16[2,25,2304]{2,1,0:T(8,128)(2,1)S(1)} %maximum_select_fusion.6), channel_id=1, source_target_pairs={{0,8},{4,12},{8,0},{12,4},{16,24},{20,28},{24,16},{28,20},{1,9},{5... | collective-permute-start | bytes 691208 | tf_op jit(solution)/shard_map/ppermute | solution.py:20
  263.3 39.8 %collective-permute-start.54 = (bf16[4,24,3072]{2,1,0:T(8,128)(2,1)}, bf16[4,24,3072]{2,1,0:T(8,128)(2,1)}, u32[]{:S(2)}, u32[]{:S(2)}) collective-permute-start(bf16[4,24,3072]{2,1,0:T(8,128)(2,1)} %maximum_select_fusion.4), channel_id=1, source_target_pairs={{0,4},{4,0},{8,12},{12,8},{16,20},{20,16},{24,28},{28,24},{1,5},{5... | collective-permute-start | bytes 1769480 | tf_op jit(solution)/shard_map/ppermute | solution.py:20
  (75 other events, 591.1 us)

commit v6 on v2

--- a/solution.py
+++ b/solution.py
@@ -443,7 +443,8 @@
         first = low[0].astype(F32) + other[:count]
         sent = (low[2].astype(F32) + other[count:]).astype(BF16)
         sent = sent if mark is None else after(sent, mark)
-        return first + far(sent).astype(F32), sent
+        other = far(sent)
+        return first + other.astype(F32), sent
 
     def at(r):
         return rank ^ r
@@ -527,7 +528,8 @@
             upper = (place & bit) != 0
             sent = jnp.where(upper, low, high).astype(BF16)
             lead = sent if order == 0 else lead
-            other = held_back(swap(sent, "dp", dp_size, bit), marks, order)
+            other = swap(sent, "dp", dp_size, bit)
+            other = held_back(other, marks, order)
             seen.append(other)
             total = jnp.where(upper, high, low).astype(F32) + other.astype(F32)
             first, second = total[:, :size], total[:, size:]
@@ -537,7 +539,8 @@
         share = share.astype(BF16)[None]
         seen = []
         for order, bit in enumerate(reversed(rounds)):
-            other = held_back(swap(share, "dp", dp_size, bit), marks, order)
+            other = swap(share, "dp", dp_size, bit)
+            other = held_back(other, marks, order)
             seen.append(other)
             upper = (place & bit) != 0
             share = jnp.where(
@@ -552,13 +555,16 @@
         return spread([lax.dynamic_index_in_dim(share, at(r), 0, False) for r in range(4)])
 
     grad_normed_two, mark_two = collect(grad_two_part)
-    grad_out = grad_mlp_own.astype(F32)
+    total_down = after(total_down, mark_two)
+    sums_middle = after(sums_middle, mark_two)
+    mlp_part = after(mlp_part, mark_two)
+    grad_out = after(grad_mlp_own, mark_two).astype(F32)
     unit_two, scale_two = norm_parts(hidden_one)
     grad_hidden = grad_out + norm_back(grad_normed_two * gain_two, unit_two, scale_two)
     grad_branch_own = grad_hidden.astype(BF16)
     grad_branch_low = jnp.concatenate(gather(grad_branch_own), axis=0)
     total_proj = left_cross(mixed_own, grad_branch_low)
-    branch_mlp = collect(mlp_part, grad_normed_two)[0] + b_down
+    branch_mlp = collect(mlp_part, grad_branch_own)[0] + b_down
     result = hidden_one + branch_mlp
     rms_sums = jnp.stack(
         [
@@ -597,7 +603,7 @@
     last, seen_back = unite(arrange(share_rows, rank, pieces_last))
     seen = [*seen, pieces_last[3], *seen_back]
 
-    early = [mark_two, grad_branch_own] + [grad_branch_low] * (count_rounds - 2)
+    early = [grad_branch_own, grad_branch_own] + [grad_branch_low] * (count_rounds - 2)
     share_down, seen_down, _ = halve(total_down[None], early)
     grad_down, _ = unite(share_down[0], [lead, seen[0], seen[1]])
     grad_down = grad_down.astype(F32).reshape(hidden_own, width)

time: 307 us -> 313 us (1.020)
  starting transfers between devices: 48.6 us -> 54.1 us
  waiting for transfers between devices: 94.1 us -> 89 us
  local copies, waits for them, and re-layouts: 30.7 us -> 34.6 us
    ppermute x60, starting transfers between devices: 48.6 us -> 54.1 us  [swap(): return lax.ppermute(value, axis, [(i, i ^ bit) for i in range(size)])]
    ppermute x60, waiting for transfers between devices: 94.1 us -> 89 us  [swap(): return lax.ppermute(value, axis, [(i, i ^ bit) for i in range(size)])]
    unnamed x82 -> x94, local copies, waits for them, and re-layouts: 7.78 us -> 7.96 us
  transfers between devices with their start and end apart: 60 -> 60, of which waited for: 24 -> 20; matrix products, arithmetic and copies ran while one was open for 21% -> 22% of each run, Pallas kernels for 21% -> 20%
where the time goes in v6:
time: 313 us; the launch traced here: 312 us
  waiting for transfers between devices  89 us (28%)
  Pallas kernels  81.6 us (26%)
  starting transfers between devices  54.1 us (17%)
  other arithmetic  49.6 us (16%)
  local copies, waits for them, and re-layouts  34.6 us (11%)
    ppermute x60, waiting for transfers between devices, swap(): return lax.ppermute(value, axis, [(i, i ^ bit) for i in range(size)])  89 us
    ppermute x60, starting transfers between devices, swap(): return lax.ppermute(value, axis, [(i, i ^ bit) for i in range(size)])  54.1 us
    pallas_call x1, Pallas kernels, back(): pl.pallas_call(functools.partial(back_body, count), in_specs=[pl.BlockSpe...  32.5 us
    pallas_call x1, Pallas kernels, front(): pl.pallas_call(functools.partial(front_body, count), out_shape=[jax.Shape...  27.8 us
    pallas_call x1, Pallas kernels, middle(): pl.pallas_call(middle_body, grid=(steps,), in_specs=[shifted(r) for r in...  18.2 us
    unnamed x94, local copies, waits for them, and re-layouts  7.96 us
  transfers between devices with their start and end apart: 60, of which 20 were waited for; matrix products, arithmetic and copies ran while one was open for 22% of the time, Pallas kernels for 20%

profile of v6, /device:TPU:0, one launch (start us, length us, event | category | flops | bytes accessed | tf_op | source)
XLA Modules:
  0.0 312.2 jit_solution(6715218597142554218)
XLA Ops:
  2.2 3.0 collective-permute-start.7
  5.7 2.8 constant_dynamic-slice_fusion.14
  10.3 1.9 pad_maximum_fusion.15
  17.3 2.0 collective-permute-start.4
  21.9 4.4 %collective-permute-done.4 = bf16[192,576]{1,0:T(8,128)(2,1)S(1)} collective-permute-done((bf16[192,576]{1,0:T(8,128)(2,1)}, bf16[192,576]{1,0:T(8,128)(2,1)S(1)}, u32[]{:S(2)}, u32[]{:S(2)}) %collective-permute-start.4) | collective-permute-done | bytes 221216 | tf_op jit(solution)/shard_map/ppermute | solution.py:20
  26.3 4.0 %collective-permute-done.5 = bf16[192,576]{1,0:T(8,128)(2,1)S(1)} collective-permute-done((bf16[192,576]{1,0:T(8,128)(2,1)}, bf16[192,576]{1,0:T(8,128)(2,1)S(1)}, u32[]{:S(2)}, u32[]{:S(2)}) %collective-permute-start.5) | collective-permute-done | bytes 221216 | tf_op jit(solution)/shard_map/ppermute | solution.py:20
  37.7 27.8 %front.1 = (bf16[1024,192]{1,0:T(8,128)(2,1)}, bf16[3,1024,1024]{2,1,0:T(8,128)(2,1)}, f32[6,1024,64]{2,1,0:T(8,128)}, bf16[3,1024,64]{2,1,0:T(8,128)(2,1)}, bf1...) custom-call(bf16[1024,768]{1,0:T(8,128)(2,1)} %copy-done.6, bf16[768,576]{1,0:T(8,128)(2,1)} %pad_maximum_fusion.4.w_ref, ...), custom_call_target="tpu_custom_call" | custom-call | flops 1711276032 | bytes 11894784 | tf_op jit(solution)/shard_map/front/pallas_call | solution.py:100
  72.7 13.5 %collective-permute-done.20 = bf16[192,768]{1,0:T(8,128)(2,1)S(1)} collective-permute-done((bf16[192,768]{1,0:T(8,128)(2,1)S(1)}, bf16[192,768]{1,0:T(8,128)(2,1)S(1)}, u32[]{:S(2)}, u32[]{:S(2)}) %collective-permute-start.20) | collective-permute-done | bytes 294944 | tf_op jit(solution)/shard_map/ppermute | solution.py:20
  86.8 5.8 %collective-permute-done.19 = bf16[192,768]{1,0:T(8,128)(2,1)S(1)} collective-permute-done((bf16[192,768]{1,0:T(8,128)(2,1)S(1)}, bf16[192,768]{1,0:T(8,128)(2,1)S(1)}, u32[]{:S(2)}, u32[]{:S(2)}) %collective-permute-start.19) | collective-permute-done | bytes 294944 | tf_op jit(solution)/shard_map/ppermute | solution.py:20
  96.3 18.2 %middle.1 = (f32[256,768]{1,0:T(8,128)}, bf16[1024,768]{1,0:T(8,128)(2,1)}, bf16[1024,768]{1,0:T(8,128)(2,1)}, f32[768,768]{1,0:T(8,128)}, f32[768,768]{1,0:T(8,128)}, /*index=5*/f32[8,768]{1,0:T(8,128)}) custom-call(bf16[1024,192]{1,0:T(8,128)(2,1)} %get-tuple-element.60.m0, bf16[1024,192]{1,0:T(8,128)(2,1)} %copy-done.41, ...), custom_call_target="tpu_custom_call" | custom-call | flops 8455716864 | bytes 16121856 | tf_op jit(solution)/shard_map/middle/pallas_call | solution.py:365
  128.5 3.0 collective-permute-done.23
  137.5 3.7 %collective-permute-done.45 = bf16[1,384,768]{2,1,0:T(8,128)(2,1)} collective-permute-done((bf16[1,384,768]{2,1,0:T(8,128)(2,1)S(1)}, bf16[1,384,768]{2,1,0:T(8,128)(2,1)}, u32[]{:S(2)}, u32[]{:S(2)}) %collective-permute-start.45) | collective-permute-done | bytes 589856 | tf_op jit(solution)/shard_map/ppermute | solution.py:20
  141.1 2.1 convert_add_fusion.1
  149.3 2.0 collective-permute-done.55
  151.4 2.7 collective-permute-start.56
  158.9 2.5 pad_maximum_fusion.z_ref
  164.2 2.7 pad_maximum_fusion.20
  171.1 32.5 %back.1 = (f32[4,200,576]{2,1,0:T(8,128)}, bf16[1024,768]{1,0:T(8,128)(2,1)}) custom-call(s32[1]{0:T(128)} %bitcast.7.rank_ref, bf16[1024,768]{1,0:T(8,128)(2,1)} %pad_maximum_fusion.z_ref, bf16[192,768]{1,0:T(8,128)(2,1)} %wp_ref.1, bf16[3,1024,1024]{2,1,0:T(8,128)(2,1)} %get-tuple-element.70.p_ref, f32[6,1024,64]{2,1,0:T(8,128)} %get-tuple-element.71.raw_ref, ...), custom_call_target="tpu_custom_call" | custom-call | flops 3724541952 | bytes 18382848 | tf_op jit(solution)/shard_map/back/pallas_call | solution.py:218
  207.5 2.1 collective-permute-start.47
  212.2 3.3 %collective-permute-done.47 = bf16[4,48,768]{2,1,0:T(8,128)(2,1)S(1)} collective-permute-done((bf16[4,48,768]{2,1,0:T(8,128)(2,1)S(1)}, bf16[4,48,768]{2,1,0:T(8,128)(2,1)S(1)}, u32[]{:S(2)}, u32[]{:S(2)}) %collective-permute-start.47) | collective-permute-done | bytes 294944 | tf_op jit(solution)/shard_map/ppermute | solution.py:20
  220.1 3.3 %collective-permute-done.48 = bf16[4,24,768]{2,1,0:T(8,128)(2,1)S(1)} collective-permute-done((bf16[4,24,768]{2,1,0:T(8,128)(2,1)S(1)}, bf16[4,24,768]{2,1,0:T(8,128)(2,1)S(1)}, u32[]{:S(2)}, u32[]{:S(2)}) %collective-permute-start.48) | collective-permute-done | bytes 147488 | tf_op jit(solution)/shard_map/ppermute | solution.py:20
  223.5 4.9 %collective-permute-done.58 = bf16[2,96,768]{2,1,0:T(8,128)(2,1)S(1)} collective-permute-done((bf16[2,96,768]{2,1,0:T(8,128)(2,1)S(1)}, bf16[2,96,768]{2,1,0:T(8,128)(2,1)S(1)}, u32[]{:S(2)}, u32[]{:S(2)}) %collective-permute-start.58) | collective-permute-done | bytes 294944 | tf_op jit(solution)/shard_map/ppermute | solution.py:20
  228.4 1.9 collective-permute-start.50
  232.8 2.0 collective-permute-start.31
  235.2 11.4 %collective-permute-done.31 = bf16[4,50,576]{2,1,0:T(8,128)(2,1)S(1)} collective-permute-done((bf16[4,50,576]{2,1,0:T(8,128)(2,1)S(1)}, bf16[4,50,576]{2,1,0:T(8,128)(2,1)S(1)}, u32[]{:S(2)}, u32[]{:S(2)}) %collective-permute-start.31) | collective-permute-done | bytes 230432 | tf_op jit(solution)/shard_map/ppermute | solution.py:20
  246.9 3.0 collective-permute-start.32
  250.0 5.6 %collective-permute-done.41 = bf16[1,24,768]{2,1,0:T(8,128)(2,1)S(1)} collective-permute-done((bf16[1,24,768]{2,1,0:T(8,128)(2,1)S(1)}, bf16[1,24,768]{2,1,0:T(8,128)(2,1)S(1)}, u32[]{:S(2)}, u32[]{:S(2)}) %collective-permute-start.41) | collective-permute-done | bytes 36896 | tf_op jit(solution)/shard_map/ppermute | solution.py:20
  255.6 2.6 collective-permute-done.32
  262.5 2.1 collective-permute-start.53
  272.5 3.8 %collective-permute-done.43 = bf16[2,24,768]{2,1,0:T(8,128)(2,1)S(1)} collective-permute-done((bf16[2,24,768]{2,1,0:T(8,128)(2,1)S(1)}, bf16[2,24,768]{2,1,0:T(8,128)(2,1)S(1)}, u32[]{:S(2)}, u32[]{:S(2)}) %collective-permute-start.43) | collective-permute-done | bytes 73760 | tf_op jit(solution)/shard_map/ppermute | solution.py:20
  289.3 8.1 %collective-permute-done.54 = bf16[4,24,3072]{2,1,0:T(8,128)(2,1)S(1)} collective-permute-done((bf16[4,24,3072]{2,1,0:T(8,128)(2,1)S(1)}, bf16[4,24,3072]{2,1,0:T(8,128)(2,1)S(1)}, u32[]{:S(2)}, u32[]{:S(2)}) %collective-permute-start.54) | collective-permute-done | bytes 589856 | tf_op jit(solution)/shard_map/ppermute | solution.py:20
  299.4 6.0 %collective-permute-done.38 = bf16[4,25,2304]{2,0,1:T(4,128)(2,1)S(1)} collective-permute-done((bf16[4,25,2304]{2,0,1:T(4,128)(2,1)S(1)}, bf16[4,25,2304]{2,0,1:T(4,128)(2,1)S(1)}, u32[]{:S(2)}, u32[]{:S(2)}) %collective-permute-start.38) | collective-permute-done | bytes 460832 | tf_op jit(solution)/shard_map/ppermute | solution.py:20
  (334 shorter events, 115.9 us)
Async XLA Ops:
  2.2 12.5 %collective-permute-start.7 = (bf16[16,192]{1,0:T(8,128)(2,1)}, bf16[16,192]{1,0:T(8,128)(2,1)S(1)}, u32[]{:S(2)}, u32[]{:S(2)}) collective-permute-start(bf16[16,192]{1,0:T(8,128)(2,1)} %pack.1), channel_id=1, source_target_pairs={{0,2},{1,3},{2,0},{3,1},{4,6},{5,7},{6,4},{7,5},{8,10},{9,11},{10,... | collective-permute-start | bytes 18440 | tf_op jit(solution)/shard_map/ppermute | solution.py:20
  5.2 12.1 %collective-permute-start.6 = (bf16[16,192]{1,0:T(8,128)(2,1)}, bf16[16,192]{1,0:T(8,128)(2,1)S(1)}, u32[]{:S(2)}, u32[]{:S(2)}) collective-permute-start(bf16[16,192]{1,0:T(8,128)(2,1)} %pack.1), channel_id=1, source_target_pairs={{0,1},{1,0},{2,3},{3,2},{4,5},{5,4},{6,7},{7,6},{8,9},{9,8},{10,11... | collective-permute-start | bytes 18440 | tf_op jit(solution)/shard_map/ppermute | solution.py:20
  5.2 29.2 %collective-permute-start = (bf16[256,768]{1,0:T(8,128)(2,1)}, bf16[256,768]{1,0:T(8,128)(2,1)}, u32[]{:S(2)}, u32[]{:S(2)}) collective-permute-start(bf16[256,768]{1,0:T(8,128)(2,1)} %param.19), channel_id=1, source_target_pairs={{0,1},{1,0},{2,3},{3,2},{4,5},{5,4},{6,7},{7,6},{8,9},{9,8},{10,11... | collective-permute-start | bytes 1179656 | tf_op jit(solution)/shard_map/ppermute | solution.py:20
  5.7 24.8 %collective-permute-start.1 = (bf16[256,768]{1,0:T(8,128)(2,1)}, bf16[256,768]{1,0:T(8,128)(2,1)}, u32[]{:S(2)}, u32[]{:S(2)}) collective-permute-start(bf16[256,768]{1,0:T(8,128)(2,1)} %param.19), channel_id=1, source_target_pairs={{0,2},{1,3},{2,0},{3,1},{4,6},{5,7},{6,4},{7,5},{8,10},{9,11},{10,... | collective-permute-start | bytes 1179656 | tf_op jit(solution)/shard_map/ppermute | solution.py:20
  9.3 12.6 %collective-permute-start.3 = (bf16[192,576]{1,0:T(8,128)(2,1)}, bf16[192,576]{1,0:T(8,128)(2,1)S(1)}, u32[]{:S(2)}, u32[]{:S(2)}) collective-permute-start(bf16[192,576]{1,0:T(8,128)(2,1)} %pad_maximum_fusion.13), channel_id=1, source_target_pairs={{0,1},{1,0},{2,3},{3,2},{4,5},{5,4},{6,7},{7,6},{8,9},{9,8},{10,11... | collective-permute-start | bytes 663560 | tf_op jit(solution)/shard_map/ppermute | solution.py:20
  32.4 35.8 %collective-permute-start.16 = (bf16[192,768]{1,0:T(8,128)(2,1)}, bf16[192,768]{1,0:T(8,128)(2,1)}, u32[]{:S(2)}, u32[]{:S(2)}) collective-permute-start(bf16[192,768]{1,0:T(8,128)(2,1)} %wp_ref.1), channel_id=1, source_target_pairs={{0,2},{1,3},{2,0},{3,1},{4,6},{5,7},{6,4},{7,5},{8,10},{9,11},{10,... | collective-permute-start | bytes 884744 | tf_op jit(solution)/shard_map/ppermute | solution.py:20
  34.1 34.4 %collective-permute-start.15 = (bf16[192,768]{1,0:T(8,128)(2,1)}, bf16[192,768]{1,0:T(8,128)(2,1)}, u32[]{:S(2)}, u32[]{:S(2)}) collective-permute-start(bf16[192,768]{1,0:T(8,128)(2,1)} %wp_ref.1), channel_id=1, source_target_pairs={{0,1},{1,0},{2,3},{3,2},{4,5},{5,4},{6,7},{7,6},{8,9},{9,8},{10,11... | collective-permute-start | bytes 884744 | tf_op jit(solution)/shard_map/ppermute | solution.py:20
  34.1 52.6 %collective-permute-start.13 = (bf16[256,768]{1,0:T(8,128)(2,1)S(1)}, bf16[256,768]{1,0:T(8,128)(2,1)}, u32[]{:S(2)}, u32[]{:S(2)}) collective-permute-start(bf16[256,768]{1,0:T(8,128)(2,1)S(1)} %multiply_convert_fusion.g0), channel_id=1, source_target_pairs={{0,2},{1,3},{2,0},{3,1},{4,6},{5,7},{6,4},{7,5},{8,10},{9,11},{10,... | collective-permute-start | bytes 1179656 | tf_op jit(solution)/shard_map/ppermute | solution.py:20
  65.5 27.0 %collective-permute-start.10 = (bf16[1024,192]{1,0:T(8,128)(2,1)}, bf16[1024,192]{1,0:T(8,128)(2,1)}, u32[]{:S(2)}, u32[]{:S(2)}) collective-permute-start(bf16[1024,192]{1,0:T(8,128)(2,1)} %get-tuple-element.60.m0), channel_id=1, source_target_pairs={{0,2},{1,3},{2,0},{3,1},{4,6},{5,7},{6,4},{7,5},{8,10},{9,11},{10,... | collective-permute-start | bytes 1179656 | tf_op jit(solution)/shard_map/ppermute | solution.py:20
  68.2 18.0 %collective-permute-start.20 = (bf16[192,768]{1,0:T(8,128)(2,1)S(1)}, bf16[192,768]{1,0:T(8,128)(2,1)S(1)}, u32[]{:S(2)}, u32[]{:S(2)}) collective-permute-start(bf16[192,768]{1,0:T(8,128)(2,1)S(1)} %get-tuple-element.144), channel_id=1, source_target_pairs={{0,3},{1,2},{2,1},{3,0},{4,7},{5,6},{6,5},{7,4},{8,11},{9,10},{10,... | collective-permute-start | bytes 884744 | tf_op jit(solution)/shard_map/ppermute | solution.py:20
  68.5 24.0 %collective-permute-start.19 = (bf16[192,768]{1,0:T(8,128)(2,1)S(1)}, bf16[192,768]{1,0:T(8,128)(2,1)S(1)}, u32[]{:S(2)}, u32[]{:S(2)}) collective-permute-start(bf16[192,768]{1,0:T(8,128)(2,1)S(1)} %get-tuple-element.145), channel_id=1, source_target_pairs={{0,2},{1,3},{2,0},{3,1},{4,6},{5,7},{6,4},{7,5},{8,10},{9,11},{10,... | collective-permute-start | bytes 884744 | tf_op jit(solution)/shard_map/ppermute | solution.py:20
  72.7 21.8 %collective-permute-start.12 = (bf16[256,768]{1,0:T(8,128)(2,1)S(1)}, bf16[256,768]{1,0:T(8,128)(2,1)S(1)}, u32[]{:S(2)}, u32[]{:S(2)}) collective-permute-start(bf16[256,768]{1,0:T(8,128)(2,1)S(1)} %multiply_convert_fusion.g0), channel_id=1, source_target_pairs={{0,1},{1,0},{2,3},{3,2},{4,5},{5,4},{6,7},{7,6},{8,9},{9,8},{10,11... | collective-permute-start | bytes 1179656 | tf_op jit(solution)/shard_map/ppermute | solution.py:20
  120.0 11.5 %collective-permute-start.23 = (bf16[256,768]{1,0:T(8,128)(2,1)}, bf16[256,768]{1,0:T(8,128)(2,1)}, u32[]{:S(2)}, u32[]{:S(2)}) collective-permute-start(bf16[256,768]{1,0:T(8,128)(2,1)} %fusion.21), channel_id=1, source_target_pairs={{0,2},{1,3},{2,0},{3,1},{4,6},{5,7},{6,4},{7,5},{8,10},{9,11},{10,... | collective-permute-start | bytes 1179656 | tf_op jit(solution)/shard_map/ppermute | solution.py:20
  125.9 15.3 %collective-permute-start.45 = (bf16[1,384,768]{2,1,0:T(8,128)(2,1)S(1)}, bf16[1,384,768]{2,1,0:T(8,128)(2,1)}, u32[]{:S(2)}, u32[]{:S(2)}) collective-permute-start(bf16[1,384,768]{2,1,0:T(8,128)(2,1)S(1)} %select_convert_fusion.1), channel_id=1, source_target_pairs={{0,4},{4,0},{8,12},{12,8},{16,20},{20,16},{24,28},{28,24},{1,5},{5... | collective-permute-start | bytes 1769480 | tf_op jit(solution)/shard_map/ppermute | solution.py:20
  128.4 19.0 %collective-permute-start.22 = (bf16[512,768]{1,0:T(8,128)(2,1)}, bf16[512,768]{1,0:T(8,128)(2,1)}, u32[]{:S(2)}, u32[]{:S(2)}) collective-permute-start(bf16[512,768]{1,0:T(8,128)(2,1)} %pad_maximum_fusion.6), channel_id=1, source_target_pairs={{0,1},{1,0},{2,3},{3,2},{4,5},{5,4},{6,7},{7,6},{8,9},{9,8},{10,11... | collective-permute-start | bytes 2359304 | tf_op jit(solution)/shard_map/ppermute | solution.py:20
  134.4 14.9 %collective-permute-start.26 = (bf16[256,768]{1,0:T(8,128)(2,1)}, bf16[256,768]{1,0:T(8,128)(2,1)}, u32[]{:S(2)}, u32[]{:S(2)}) collective-permute-start(bf16[256,768]{1,0:T(8,128)(2,1)} %get-tuple-element.124), channel_id=1, source_target_pairs={{0,2},{1,3},{2,0},{3,1},{4,6},{5,7},{6,4},{7,5},{8,10},{9,11},{10,... | collective-permute-start | bytes 1179656 | tf_op jit(solution)/shard_map/ppermute | solution.py:20
  136.1 18.0 %collective-permute-start.25 = (bf16[256,768]{1,0:T(8,128)(2,1)}, bf16[256,768]{1,0:T(8,128)(2,1)}, u32[]{:S(2)}, u32[]{:S(2)}) collective-permute-start(bf16[256,768]{1,0:T(8,128)(2,1)} %get-tuple-element.124), channel_id=1, source_target_pairs={{0,1},{1,0},{2,3},{3,2},{4,5},{5,4},{6,7},{7,6},{8,9},{9,8},{10,11... | collective-permute-start | bytes 1179656 | tf_op jit(solution)/shard_map/ppermute | solution.py:20
  145.9 60.3 %collective-permute-start.46 = (bf16[4,96,768]{2,1,0:T(8,128)(2,1)}, bf16[4,96,768]{2,1,0:T(8,128)(2,1)}, u32[]{:S(2)}, u32[]{:S(2)}) collective-permute-start(bf16[4,96,768]{2,1,0:T(8,128)(2,1)} %select_convert_fusion), channel_id=1, source_target_pairs={{0,4},{4,0},{8,12},{12,8},{16,20},{20,16},{24,28},{28,24},{1,5},{5... | collective-permute-start | bytes 1769480 | tf_op jit(solution)/shard_map/ppermute | solution.py:20
  148.7 13.7 %collective-permute-start.24 = (bf16[256,768]{1,0:T(8,128)(2,1)S(1)}, bf16[256,768]{1,0:T(8,128)(2,1)S(1)}, u32[]{:S(2)}, u32[]{:S(2)}) collective-permute-start(bf16[256,768]{1,0:T(8,128)(2,1)S(1)} %fusion.18), channel_id=1, source_target_pairs={{0,2},{1,3},{2,0},{3,1},{4,6},{5,7},{6,4},{7,5},{8,10},{9,11},{10,... | collective-permute-start | bytes 1179656 | tf_op jit(solution)/shard_map/ppermute | solution.py:20
  157.4 73.3 %collective-permute-start.39 = (bf16[1,96,768]{2,1,0:T(8,128)(2,1)}, bf16[1,96,768]{2,1,0:T(8,128)(2,1)}, u32[]{:S(2)}, u32[]{:S(2)}) collective-permute-start(bf16[1,96,768]{2,1,0:T(8,128)(2,1)} %select_convert_fusion.9), channel_id=1, source_target_pairs={{0,4},{4,0},{8,12},{12,8},{16,20},{20,16},{24,28},{28,24},{1,5},{5... | collective-permute-start | bytes 442376 | tf_op jit(solution)/shard_map/ppermute | solution.py:20
  162.0 55.2 %collective-permute-start.57 = (bf16[1,96,768]{2,1,0:T(8,128)(2,1)}, bf16[1,96,768]{2,1,0:T(8,128)(2,1)}, u32[]{:S(2)}, u32[]{:S(2)}) collective-permute-start(bf16[1,96,768]{2,1,0:T(8,128)(2,1)} %add_convert_fusion.2), channel_id=1, source_target_pairs={{0,16},{4,20},{8,24},{12,28},{16,0},{20,4},{24,8},{28,12},{1,17},{... | collective-permute-start | bytes 442376 | tf_op jit(solution)/shard_map/ppermute | solution.py:20
  210.0 20.4 %collective-permute-start.30 = (bf16[4,100,576]{2,0,1:T(4,128)(2,1)S(1)}, bf16[4,100,576]{2,0,1:T(4,128)(2,1)S(1)}, u32[]{:S(2)}, u32[]{:S(2)}) collective-permute-start(bf16[4,100,576]{2,0,1:T(4,128)(2,1)S(1)} %copy.39), channel_id=1, source_target_pairs={{0,4},{4,0},{8,12},{12,8},{16,20},{20,16},{24,28},{28,24},{1,5},{5... | collective-permute-start | bytes 1382408 | tf_op jit(solution)/shard_map/ppermute | solution.py:20
  217.2 43.8 %collective-permute-start.28 = (bf16[512,768]{1,0:T(8,128)(2,1)S(1)}, bf16[512,768]{1,0:T(8,128)(2,1)S(1)}, u32[]{:S(2)}, u32[]{:S(2)}) collective-permute-start(bf16[512,768]{1,0:T(8,128)(2,1)S(1)} %pad_maximum_fusion.7), channel_id=1, source_target_pairs={{0,1},{1,0},{2,3},{3,2},{4,5},{5,4},{6,7},{7,6},{8,9},{9,8},{10,11... | collective-permute-start | bytes 2359304 | tf_op jit(solution)/shard_map/ppermute | solution.py:20
  232.6 14.2 %collective-permute-start.40 = (bf16[1,48,768]{2,1,0:T(8,128)(2,1)S(1)}, bf16[1,48,768]{2,1,0:T(8,128)(2,1)S(1)}, u32[]{:S(2)}, u32[]{:S(2)}) collective-permute-start(bf16[1,48,768]{2,1,0:T(8,128)(2,1)S(1)} %select_convert_fusion.10), channel_id=1, source_target_pairs={{0,8},{4,12},{8,0},{12,4},{16,24},{20,28},{24,16},{28,20},{1,9},{5... | collective-permute-start | bytes 221192 | tf_op jit(solution)/shard_map/ppermute | solution.py:20
  232.8 13.8 %collective-permute-start.31 = (bf16[4,50,576]{2,1,0:T(8,128)(2,1)S(1)}, bf16[4,50,576]{2,1,0:T(8,128)(2,1)S(1)}, u32[]{:S(2)}, u32[]{:S(2)}) collective-permute-start(bf16[4,50,576]{2,1,0:T(8,128)(2,1)S(1)} %select_convert_fusion.5), channel_id=1, source_target_pairs={{0,8},{4,12},{8,0},{12,4},{16,24},{20,28},{24,16},{28,20},{1,9},{5... | collective-permute-start | bytes 691208 | tf_op jit(solution)/shard_map/ppermute | solution.py:20
  234.8 15.2 %collective-permute-start.52 = (bf16[1,24,3072]{2,1,0:T(8,128)(2,1)S(1)}, bf16[1,24,3072]{2,1,0:T(8,128)(2,1)S(1)}, u32[]{:S(2)}, u32[]{:S(2)}) collective-permute-start(bf16[1,24,3072]{2,1,0:T(8,128)(2,1)S(1)} %maximum_bitcast_fusion), channel_id=1, source_target_pairs={{0,16},{4,20},{8,24},{12,28},{16,0},{20,4},{24,8},{28,12},{1,17},{... | collective-permute-start | bytes 442376 | tf_op jit(solution)/shard_map/ppermute | solution.py:20
  246.9 11.3 %collective-permute-start.32 = (bf16[4,25,576]{2,1,0:T(8,128)(2,1)S(1)}, bf16[4,25,576]{2,1,0:T(8,128)(2,1)S(1)}, u32[]{:S(2)}, u32[]{:S(2)}) collective-permute-start(bf16[4,25,576]{2,1,0:T(8,128)(2,1)S(1)} %select_convert_fusion.6), channel_id=1, source_target_pairs={{0,16},{4,20},{8,24},{12,28},{16,0},{20,4},{24,8},{28,12},{1,17},{... | collective-permute-start | bytes 345608 | tf_op jit(solution)/shard_map/ppermute | solution.py:20
  260.9 21.2 %collective-permute-start.59 = (bf16[4,96,768]{2,1,0:T(8,128)(2,1)S(1)}, bf16[4,96,768]{2,1,0:T(8,128)(2,1)S(1)}, u32[]{:S(2)}, u32[]{:S(2)}) collective-permute-start(bf16[4,96,768]{2,1,0:T(8,128)(2,1)S(1)} %maximum_select_fusion.5), channel_id=1, source_target_pairs={{0,4},{4,0},{8,12},{12,8},{16,20},{20,16},{24,28},{28,24},{1,5},{5... | collective-permute-start | bytes 1769480 | tf_op jit(solution)/shard_map/ppermute | solution.py:20
  262.5 17.6 %collective-permute-start.53 = (bf16[2,24,3072]{2,1,0:T(8,128)(2,1)S(1)}, bf16[2,24,3072]{2,1,0:T(8,128)(2,1)}, u32[]{:S(2)}, u32[]{:S(2)}) collective-permute-start(bf16[2,24,3072]{2,1,0:T(8,128)(2,1)S(1)} %maximum_select_fusion.8), channel_id=1, source_target_pairs={{0,8},{4,12},{8,0},{12,4},{16,24},{20,28},{24,16},{28,20},{1,9},{5... | collective-permute-start | bytes 884744 | tf_op jit(solution)/shard_map/ppermute | solution.py:20
  271.4 12.6 %collective-permute-start.29 = (bf16[256,768]{1,0:T(8,128)(2,1)S(1)}, bf16[256,768]{1,0:T(8,128)(2,1)S(1)}, u32[]{:S(2)}, u32[]{:S(2)}) collective-permute-start(bf16[256,768]{1,0:T(8,128)(2,1)S(1)} %fusion.13), channel_id=1, source_target_pairs={{0,2},{1,3},{2,0},{3,1},{4,6},{5,7},{6,4},{7,5},{8,10},{9,11},{10,... | collective-permute-start | bytes 1179656 | tf_op jit(solution)/shard_map/ppermute | solution.py:20
  281.2 16.3 %collective-permute-start.54 = (bf16[4,24,3072]{2,1,0:T(8,128)(2,1)S(1)}, bf16[4,24,3072]{2,1,0:T(8,128)(2,1)S(1)}, u32[]{:S(2)}, u32[]{:S(2)}) collective-permute-start(bf16[4,24,3072]{2,1,0:T(8,128)(2,1)S(1)} %maximum_select_fusion.4), channel_id=1, source_target_pairs={{0,4},{4,0},{8,12},{12,8},{16,20},{20,16},{24,28},{28,24},{1,5},{5... | collective-permute-start | bytes 1769480 | tf_op jit(solution)/shard_map/ppermute | solution.py:20
  287.3 18.1 %collective-permute-start.38 = (bf16[4,25,2304]{2,0,1:T(4,128)(2,1)S(1)}, bf16[4,25,2304]{2,0,1:T(4,128)(2,1)S(1)}, u32[]{:S(2)}, u32[]{:S(2)}) collective-permute-start(bf16[4,25,2304]{2,0,1:T(4,128)(2,1)S(1)} %copy.41), channel_id=1, source_target_pairs={{0,4},{4,0},{8,12},{12,8},{16,20},{20,16},{24,28},{28,24},{1,5},{5... | collective-permute-start | bytes 1382408 | tf_op jit(solution)/shard_map/ppermute | solution.py:20
  (73 other events, 524.8 us)
